TPU v7x, 16 devices: a whole 2x2x2 slice. The times are simulated.
16 devices in a mesh: dp: 4 (over z, y), tp: 4 (over x, core).
Axes of the slice: x: 2, y: 2, z: 2, core: 2. Of those that a mesh axis runs over, the one named last changes fastest.
Arguments:
- hidden: bfloat16 [128, 4096], P('dp'), parts along dimension 0
- cache_len: int32 [128], P('dp'), parts along dimension 0
- lin_state: float32 [128, 32, 128, 128], P('dp', 'tp'), parts along dimension 0
- k_cache: bfloat16 [128, 8, 512, 128], P('dp', 'tp'), parts along dimension 0
- v_cache: bfloat16 [128, 8, 512, 128], P('dp', 'tp'), parts along dimension 0
- norm_first: float32 [4096], replicated
- w_qkv: bfloat16 [4096, 3, 32, 128], P(None, None, 'tp')
- w_gate: bfloat16 [4096, 32, 128], P(None, 'tp')
- slopes: float32 [32], P('tp')
- out_norm: float32 [32, 128], P('tp')
- w_out_lin: bfloat16 [32, 128, 4096], P('tp')
- norm_second: float32 [4096], replicated
- w_attn: bfloat16 [4096, 8, 6, 128], P(None, 'tp')
- w_out_attn: bfloat16 [32, 128, 4096], P('tp')
- mix_alpha: float32 [2], replicated
- mix_beta: float32 [2], replicated
Outputs:
- output 1: bfloat16 [128, 4096], P('dp'), parts along dimension 0
- output 2: float32 [128, 32, 128, 128], P('dp', 'tp'), parts along dimension 0
- output 3: bfloat16 [128, 8, 512, 128], P('dp', 'tp'), parts along dimension 0
- output 4: bfloat16 [128, 8, 512, 128], P('dp', 'tp'), parts along dimension 0
There are 4 independent parts. A program takes and returns all parts, laid end to end along the dimension named above; an argument that names none is the same for every part.
All inputs are finite; a program needn't handle non-finite values.
Results may differ from a plain program's by a relative error of at most 0.0114328.
Values sent between devices are 32-bit elements.
A program may use at most 1 GiB of HBM per device.

v0:
```python
import jax
import jax.numpy as jnp
from jax import lax
from jax.sharding import PartitionSpec as P

EPS = 1e-5
ROPE_BASE = 10000000.0


def rms_scale(values, gain_vec):
    wide_vals = values.astype(jnp.float32)
    return wide_vals * lax.rsqrt(jnp.mean(wide_vals * wide_vals, axis=-1, keepdims=True) + EPS) * gain_vec


def rotary(values, positions):
    rot_dim = values.shape[-1] // 2
    half_dim = rot_dim // 2
    inv_freq = ROPE_BASE ** (-2.0 * jnp.arange(half_dim, dtype=jnp.float32) / rot_dim)
    angles = positions.astype(jnp.float32)[:, None] * inv_freq[None, :]
    cosine = jnp.cos(angles)[:, None, None, :]
    sine_val = jnp.sin(angles)[:, None, None, :]
    rot_first = values[..., :half_dim]
    rot_second = values[..., half_dim:rot_dim]
    return jnp.concatenate([rot_first * cosine - rot_second * sine_val,
                            rot_second * cosine + rot_first * sine_val,
                            values[..., rot_dim:]], axis=-1)


def solution(mesh):
    tp_size = mesh.shape['tp']
    row_spec = P('dp', None)
    cache_spec = P('dp', 'tp', None, None)
    in_specs = (row_spec, P('dp'), cache_spec, cache_spec, cache_spec, P(None), P(None, None, 'tp', None),
                P(None, 'tp', None), P('tp'), P('tp', None), P('tp', None, None), P(None),
                P(None, 'tp', None, None), P('tp', None, None), P(None), P(None))
    out_specs = (row_spec, cache_spec, cache_spec, cache_spec)

    def local_step(hidden, cache_len, lin_state, k_cache, v_cache, norm_first, w_qkv, w_gate, slopes, out_norm,
                   w_out_lin, norm_second, w_attn, w_out_attn, mix_alpha, mix_beta):
        head_dim = k_cache.shape[3]
        full_width = w_out_lin.shape[0] * head_dim * tp_size
        kv_local = w_attn.shape[1]
        group_size = w_attn.shape[2] - 2
        h_first = rms_scale(hidden, norm_first).astype(jnp.bfloat16)
        proj_lin = jax.nn.silu(jnp.einsum('bd,dchk->bchk', h_first, w_qkv, preferred_element_type=jnp.float32)).astype(jnp.bfloat16)
        decay_rate = jnp.exp(-slopes)[None, :, None, None]
        state_out = decay_rate * lin_state + jnp.einsum('bhk,bhv->bhkv', proj_lin[:, 1], proj_lin[:, 2], preferred_element_type=jnp.float32)
        lin_attn = jnp.einsum('bhk,bhkv->bhv', proj_lin[:, 0].astype(jnp.float32), state_out, precision=lax.Precision.HIGHEST)
        sq_sum = lax.psum(jnp.sum(lin_attn * lin_attn, axis=(1, 2)), 'tp')
        inv_rms = lax.rsqrt(sq_sum / full_width + EPS)[:, None, None]
        gate_val = jax.nn.sigmoid(jnp.einsum('bd,dhk->bhk', h_first, w_gate, preferred_element_type=jnp.float32))
        gated_out = (lin_attn * inv_rms * out_norm * gate_val).astype(jnp.bfloat16)
        lin_part = jnp.einsum('bhk,hkd->bd', gated_out, w_out_lin, preferred_element_type=jnp.float32)
        lin_out = lax.psum(lin_part, 'tp')
        mid_hidden = (mix_alpha[0] * h_first.astype(jnp.float32) + mix_beta[0] * lin_out).astype(jnp.bfloat16)
        h_second = rms_scale(mid_hidden, norm_second).astype(jnp.bfloat16)
        proj_attn = jnp.einsum('bd,dkjc->bkjc', h_second, w_attn, preferred_element_type=jnp.float32)
        turned = rotary(proj_attn[:, :, :group_size + 1], cache_len).astype(jnp.bfloat16)
        key_new = turned[:, :, group_size][:, :, None, :]
        value_new = proj_attn[:, :, group_size + 1].astype(jnp.bfloat16)[:, :, None, :]
        positions = jnp.arange(k_cache.shape[2], dtype=jnp.int32)
        write_mask = (positions[None, :] == cache_len[:, None])[:, None, :, None]
        k_out = jnp.where(write_mask, key_new, k_cache)
        v_out = jnp.where(write_mask, value_new, v_cache)
        scores = jnp.einsum('bkgc,bktc->bkgt', turned[:, :, :group_size], k_out, preferred_element_type=jnp.float32) * head_dim ** -0.5
        valid_mask = (positions[None, :] <= cache_len[:, None])[:, None, None, :]
        probs_bf = jax.nn.softmax(jnp.where(valid_mask, scores, -jnp.inf), axis=-1).astype(jnp.bfloat16)
        attn_rows = jnp.einsum('bkgt,bktc->bkgc', probs_bf, v_out, preferred_element_type=jnp.float32).astype(jnp.bfloat16)
        w_out_grouped = w_out_attn.reshape(kv_local, group_size, head_dim, w_out_attn.shape[2])
        attn_part = jnp.einsum('bkgc,kgcd->bd', attn_rows, w_out_grouped, preferred_element_type=jnp.float32)
        attn_out = lax.psum(attn_part, 'tp')
        hidden_out = (mix_alpha[1] * h_second.astype(jnp.float32) + mix_beta[1] * attn_out).astype(jnp.bfloat16)
        return hidden_out, state_out, k_out, v_out

    return jax.shard_map(local_step, mesh=mesh, in_specs=in_specs, out_specs=out_specs, check_vma=False)
```

profile of v0, /device:TPU:0, one launch (start us, length us, event | category | flops | bytes accessed | tf_op | source)
XLA Modules:
  0.0 166.1 jit_solution(14661184683376408572)
XLA Ops:
  7.2 0.0 all-reduce.3.cloned.1.call-start
  7.2 0.7 negate_exponential_fusion
  7.9 1.1 fusion.35
  9.0 12.4 %multiply_convert_fusion = bf16[32,3,8,128]{3,0,2,1:T(8,128)(2,1)S(1)} fusion(bf16[4096,3,8,128]{3,2,1,0:T(8,128)(2,1)} %param.22, bf16[32,4096]{1,0:T(8,128)(2,1)} %param.16, f32[4096]{0:T(1024)} %param.21, f32[32]{0:T(128)S(1)} %add_rsqrt_fusion.2), kind=kOutput, calls=%fused_computation.37 | convolution fusion | flops 806322176 | bytes 25641088 | tf_op jit(solution)/shard_map/bd,dchk->bchk/dot_general | solution.py:45
  21.5 0.1 copy.22
  21.6 0.1 copy.21
  21.7 7.9 %multiply_add_fusion = f32[32,8,128,128]{3,2,1,0:T(8,128)S(1)} fusion(f32[32,8,128,128]{3,2,1,0:T(8,128)} %param.18, f32[32,8,128]{2,1,0:T(8,128)S(1)} %copy.22, f32[32,8,128]{2,1,0:T(8,128)S(1)} %copy.21, f32[8]{0:T(128)S(1)} %negate_exponential_fusion), kind=kLoop, calls=%fused_computation.3 | loop fusion | flops 12582912 | bytes 33816608 | tf_op jit(solution)/shard_map/add | solution.py:47
  29.6 0.0 copy-start
  29.6 7.7 %fusion.52 = f32[32,8,1,128]{3,2,1,0:T(1,128)S(1)} fusion(f32[32,8,128,128]{3,2,1,0:T(8,128)S(1)} %multiply_add_fusion, bf16[32,8,128,1]{2,0,1,3:T(8,128)(2,1)S(1)} %get-tuple-element.8), kind=kOutput, calls=%fused_computation.50 | convolution fusion | flops 50331648 | bytes 16973824 | tf_op jit(solution)/shard_map/bhk,bhkv->bhv/dot_general | solution.py:48
  37.3 0.1 fusion.49
  37.4 8.6 %psum.21 = f32[32]{0:T(128)S(1)} all-reduce(f32[32]{0:T(128)S(1)} %fusion.49), channel_id=1, replica_groups=mesh['dp'=4,'tp'=4] {'tp'}, use_global_device_ids=true, to_apply=%region_2.3 | all-reduce | flops 32 | bytes 256 | tf_op jit(solution)/shard_map/psum | solution.py:49
  46.1 9.7 %convolution_bitcast_fusion = f32[32,4096]{1,0:T(8,128)} fusion(bf16[8,128,4096]{2,1,0:T(8,128)(2,1)} %param.26, bf16[4096,8,128]{2,1,0:T(8,128)(2,1)} %param.23, f32[32,8,1,128]{3,2,1,0:T(1,128)S(1)} %fusion.52, f32[8,128]{1,0:T(8,128)S(1)} %copy-done.4, f32[32]{0:T(128)S(1)} %add_rsqrt_fusion.1, bf16[32,4096]{1,0:T(8,128)(2,1)S(1)} %copy-done.1, ...), kind=kOutput, calls=%fused_computation.13 | convolution fusion | flops 537624576 | bytes 17715456 | tf_op jit(solution)/shard_map/bhk,hkd->bd/dot_general | solution.py:53
  55.8 0.0 all-reduce.3.cloned.1.call-update
  55.8 0.0 all-reduce.5.cloned.1.call-start
  55.9 0.6 fusion.66
  56.5 0.6 fusion.67
  57.1 0.1 iota_compare_fusion.1
  57.2 0.1 multiply_cosine_fusion
  57.3 28.3 %all-reduce.3.cloned.1.call-done = f32[32,4096]{1,0:T(8,128)} async-done(((f32[32,4096]{1,0:T(8,128)}), f32[32,4096]{1,0:T(8,128)}) %all-reduce.3.cloned.1.call-update) | async-done | bytes 524304 | tf_op jit(solution)/shard_map/psum | solution.py:54
  85.7 2.6 %fusion.38 = (f32[32]{0:T(128)S(1)}, bf16[32,4096]{1,0:T(8,128)(2,1)S(1)}) fusion(f32[32,4096]{1,0:T(8,128)} %all-reduce.3.cloned.1.call-done, f32[]{:T(128)} %bitcast.2, f32[4096]{0:T(1024)S(1)} %copy-done.2, f32[32]{0:T(128)S(1)} %add_rsqrt_fusion.2, bf16[32,4096]{1,0:T(8,128)(2,1)S(1)} %copy-done.1, f32[]{:T(128)} %bitcast.1), kind=kLoop, calls=%fused_computation.31 | loop fusion | flops 1572832 | bytes 1065224 | tf_op jit(solution)/shard_map/reduce_sum | solution.py:12
  88.3 8.0 %fusion.68 = (bf16[32,2,6,128]{3,0,2,1:T(8,128)(2,1)S(1)}, f32[32,2,6,128]{3,0,2,1:T(8,128)S(1)}) fusion(bf16[4096,2,6,128]{3,1,2,0:T(2,128)(2,1)} %param.28, f32[4096]{0:T(1024)S(1)} %copy-done.3, f32[32]{0:T(128)S(1)} %add_rsqrt_fusion, bf16[32,4096]{1,0:T(8,128)(2,1)S(1)} %get-tuple-element.5), kind=kOutput, calls=%fused_computation.77 | convolution fusion | flops 403226624 | bytes 13156480 | tf_op jit(solution)/shard_map/bd,dkjc->bkjc/dot_general | solution.py:57
  96.4 0.1 slice.63
  96.5 0.1 subtract_convert_fusion
  96.6 0.1 maximum_bitcast_fusion
  96.7 0.1 pad_maximum_fusion
  96.9 13.3 %broadcast_select_fusion.1 = (bf16[32,2,512,128]{3,2,1,0:T(8,128)(2,1)}, bf16[32,2,512,128]{3,2,1,0:T(8,128)(2,1)}) fusion(bf16[32,2,512,128]{3,2,1,0:T(8,128)(2,1)} %param.19, pred[32,512]{1,0:T(8,128)(4,1)S(1)} %get-tuple-element.20, bf16[32,2,128]{2,1,0:T(2,128)(2,1)S(1)} %copy.24, bf16[32,2,512,128]{3,2,1,0:T(8,128)(2,1)} %param.20, ...), kind=kLoop, calls=%fused_computation.11 | loop fusion | flops 8388608 | bytes 33603584 | tf_op jit(solution)/shard_map/jit(_where)/select_n | solution.py:63
  110.2 5.8 %fusion.69 = (f32[32,2,4]{2,1,0:T(2,128)S(1)}, f32[32,2,4,512]{3,2,1,0:T(4,128)S(1)}) fusion(bf16[32,2,512,128]{3,2,1,0:T(8,128)(2,1)} %get-tuple-element.11, pred[32,512]{1,0:T(8,128)(4,1)S(1)} %get-tuple-element.19, bf16[32,2,4,128]{3,0,2,1:T(8,128)(2,1)S(1)} %slice.64), kind=kOutput, calls=%fused_computation.78 | convolution fusion | flops 34079232 | bytes 8995840 | tf_op jit(solution)/shard_map/sub | solution.py:67
  116.0 4.6 %fusion.43 = bf16[32,2,4,128]{3,2,1,0:T(4,128)(2,1)S(1)} fusion(bf16[32,2,512,128]{3,2,1,0:T(8,128)(2,1)} %get-tuple-element.12, f32[32,2,4,512]{3,2,1,0:T(4,128)S(1)} %get-tuple-element.24, f32[32,2,4]{2,1,0:T(2,128)S(1)} %get-tuple-element.23), kind=kOutput, calls=%fused_computation.38 | convolution fusion | flops 33816576 | bytes 8979456 | tf_op jit(solution)/shard_map/bkgt,bktc->bkgc/dot_general | solution.py:68
  120.6 5.8 %fusion.9 = f32[32,4096]{1,0:T(8,128)} fusion(bf16[2,4,128,4096]{3,2,1,0:T(8,128)(2,1)} %bitcast.58, bf16[32,2,4,128]{3,2,1,0:T(4,128)(2,1)S(1)} %fusion.43), kind=kOutput, calls=%fused_computation.12 | convolution fusion | flops 268435456 | bytes 8978432 | tf_op jit(solution)/shard_map/bkgc,kgcd->bd/dot_general | solution.py:70
  126.4 0.0 all-reduce.5.cloned.1.call-update
  126.4 29.7 %all-reduce.5.cloned.1.call-done = f32[32,4096]{1,0:T(8,128)} async-done(((f32[32,4096]{1,0:T(8,128)}), f32[32,4096]{1,0:T(8,128)}) %all-reduce.5.cloned.1.call-update) | async-done | bytes 524304 | tf_op jit(solution)/shard_map/psum | solution.py:71
  156.1 3.1 %add_convert_fusion = bf16[32,4096]{1,0:T(8,128)(2,1)} fusion(f32[32,4096]{1,0:T(8,128)} %all-reduce.5.cloned.1.call-done, f32[]{:T(128)} %bitcast.12, f32[]{:T(128)} %bitcast, f32[4096]{0:T(1024)S(1)} %copy-done.3, f32[32]{0:T(128)S(1)} %add_rsqrt_fusion, bf16[32,4096]{1,0:T(8,128)(2,1)S(1)} %get-tuple-element.5), kind=kLoop, calls=%fused_computation.34 | loop fusion | flops 1179648 | bytes 1065096 | tf_op jit(solution)/shard_map/convert_element_type | solution.py:72
  (25 shorter events, 0.1 us)
Async XLA Ops:
  7.2 78.5 %all-reduce.3.cloned.1.call-start = ((), (), s32[]{:S(2)}) async-start(), calls=%async_computation | async-start | bytes 1048576 | tf_op jit(solution)/shard_map/psum | solution.py:54
  29.6 7.7 %copy-start = (f32[32,8,128,128]{3,2,1,0:T(8,128)}, f32[32,8,128,128]{3,2,1,0:T(8,128)S(1)}, u32[]{:S(2)}) copy-start(f32[32,8,128,128]{3,2,1,0:T(8,128)S(1)} %multiply_add_fusion) | copy-start | bytes 50331652
  29.6 16.5 %copy-start.1 = (bf16[32,4096]{1,0:T(8,128)(2,1)S(1)}, bf16[32,4096]{1,0:T(8,128)(2,1)}, u32[]{:S(2)}) copy-start(bf16[32,4096]{1,0:T(8,128)(2,1)} %param.16) | copy-start | bytes 786436
  29.6 16.5 %copy-start.2 = (f32[4096]{0:T(1024)S(1)}, f32[4096]{0:T(1024)}, u32[]{:S(2)}) copy-start(f32[4096]{0:T(1024)} %param.21) | copy-start | bytes 49156
  29.6 16.5 %copy-start.4 = (f32[8,128]{1,0:T(8,128)S(1)}, f32[8,128]{1,0:T(8,128)}, u32[]{:S(2)}) copy-start(f32[8,128]{1,0:T(8,128)} %param.25) | copy-start | bytes 12292
  46.1 9.8 %copy-start.5 = (f32[2]{0:T(128)S(1)}, f32[2]{0:T(128)}, u32[]{:S(2)}) copy-start(f32[2]{0:T(128)} %param.30) | copy-start | bytes 28
  46.1 10.4 %copy-start.6 = (f32[2]{0:T(128)S(1)}, f32[2]{0:T(128)}, u32[]{:S(2)}) copy-start(f32[2]{0:T(128)} %param.31) | copy-start | bytes 28
  46.1 11.0 %copy-start.7 = (s32[32]{0:T(128)S(1)}, s32[32]{0:T(128)}, u32[]{:S(2)}) copy-start(s32[32]{0:T(128)} %param.17) | copy-start | bytes 388
  46.1 42.2 %copy-start.3 = (f32[4096]{0:T(1024)S(1)}, f32[4096]{0:T(1024)}, u32[]{:S(2)}) copy-start(f32[4096]{0:T(1024)} %param.27) | copy-start | bytes 49156
  55.8 100.3 %all-reduce.5.cloned.1.call-start = ((), (), s32[]{:S(2)}) async-start(), calls=%async_computation.1 | async-start | bytes 1048576 | tf_op jit(solution)/shard_map/psum | solution.py:71
Sparse Core Ops, SparseCore 0:
  55.9 29.6 all-reduce.2
  126.5 29.5 all-reduce.4
where the time goes:
time: 167 us; the launch traced here: 166 us
  waiting for transfers between devices  58.1 us (35%)
  matrix products  54.1 us (32%)
  other arithmetic  29.4 us (18%)
  between operations  14.3 us (9%)
  blocking collectives  8.63 us (5%)
    psum x1, waiting for transfers between devices, local_step(): attn_out = lax.psum(attn_part, 'tp')  29.7 us
    psum x1, waiting for transfers between devices, local_step(): lin_out = lax.psum(lin_part, 'tp')  28.3 us
    select_n x1, other arithmetic, local_step(): k_out = jnp.where(write_mask, key_new, k_cache)  13.3 us
    dot_general x1, matrix products, local_step(): jnp.einsum('bd,dchk->bchk', h_first, w_qkv, preferred_element_type=jnp.fl...  12.4 us
    dot_general x1, matrix products, local_step(): jnp.einsum('bhk,hkd->bd', gated_out, w_out_lin, preferred_element_type=jn...  9.65 us
    psum x1, blocking collectives, local_step(): sq_sum = lax.psum(jnp.sum(lin_attn * lin_attn, axis=(1, 2)), 'tp')  8.63 us
    dot_general x1, matrix products, local_step(): jnp.einsum('bd,dkjc->bkjc', h_second, w_attn, preferred_element_type=jnp....  8.05 us
    add x1, other arithmetic, local_step(): decay_rate * lin_state  7.89 us
  transfers between devices with their start and end apart: 2, of which 2 were waited for; matrix products, arithmetic and copies ran while one was open for 1% of the time, Pallas kernels for 0%

commit v1 on v0

v1 whole, which is shorter than its diff:
```python
import functools
import math

import jax
import jax.numpy as jnp
from jax import lax
from jax.experimental import pallas as pl
from jax.experimental.pallas import tpu as pltpu
from jax.sharding import PartitionSpec as P

EPS = 1e-5
ROPE_BASE = 10000000.0
MESH = pl.DeviceIdType.MESH
F32 = jnp.float32
BF16 = jnp.bfloat16
VMEM_LIMIT = 62 * 1024 * 1024

B = 32
D = 4096
HL = 8
HD = 128
KV = 2
GQ = 4
T = 512
NC = D // HD

DCH = 128
STEPS = D // DCH
RING = 8


def any_spec():
    return pl.BlockSpec(memory_space=pl.ANY)


def vmem_spec():
    return pl.BlockSpec(memory_space=pltpu.VMEM)


def smem_spec():
    return pl.BlockSpec(memory_space=pltpu.SMEM)


def dot(a, b):
    return jnp.dot(a, b, preferred_element_type=F32)


def lightning_kernel(hid_ref, g1_ref, slopes_ref, onorm_ref, state_ref, wqkv_ref, wgate_ref,
                     sout_ref, og_ref, ss_ref, h1_ref,
                     wbuf, sbuf, ebuf, lbuf, acc, qk_t, v_s, o_s, wsem, ssem, osem):
    def w_copies(step, slot):
        rows = pl.ds(step * DCH, DCH)
        out = [pltpu.make_async_copy(wqkv_ref.at[rows, c], wbuf.at[slot, c], wsem.at[slot, c]) for c in range(3)]
        out.append(pltpu.make_async_copy(wgate_ref.at[rows], wbuf.at[slot, 3], wsem.at[slot, 3]))
        return out

    def s_copy(b):
        return pltpu.make_async_copy(state_ref.at[b], sbuf.at[b], ssem.at[b])

    def o_copy(b):
        return pltpu.make_async_copy(sbuf.at[b], sout_ref.at[b], osem.at[b])

    for i in range(RING):
        for cp in w_copies(i, i):
            cp.start()

    sq = jnp.zeros((B, HD), F32)
    for c in range(NC):
        x = hid_ref[:, c * HD:(c + 1) * HD].astype(F32)
        sq = sq + x * x
    inv = lax.rsqrt(jnp.sum(sq, axis=1, keepdims=True) / D + EPS)
    rr = lax.broadcasted_iota(jnp.int32, (HD, 256), 1)
    dd = lax.broadcasted_iota(jnp.int32, (HD, 256), 0)
    for c in range(NC):
        x = hid_ref[:, c * HD:(c + 1) * HD].astype(F32)
        h1 = (x * inv * g1_ref[c:c + 1, :]).astype(BF16)
        h1_ref[:, c * HD:(c + 1) * HD] = h1
        lbuf[c * B:(c + 1) * B, 0:HD] = h1
    for n in range(4):
        spread = jnp.where(rr // 8 + 32 * n == dd, 1.0, 0.0).astype(BF16)
        for c in range(NC // 8):
            e = dot(lbuf[c * 256:(c + 1) * 256, 0:HD], spread).astype(BF16)
            for k in range(8):
                ebuf[c * 8 + k, :, n * 256:(n + 1) * 256] = e[k * B:(k + 1) * B, :]

    acc[...] = jnp.zeros_like(acc)
    lane = lax.broadcasted_iota(jnp.int32, (B, 1024), 1) % 8

    def step_fn(i, carry):
        slot = lax.rem(i, RING)
        s_copy(i).start()
        e = ebuf[i]
        for h in range(HL):
            keep = jnp.where(lane == h, 1.0, 0.0).astype(BF16)
            lbuf[h * B:(h + 1) * B, :] = e * keep
        for cp in w_copies(i, slot):
            cp.wait()
        left = lbuf[0:HL * B, :]
        for pair in range(2):
            right = jnp.concatenate([wbuf[slot, 2 * pair].reshape(DCH * HL, HD),
                                     wbuf[slot, 2 * pair + 1].reshape(DCH * HL, HD)], axis=1)
            acc[pair] += dot(left, right)

        @pl.when(i + RING < STEPS)
        def _():
            for cp in w_copies(i + RING, slot):
                cp.start()
        return carry

    lax.fori_loop(0, STEPS, step_fn, 0)

    for h in range(HL):
        rows = slice(h * B, (h + 1) * B)
        q = jax.nn.silu(acc[0, rows, 0:HD]).astype(BF16)
        k = jax.nn.silu(acc[0, rows, HD:2 * HD]).astype(BF16)
        v = jax.nn.silu(acc[1, rows, 0:HD]).astype(BF16)
        qk = jnp.concatenate([k, q], axis=0).astype(F32)
        qk_t[h] = jnp.transpose(qk).astype(BF16)
        v_s[h] = v

    def row_fn(b, carry):
        s_copy(b).wait()
        row_i = lax.broadcasted_iota(jnp.int32, (B, HD), 0)
        hit = row_i == b
        ones = jnp.where(hit, 1.0, 0.0).astype(BF16)
        zero = jnp.zeros((B, HD), BF16)
        for h in range(HL):
            top = jnp.concatenate([v_s[h] * ones, zero], axis=1)
            bot = jnp.concatenate([zero, ones], axis=1)
            prod = dot(qk_t[h], jnp.concatenate([top, bot], axis=0))
            decay = jnp.exp(jnp.full((1, HD), -slopes_ref[h], F32))
            new = decay * sbuf[b, h] + prod[:, 0:HD]
            sbuf[b, h] = new
            o_s[b, h:h + 1, :] = jnp.sum(prod[:, HD:] * new, axis=0, keepdims=True)
        o_copy(b).start()
        return carry

    lax.fori_loop(0, B, row_fn, 0)

    ss = jnp.zeros((B, HD), F32)
    for h in range(HL):
        o = o_s[:, h, :]
        ss = ss + o * o
        gate = jax.nn.sigmoid(acc[1, h * B:(h + 1) * B, HD:2 * HD])
        og_ref[:, h * HD:(h + 1) * HD] = o * onorm_ref[h:h + 1, :] * gate
    ss_ref[...] = jnp.broadcast_to(jnp.sum(ss, axis=1, keepdims=True), (B, HD))

    def drain(b, carry):
        o_copy(b).wait()
        return carry

    lax.fori_loop(0, B, drain, 0)


def lightning(hidden, g1, slopes, out_norm, lin_state, w_qkv, w_gate):
    return pl.pallas_call(
        lightning_kernel,
        out_shape=[jax.ShapeDtypeStruct((B, HL, HD, HD), F32), jax.ShapeDtypeStruct((B, HL * HD), F32),
                   jax.ShapeDtypeStruct((B, HD), F32), jax.ShapeDtypeStruct((B, D), BF16)],
        in_specs=[vmem_spec(), vmem_spec(), smem_spec(), vmem_spec(), any_spec(), any_spec(), any_spec()],
        out_specs=[any_spec(), vmem_spec(), vmem_spec(), vmem_spec()],
        scratch_shapes=[
            pltpu.VMEM((RING, 4, DCH, HL, HD), BF16),
            pltpu.VMEM((B, HL, HD, HD), F32),
            pltpu.VMEM((STEPS, B, DCH * HL), BF16),
            pltpu.VMEM((1024, 1024), BF16),
            pltpu.VMEM((2, HL * B, 2 * HD), F32),
            pltpu.VMEM((HL, HD, 2 * B), BF16),
            pltpu.VMEM((HL, B, HD), BF16),
            pltpu.VMEM((B, HL, HD), F32),
            pltpu.SemaphoreType.DMA((RING, 4)),
            pltpu.SemaphoreType.DMA((B,)),
            pltpu.SemaphoreType.DMA((B,)),
        ],
        compiler_params=pltpu.CompilerParams(vmem_limit_bytes=VMEM_LIMIT),
        name="lightning",
    )(hidden, g1, slopes, out_norm, lin_state, w_qkv, w_gate)


NCH = 4
CW = D // 2 // NCH


def peers():
    dp = lax.axis_index("dp")
    me = lax.axis_index("tp")
    core = lax.rem(me, 2)
    chip = me // 2
    mate = (dp, chip * 2 + (1 - core))
    across = (dp, (1 - chip) * 2 + core)
    diag = (dp, (1 - chip) * 2 + (1 - core))
    return core, mate, across, diag


def entry_barrier(targets):
    barrier = pltpu.get_barrier_semaphore()
    for dev in targets:
        pl.semaphore_signal(barrier, inc=1, device_id=dev, device_id_type=MESH)
    pl.semaphore_wait(barrier, len(targets))


def rcopy(src, dst, send, recv, dev):
    return pltpu.make_async_remote_copy(src_ref=src, dst_ref=dst, send_sem=send, recv_sem=recv,
                                        device_id=dev, device_id_type=MESH)


def exchange(left, wbuf, wwait, mid_work, core, mate, across,
             a_send, a_recv, b_send, b_recv, total, sems):
    sa, ra, sb, rb, sc, rc = sems
    per = CW // HD

    def product(half, j):
        base = half * (NC // 2) + j * per
        cols = []
        for p in range(per // 2):
            w = jnp.concatenate([wbuf[base + 2 * p], wbuf[base + 2 * p + 1]], axis=1)
            cols.append(dot(left, w))
        return jnp.concatenate(cols, axis=1)

    a_copies, b_copies, c_copies = [], [], []
    for j in range(NCH):
        wwait(1 - core, j)
        a_send[j] = product(1 - core, j)
        cp = rcopy(a_send.at[j], a_recv.at[j], sa.at[j], ra.at[j], mate)
        cp.start()
        a_copies.append(cp)
        wwait(core, j)
        b_send[j] = product(core, j)
        if j >= 1:
            send_across(j - 1, a_copies, b_copies, a_recv, b_send, b_recv, sb, rb, across)
    send_across(NCH - 1, a_copies, b_copies, a_recv, b_send, b_recv, sb, rb, across)
    mid_work()
    for j in range(NCH):
        b_copies[j].wait_recv()
        total[core, j] = b_send[j] + b_recv[j]
        cp = rcopy(total.at[core, j], total.at[core, j], sc.at[j], rc.at[j], mate)
        cp.start()
        c_copies.append(cp)
    for j in range(NCH):
        c_copies[j].wait_recv()
    for j in range(NCH):
        a_copies[j].wait_send()
        b_copies[j].wait_send()
        c_copies[j].wait_send()


def send_across(j, a_copies, b_copies, a_recv, b_send, b_recv, sb, rb, across):
    a_copies[j].wait_recv()
    b_send[j] = b_send[j] + a_recv[j]
    cp = rcopy(b_send.at[j], b_recv.at[j], sb.at[j], rb.at[j], across)
    cp.start()
    b_copies.append(cp)


def exchange_scratch():
    return [
        pltpu.VMEM((NC, HL * HD, HD), BF16),
        pltpu.VMEM((NCH, B, CW), F32),
        pltpu.VMEM((NCH, B, CW), F32),
        pltpu.VMEM((NCH, B, CW), F32),
        pltpu.VMEM((NCH, B, CW), F32),
        pltpu.VMEM((2, NCH, B, CW), F32),
        pltpu.SemaphoreType.DMA((NC,)),
        pltpu.SemaphoreType.DMA((NCH,)),
        pltpu.SemaphoreType.DMA((NCH,)),
        pltpu.SemaphoreType.DMA((NCH,)),
        pltpu.SemaphoreType.DMA((NCH,)),
        pltpu.SemaphoreType.DMA((NCH,)),
        pltpu.SemaphoreType.DMA((NCH,)),
    ]


def out_weights(w_ref, wbuf, wsem, core):
    per = CW // HD

    def copy(c):
        cols = pl.ds(pl.multiple_of(c * HD, HD), HD)
        return pltpu.make_async_copy(w_ref.at[:, cols], wbuf.at[c], wsem.at[c])

    def start():
        for j in range(NCH):
            for half in (1 - core, core):
                for p in range(per):
                    copy(half * (NC // 2) + j * per + p).start()

    def wait(half, j):
        for p in range(per):
            copy(half * (NC // 2) + j * per + p).wait()

    return start, wait


WA_ROWS = D * KV * (GQ + 2)
WA_CH = 32
WA_STEP = WA_ROWS // WA_CH
NJ = KV * (GQ + 2)


def mid_kernel(og_ref, ss_ref, h1_ref, g2_ref, alpha_ref, beta_ref, len_ref, wout_ref, wattn_ref,
               q_ref, kn_ref, vn_ref, h2_ref,
               wbuf, a_send, a_recv, b_send, b_recv, total, wsem, sa, ra, sb, rb, sc, rc,
               wraw, wide, w2, ss_recv, wasem, ss_s, ss_r):
    core, mate, across, diag = peers()
    start_w, wait_w = out_weights(wout_ref, wbuf, wsem, core)
    start_w()

    def wa_copy(i):
        return pltpu.make_async_copy(wattn_ref.at[pl.ds(i * WA_STEP, WA_STEP)], wraw.at[i], wasem.at[i])

    def wa_start(i, carry):
        wa_copy(i).start()
        return carry

    lax.fori_loop(0, WA_CH, wa_start, 0)
    entry_barrier((mate, across, diag))
    ss_copies = []
    for n, dev in enumerate((mate, across, diag)):
        cp = rcopy(ss_ref, ss_recv.at[n], ss_s.at[n], ss_r.at[n], dev)
        cp.start()
        ss_copies.append(cp)
    for cp in ss_copies:
        cp.wait_recv()
    ssum = (ss_ref[...] + ss_recv[0]) + (ss_recv[1] + ss_recv[2])
    inv = lax.rsqrt(ssum[:, 0:1] / D + EPS)
    left = (og_ref[...] * inv).astype(BF16)

    def relayout():
        def body(i, carry):
            wa_copy(i).wait()
            wide[...] = wraw[i].astype(F32)
            for j in range(NJ):
                w2[j, pl.ds(pl.multiple_of(i * HD, HD), HD), :] = wide[pl.ds(j, HD, stride=NJ), :].astype(BF16)
            return carry
        lax.fori_loop(0, WA_CH, body, 0)

    exchange(left, wbuf, wait_w, relayout, core, mate, across, a_send, a_recv, b_send, b_recv, total,
             (sa, ra, sb, rb, sc, rc))
    for cp in ss_copies:
        cp.wait_send()

    per = CW // HD
    alpha = alpha_ref[0]
    beta = beta_ref[0]
    sq = jnp.zeros((B, HD), F32)
    mids = []
    for c in range(NC):
        a1 = total[c // (NC // 2), (c % (NC // 2)) // per, :, (c % per) * HD:(c % per + 1) * HD]
        m = (alpha * h1_ref[:, c * HD:(c + 1) * HD].astype(F32) + beta * a1).astype(BF16)
        h2_ref[:, c * HD:(c + 1) * HD] = m
        x = m.astype(F32)
        sq = sq + x * x
    inv2 = lax.rsqrt(jnp.sum(sq, axis=1, keepdims=True) / D + EPS)
    for c in range(NC):
        m = h2_ref[:, c * HD:(c + 1) * HD].astype(F32)
        h2_ref[:, c * HD:(c + 1) * HD] = (m * inv2 * g2_ref[c:c + 1, :]).astype(BF16)

    pos = jnp.zeros((B, HD), F32)
    row_i = lax.broadcasted_iota(jnp.int32, (B, HD), 0)
    for b in range(B):
        pos = jnp.where(row_i == b, jnp.full((B, HD), len_ref[b]).astype(F32), pos)
    lane = lax.broadcasted_iota(jnp.int32, (B, HD), 1)
    freq = jnp.exp((lane % 32).astype(F32) * (-2.0 * math.log(ROPE_BASE) / 64))
    ang = pos * freq
    rot = lane < 64
    cosv = jnp.where(rot, jnp.cos(ang), 1.0)
    sinv = jnp.sin(ang)
    sin_lo = jnp.where(lane < 32, -sinv, 0.0)
    sin_hi = jnp.where((lane >= 32) & rot, sinv, 0.0)

    def turn(x):
        return x * cosv + pltpu.roll(x, HD - 32, 1) * sin_lo + pltpu.roll(x, 32, 1) * sin_hi

    h2 = h2_ref[...]
    for j in range(GQ + 2):
        w = jnp.concatenate([w2[2 * j], w2[2 * j + 1]], axis=1)
        pr = dot(h2, w)
        for kv in range(KV):
            x = pr[:, kv * HD:(kv + 1) * HD]
            if j < GQ:
                q_ref[pl.ds(kv * GQ + j, B, stride=8), :] = turn(x).astype(BF16).astype(F32)
            elif j == GQ:
                kn_ref[kv] = turn(x).astype(BF16).astype(F32)
            else:
                vn_ref[kv] = x.astype(BF16).astype(F32)


def middle(og, ss, h1, g2, alpha, beta, cache_len, w_out, w_attn):
    return pl.pallas_call(
        mid_kernel,
        out_shape=[jax.ShapeDtypeStruct((B * 8, HD), F32), jax.ShapeDtypeStruct((KV, B, HD), F32),
                   jax.ShapeDtypeStruct((KV, B, HD), F32), jax.ShapeDtypeStruct((B, D), BF16)],
        in_specs=[vmem_spec(), vmem_spec(), vmem_spec(), vmem_spec(), smem_spec(), smem_spec(), smem_spec(),
                  any_spec(), any_spec()],
        out_specs=[vmem_spec()] * 4,
        scratch_shapes=exchange_scratch() + [
            pltpu.VMEM((WA_CH, WA_STEP, HD), BF16),
            pltpu.VMEM((WA_STEP, HD), F32),
            pltpu.VMEM((NJ, D, HD), BF16),
            pltpu.VMEM((3, B, HD), F32),
            pltpu.SemaphoreType.DMA((WA_CH,)),
            pltpu.SemaphoreType.DMA((3,)),
            pltpu.SemaphoreType.DMA((3,)),
        ],
        compiler_params=pltpu.CompilerParams(vmem_limit_bytes=VMEM_LIMIT, collective_id=0, has_side_effects=True),
        name="middle",
    )(og, ss, h1, g2, alpha, beta, cache_len, w_out, w_attn)


def attention_kernel(len_ref, q_ref, kn_ref, vn_ref, k_ref, v_ref, at_ref, ko_ref, vo_ref,
                     kbuf, vbuf, isem, osem):
    def ins(b):
        return (pltpu.make_async_copy(k_ref.at[b], kbuf.at[b], isem.at[0, b]),
                pltpu.make_async_copy(v_ref.at[b], vbuf.at[b], isem.at[1, b]))

    def outs(b):
        return (pltpu.make_async_copy(kbuf.at[b], ko_ref.at[b], osem.at[0, b]),
                pltpu.make_async_copy(vbuf.at[b], vo_ref.at[b], osem.at[1, b]))

    def start_in(b, carry):
        for cp in ins(b):
            cp.start()
        return carry

    lax.fori_loop(0, B, start_in, 0)
    row8 = lax.broadcasted_iota(jnp.int32, (8, HD), 0)
    row16 = lax.broadcasted_iota(jnp.int32, (16, HD), 0)
    tpos = lax.broadcasted_iota(jnp.int32, (8, T), 1)

    def body(b, carry):
        for cp in ins(b):
            cp.wait()
        p = len_ref[b]
        base = pl.multiple_of((p // 16) * 16, 16)
        hit = row16 == p - base
        for kv in range(KV):
            kn = kn_ref[kv, pl.ds(b, 1), :]
            vn = vn_ref[kv, pl.ds(b, 1), :]
            old_k = kbuf[b, kv, pl.ds(base, 16), :].astype(F32)
            old_v = vbuf[b, kv, pl.ds(base, 16), :].astype(F32)
            kbuf[b, kv, pl.ds(base, 16), :] = jnp.where(hit, kn, old_k).astype(BF16)
            vbuf[b, kv, pl.ds(base, 16), :] = jnp.where(hit, vn, old_v).astype(BF16)
        for cp in outs(b):
            cp.start()
        q = q_ref[pl.ds(b * 8, 8), :]
        q2 = jnp.concatenate([jnp.where(row8 < 4, q, 0.0), jnp.where(row8 < 4, 0.0, q)], axis=1).astype(BF16)
        k2 = jnp.concatenate([kbuf[b, 0], kbuf[b, 1]], axis=1)
        s = lax.dot_general(q2, k2, (((1,), (1,)), ((), ())), preferred_element_type=F32) * HD ** -0.5
        s = jnp.where(tpos <= p, s, -jnp.inf)
        e = jnp.exp(s - jnp.max(s, axis=1, keepdims=True))
        pr = (e / jnp.sum(e, axis=1, keepdims=True)).astype(BF16)
        v2 = jnp.concatenate([vbuf[b, 0], vbuf[b, 1]], axis=1)
        o = dot(pr, v2)
        at_ref[pl.ds(b * 8, 8), :] = jnp.where(row8 < 4, o[:, 0:HD], o[:, HD:])
        return carry

    lax.fori_loop(0, B, body, 0)

    def drain(b, carry):
        for cp in outs(b):
            cp.wait()
        return carry

    lax.fori_loop(0, B, drain, 0)


def attention(cache_len, q, kn, vn, k_cache, v_cache):
    return pl.pallas_call(
        attention_kernel,
        out_shape=[jax.ShapeDtypeStruct((B * 8, HD), F32), jax.ShapeDtypeStruct((B, KV, T, HD), BF16),
                   jax.ShapeDtypeStruct((B, KV, T, HD), BF16)],
        in_specs=[smem_spec(), vmem_spec(), vmem_spec(), vmem_spec(), any_spec(), any_spec()],
        out_specs=[vmem_spec(), any_spec(), any_spec()],
        scratch_shapes=[
            pltpu.VMEM((B, KV, T, HD), BF16),
            pltpu.VMEM((B, KV, T, HD), BF16),
            pltpu.SemaphoreType.DMA((2, B)),
            pltpu.SemaphoreType.DMA((2, B)),
        ],
        compiler_params=pltpu.CompilerParams(vmem_limit_bytes=VMEM_LIMIT),
        name="attention",
    )(cache_len, q, kn, vn, k_cache, v_cache)


def last_kernel(at_ref, h2_ref, alpha_ref, beta_ref, wout_ref, out_ref,
                wbuf, a_send, a_recv, b_send, b_recv, total, wsem, sa, ra, sb, rb, sc, rc):
    core, mate, across, diag = peers()
    start_w, wait_w = out_weights(wout_ref, wbuf, wsem, core)
    start_w()
    entry_barrier((mate, across))
    left = jnp.concatenate([at_ref[pl.ds(j, B, stride=8), :].astype(BF16) for j in range(8)], axis=1)
    exchange(left, wbuf, wait_w, lambda: None, core, mate, across, a_send, a_recv, b_send, b_recv, total,
             (sa, ra, sb, rb, sc, rc))
    per = CW // HD
    alpha = alpha_ref[1]
    beta = beta_ref[1]
    for c in range(NC):
        a2 = total[c // (NC // 2), (c % (NC // 2)) // per, :, (c % per) * HD:(c % per + 1) * HD]
        cols = slice(c * HD, (c + 1) * HD)
        out_ref[:, cols] = (alpha * h2_ref[:, cols].astype(F32) + beta * a2).astype(BF16)


def last(at, h2, alpha, beta, w_out):
    return pl.pallas_call(
        last_kernel,
        out_shape=jax.ShapeDtypeStruct((B, D), BF16),
        in_specs=[vmem_spec(), vmem_spec(), smem_spec(), smem_spec(), any_spec()],
        out_specs=vmem_spec(),
        scratch_shapes=exchange_scratch(),
        compiler_params=pltpu.CompilerParams(vmem_limit_bytes=VMEM_LIMIT, collective_id=1, has_side_effects=True),
        name="last",
    )(at, h2, alpha, beta, w_out)


def solution(mesh):
    row_spec = P('dp', None)
    cache_spec = P('dp', 'tp', None, None)
    in_specs = (row_spec, P('dp'), cache_spec, cache_spec, cache_spec, P(None), P(None, None, 'tp', None),
                P(None, 'tp', None), P('tp'), P('tp', None), P('tp', None, None), P(None),
                P(None, 'tp', None, None), P('tp', None, None), P(None), P(None))
    out_specs = (row_spec, cache_spec, cache_spec, cache_spec)

    def local_step(hidden, cache_len, lin_state, k_cache, v_cache, norm_first, w_qkv, w_gate, slopes, out_norm,
                   w_out_lin, norm_second, w_attn, w_out_attn, mix_alpha, mix_beta):
        g1 = norm_first.reshape(NC, HD)
        g2 = norm_second.reshape(NC, HD)
        wa = jnp.transpose(w_attn, (0, 2, 1, 3)).reshape(WA_ROWS, HD)
        state_out, og, ss, h1 = lightning(hidden, g1, slopes, out_norm, lin_state, w_qkv, w_gate)
        q, kn, vn, h2 = middle(og, ss, h1, g2, mix_alpha, mix_beta, cache_len, w_out_lin.reshape(HL * HD, D), wa)
        at, k_out, v_out = attention(cache_len, q, kn, vn, k_cache, v_cache)
        hidden_out = last(at, h2, mix_alpha, mix_beta, w_out_attn.reshape(HL * HD, D))
        return hidden_out, state_out, k_out, v_out

    return jax.shard_map(local_step, mesh=mesh, in_specs=in_specs, out_specs=out_specs, check_vma=False)
```

time: 167 us -> 86.8 us (0.52)
  Pallas kernels: 0 us -> 84.2 us
  waiting for transfers between devices: 58.1 us -> 0 us
  matrix products: 54.1 us -> 0 us
  other arithmetic: 29.4 us -> 0 us
  between operations: 14.3 us -> 0.66 us
  blocking collectives: 8.63 us -> 0 us
    pallas_call x0 -> x4, Pallas kernels: none -> 84.2 us  [the longest x1 29.7 us: lightning(): pl.pallas_call(lightning_kernel, out_shape=[jax.ShapeDtypeStruct((B, HL,...]
    psum x2 -> x0, waiting for transfers between devices: 58.1 us -> none  [the longest x1 29.7 us: local_step(): attn_out = lax.psum(attn_part, 'tp')]
    dot_general x6 -> x0, matrix products: 48.2 us -> none  [the longest x1 12.4 us: local_step(): jnp.einsum('bd,dchk->bchk', h_first, w_qkv, preferred_element_type=jnp.fl...]
    select_n x1 -> x0, other arithmetic: 13.3 us -> none  [local_step(): k_out = jnp.where(write_mask, key_new, k_cache)]
    psum x1 -> x0, blocking collectives: 8.63 us -> none  [local_step(): sq_sum = lax.psum(jnp.sum(lin_attn * lin_attn, axis=(1, 2)), 'tp')]
    add x1 -> x0, other arithmetic: 7.89 us -> none  [local_step(): decay_rate * lin_state]
    sub x1 -> x0, matrix products: 5.84 us -> none  [local_step(): jax.nn.softmax(jnp.where(valid_mask, scores, -jnp.inf), axis=-1)]
    reduce_sum x3 -> x0, other arithmetic: 3.88 us -> none  [the longest x2 3.75 us: rms_scale(): jnp.mean(wide_vals * wide_vals, axis=-1, keepdims=True) + EPS]
  transfers between devices with their start and end apart: 2 -> 0, of which waited for: 2 -> 0; matrix products, arithmetic and copies ran while one was open for 1% -> 0% of each run, Pallas kernels for 0% -> 0%
where the time goes in v1:
time: 86.8 us; the launch traced here: 86.5 us
  Pallas kernels  84.2 us (97%)
  local copies, waits for them, and re-layouts  1.67 us (2%)
    pallas_call x1, Pallas kernels, lightning(): pl.pallas_call(lightning_kernel, out_shape=[jax.ShapeDtypeStruct((B, HL,...  29.7 us
    pallas_call x1, Pallas kernels, middle(): pl.pallas_call(mid_kernel, out_shape=[jax.ShapeDtypeStruct((B * 8, HD), F...  21.5 us
    pallas_call x1, Pallas kernels, attention(): pl.pallas_call(attention_kernel, out_shape=[jax.ShapeDtypeStruct((B * 8,...  19.6 us
    pallas_call x1, Pallas kernels, last(): pl.pallas_call(last_kernel, out_shape=jax.ShapeDtypeStruct((B, D), BF16),...  13.4 us

profile of v1, /device:TPU:0, one launch (start us, length us, event | category | flops | bytes accessed | tf_op | source)
XLA Modules:
  0.0 86.5 jit_solution(7603251511543305840)
XLA Ops:
  0.6 29.7 %lightning.1 = (f32[32,8,128,128]{3,2,1,0:T(8,128)}, f32[32,1024]{1,0:T(8,128)}, f32[32,128]{1,0:T(8,128)}, bf16[32,4096]{1,0:T(8,128)(2,1)}) custom-call(bf16[32,4096]{1,0:T(8,128)(2,1)} %hid_ref.1, f32[32,128]{1,0:T(8,128)} %bitcast.10, f32[8]{0:T(128)} %slopes_ref.1, f32[8,128]{1,0:T(8,128)} %onorm_ref.1, f32[32,8,128,128]{3,2,1,0:T(8,128)} %state_ref.1, ...), custom_call_target="tpu_custom_call" | custom-call | tf_op jit(solution)/shard_map/lightning/pallas_call | solution.py:156
  30.3 21.5 %middle.1 = (f32[256,128]{1,0:T(8,128)}, f32[2,32,128]{2,1,0:T(8,128)}, f32[2,32,128]{2,1,0:T(8,128)}, bf16[32,4096]{1,0:T(8,128)(2,1)}) custom-call(f32[32,1024]{1,0:T(8,128)} %get-tuple-element.15.og_ref, f32[32,128]{1,0:T(8,128)} %get-tuple-element.16.ss_ref, bf16[32,4096]{1,0:T(8,128)(2,1)} %get-tuple-element.17.h1_ref, f32[32,128]{1,0:T(8,128)} %bitcast.11, ...), custom_call_target="tpu_custom_call" | custom-call | tf_op jit(solution)/shard_map/middle/pallas_call | solution.py:388
  51.8 19.6 %attention.1 = (f32[256,128]{1,0:T(8,128)}, bf16[32,2,512,128]{3,2,1,0:T(8,128)(2,1)}, bf16[32,2,512,128]{3,2,1,0:T(8,128)(2,1)}) custom-call(s32[32]{0:T(128)} %len_ref.3, f32[256,128]{1,0:T(8,128)} %get-tuple-element.18.q_ref, f32[2,32,128]{2,1,0:T(8,128)} %get-tuple-element.19.kn_ref, f32[2,32,128]{2,1,0:T(8,128)} %get-tuple-element.20.vn_ref, ...), custom_call_target="tpu_custom_call" | custom-call | tf_op jit(solution)/shard_map/attention/pallas_call | solution.py:467
  71.5 13.4 %last.1 = bf16[32,4096]{1,0:T(8,128)(2,1)} custom-call(f32[256,128]{1,0:T(8,128)} %get-tuple-element.21.at_ref, bf16[32,4096]{1,0:T(8,128)(2,1)} %get-tuple-element.22.h2_ref, f32[2]{0:T(128)} %alpha_ref.3, f32[2]{0:T(128)} %beta_ref.3, bf16[1024,4096]{1,0:T(8,128)(2,1)} %bitcast.9), custom_call_target="tpu_custom_call" | custom-call | tf_op jit(solution)/shard_map/last/pallas_call | solution.py:503
  84.9 1.7 %copy.21 = bf16[32,4096]{1,0:T(8,128)(2,1)} copy(bf16[32,4096]{1,0:T(8,128)(2,1)} %last.1) | data formatting | bytes 524288

commit v2 on v1

--- a/solution.py
+++ b/solution.py
@@ -13,7 +13,7 @@
 MESH = pl.DeviceIdType.MESH
 F32 = jnp.float32
 BF16 = jnp.bfloat16
-VMEM_LIMIT = 62 * 1024 * 1024
+MIB = 1024 * 1024
 
 B = 32
 D = 4096
@@ -24,9 +24,9 @@
 T = 512
 NC = D // HD
 
-DCH = 128
+DCH = 256
 STEPS = D // DCH
-RING = 8
+RING = 4
 
 
 def any_spec():
@@ -47,7 +47,7 @@
 
 def lightning_kernel(hid_ref, g1_ref, slopes_ref, onorm_ref, state_ref, wqkv_ref, wgate_ref,
                      sout_ref, og_ref, ss_ref, h1_ref,
-                     wbuf, sbuf, ebuf, lbuf, acc, qk_t, v_s, o_s, wsem, ssem, osem):
+                     wbuf, sbuf, hstack, ebuf, lbuf, acc, qk_t, v_s, o_s, wsem, ssem, osem):
     def w_copies(step, slot):
         rows = pl.ds(step * DCH, DCH)
         out = [pltpu.make_async_copy(wqkv_ref.at[rows, c], wbuf.at[slot, c], wsem.at[slot, c]) for c in range(3)]
@@ -75,27 +75,30 @@
         x = hid_ref[:, c * HD:(c + 1) * HD].astype(F32)
         h1 = (x * inv * g1_ref[c:c + 1, :]).astype(BF16)
         h1_ref[:, c * HD:(c + 1) * HD] = h1
-        lbuf[c * B:(c + 1) * B, 0:HD] = h1
+        hstack[c * B:(c + 1) * B, :] = h1
     for n in range(4):
         spread = jnp.where(rr // 8 + 32 * n == dd, 1.0, 0.0).astype(BF16)
         for c in range(NC // 8):
-            e = dot(lbuf[c * 256:(c + 1) * 256, 0:HD], spread).astype(BF16)
+            e = dot(hstack[c * 256:(c + 1) * 256, :], spread).astype(BF16)
             for k in range(8):
-                ebuf[c * 8 + k, :, n * 256:(n + 1) * 256] = e[k * B:(k + 1) * B, :]
+                cc = c * 8 + k
+                off = (cc % (DCH // HD)) * 1024 + n * 256
+                ebuf[cc // (DCH // HD), :, off:off + 256] = e[k * B:(k + 1) * B, :]
 
     acc[...] = jnp.zeros_like(acc)
-    lane = lax.broadcasted_iota(jnp.int32, (B, 1024), 1) % 8
+    lane = lax.broadcasted_iota(jnp.int32, (B, DCH * HL), 1) % 8
 
     def step_fn(i, carry):
         slot = lax.rem(i, RING)
-        s_copy(i).start()
+        for k in range(B // STEPS):
+            s_copy(i * (B // STEPS) + k).start()
         e = ebuf[i]
         for h in range(HL):
             keep = jnp.where(lane == h, 1.0, 0.0).astype(BF16)
             lbuf[h * B:(h + 1) * B, :] = e * keep
         for cp in w_copies(i, slot):
             cp.wait()
-        left = lbuf[0:HL * B, :]
+        left = lbuf[...]
         for pair in range(2):
             right = jnp.concatenate([wbuf[slot, 2 * pair].reshape(DCH * HL, HD),
                                      wbuf[slot, 2 * pair + 1].reshape(DCH * HL, HD)], axis=1)
@@ -162,8 +165,9 @@
         scratch_shapes=[
             pltpu.VMEM((RING, 4, DCH, HL, HD), BF16),
             pltpu.VMEM((B, HL, HD, HD), F32),
+            pltpu.VMEM((NC * B, HD), BF16),
             pltpu.VMEM((STEPS, B, DCH * HL), BF16),
-            pltpu.VMEM((1024, 1024), BF16),
+            pltpu.VMEM((HL * B, DCH * HL), BF16),
             pltpu.VMEM((2, HL * B, 2 * HD), F32),
             pltpu.VMEM((HL, HD, 2 * B), BF16),
             pltpu.VMEM((HL, B, HD), BF16),
@@ -172,7 +176,7 @@
             pltpu.SemaphoreType.DMA((B,)),
             pltpu.SemaphoreType.DMA((B,)),
         ],
-        compiler_params=pltpu.CompilerParams(vmem_limit_bytes=VMEM_LIMIT),
+        compiler_params=pltpu.CompilerParams(vmem_limit_bytes=40 * MIB),
         name="lightning",
     )(hidden, g1, slopes, out_norm, lin_state, w_qkv, w_gate)
 
@@ -297,9 +301,9 @@
 
 
 def mid_kernel(og_ref, ss_ref, h1_ref, g2_ref, alpha_ref, beta_ref, len_ref, wout_ref, wattn_ref,
-               q_ref, kn_ref, vn_ref, h2_ref,
+               k_ref, v_ref, q_ref, kn_ref, vn_ref, h2_ref, kbuf, vbuf,
                wbuf, a_send, a_recv, b_send, b_recv, total, wsem, sa, ra, sb, rb, sc, rc,
-               wraw, wide, w2, ss_recv, wasem, ss_s, ss_r):
+               wraw, wide, w2, ss_recv, wasem, ss_s, ss_r, csem):
     core, mate, across, diag = peers()
     start_w, wait_w = out_weights(wout_ref, wbuf, wsem, core)
     start_w()
@@ -312,6 +316,9 @@
         return carry
 
     lax.fori_loop(0, WA_CH, wa_start, 0)
+    caches = [pltpu.make_async_copy(k_ref, kbuf, csem.at[0]), pltpu.make_async_copy(v_ref, vbuf, csem.at[1])]
+    for cp in caches:
+        cp.start()
     entry_barrier((mate, across, diag))
     ss_copies = []
     for n, dev in enumerate((mate, across, diag)):
@@ -382,16 +389,19 @@
                 kn_ref[kv] = turn(x).astype(BF16).astype(F32)
             else:
                 vn_ref[kv] = x.astype(BF16).astype(F32)
-
-
-def middle(og, ss, h1, g2, alpha, beta, cache_len, w_out, w_attn):
+    for cp in caches:
+        cp.wait()
+
+
+def middle(og, ss, h1, g2, alpha, beta, cache_len, w_out, w_attn, k_cache, v_cache):
     return pl.pallas_call(
         mid_kernel,
         out_shape=[jax.ShapeDtypeStruct((B * 8, HD), F32), jax.ShapeDtypeStruct((KV, B, HD), F32),
-                   jax.ShapeDtypeStruct((KV, B, HD), F32), jax.ShapeDtypeStruct((B, D), BF16)],
+                   jax.ShapeDtypeStruct((KV, B, HD), F32), jax.ShapeDtypeStruct((B, D), BF16),
+                   pltpu.VMEM((B, KV, T, HD), BF16), pltpu.VMEM((B, KV, T, HD), BF16)],
         in_specs=[vmem_spec(), vmem_spec(), vmem_spec(), vmem_spec(), smem_spec(), smem_spec(), smem_spec(),
-                  any_spec(), any_spec()],
-        out_specs=[vmem_spec()] * 4,
+                  any_spec(), any_spec(), any_spec(), any_spec()],
+        out_specs=[vmem_spec()] * 6,
         scratch_shapes=exchange_scratch() + [
             pltpu.VMEM((WA_CH, WA_STEP, HD), BF16),
             pltpu.VMEM((WA_STEP, HD), F32),
@@ -400,60 +410,55 @@
             pltpu.SemaphoreType.DMA((WA_CH,)),
             pltpu.SemaphoreType.DMA((3,)),
             pltpu.SemaphoreType.DMA((3,)),
+            pltpu.SemaphoreType.DMA((2,)),
         ],
-        compiler_params=pltpu.CompilerParams(vmem_limit_bytes=VMEM_LIMIT, collective_id=0, has_side_effects=True),
+        compiler_params=pltpu.CompilerParams(vmem_limit_bytes=37 * MIB, collective_id=0, has_side_effects=True),
         name="middle",
-    )(og, ss, h1, g2, alpha, beta, cache_len, w_out, w_attn)
-
-
-def attention_kernel(len_ref, q_ref, kn_ref, vn_ref, k_ref, v_ref, at_ref, ko_ref, vo_ref,
-                     kbuf, vbuf, isem, osem):
-    def ins(b):
-        return (pltpu.make_async_copy(k_ref.at[b], kbuf.at[b], isem.at[0, b]),
-                pltpu.make_async_copy(v_ref.at[b], vbuf.at[b], isem.at[1, b]))
-
+    )(og, ss, h1, g2, alpha, beta, cache_len, w_out, w_attn, k_cache, v_cache)
+
+
+ROWS = 4
+
+
+def attention_kernel(len_ref, q_ref, kn_ref, vn_ref, kin_ref, vin_ref, at_ref, ko_ref, vo_ref, kbuf, vbuf, osem):
     def outs(b):
         return (pltpu.make_async_copy(kbuf.at[b], ko_ref.at[b], osem.at[0, b]),
                 pltpu.make_async_copy(vbuf.at[b], vo_ref.at[b], osem.at[1, b]))
 
-    def start_in(b, carry):
-        for cp in ins(b):
-            cp.start()
-        return carry
-
-    lax.fori_loop(0, B, start_in, 0)
     row8 = lax.broadcasted_iota(jnp.int32, (8, HD), 0)
     row16 = lax.broadcasted_iota(jnp.int32, (16, HD), 0)
     tpos = lax.broadcasted_iota(jnp.int32, (8, T), 1)
 
-    def body(b, carry):
-        for cp in ins(b):
-            cp.wait()
-        p = len_ref[b]
-        base = pl.multiple_of((p // 16) * 16, 16)
-        hit = row16 == p - base
-        for kv in range(KV):
-            kn = kn_ref[kv, pl.ds(b, 1), :]
-            vn = vn_ref[kv, pl.ds(b, 1), :]
-            old_k = kbuf[b, kv, pl.ds(base, 16), :].astype(F32)
-            old_v = vbuf[b, kv, pl.ds(base, 16), :].astype(F32)
-            kbuf[b, kv, pl.ds(base, 16), :] = jnp.where(hit, kn, old_k).astype(BF16)
-            vbuf[b, kv, pl.ds(base, 16), :] = jnp.where(hit, vn, old_v).astype(BF16)
-        for cp in outs(b):
-            cp.start()
-        q = q_ref[pl.ds(b * 8, 8), :]
-        q2 = jnp.concatenate([jnp.where(row8 < 4, q, 0.0), jnp.where(row8 < 4, 0.0, q)], axis=1).astype(BF16)
-        k2 = jnp.concatenate([kbuf[b, 0], kbuf[b, 1]], axis=1)
-        s = lax.dot_general(q2, k2, (((1,), (1,)), ((), ())), preferred_element_type=F32) * HD ** -0.5
-        s = jnp.where(tpos <= p, s, -jnp.inf)
-        e = jnp.exp(s - jnp.max(s, axis=1, keepdims=True))
-        pr = (e / jnp.sum(e, axis=1, keepdims=True)).astype(BF16)
-        v2 = jnp.concatenate([vbuf[b, 0], vbuf[b, 1]], axis=1)
-        o = dot(pr, v2)
-        at_ref[pl.ds(b * 8, 8), :] = jnp.where(row8 < 4, o[:, 0:HD], o[:, HD:])
+    def body(i, carry):
+        rows = [i * ROWS + r for r in range(ROWS)]
+        lens = [len_ref[b] for b in rows]
+        for b, p in zip(rows, lens):
+            base = pl.multiple_of((p // 16) * 16, 16)
+            hit = row16 == p - base
+            for kv in range(KV):
+                for buf, new in ((kbuf, kn_ref), (vbuf, vn_ref)):
+                    old = buf[b, kv, pl.ds(base, 16), :].astype(F32)
+                    buf[b, kv, pl.ds(base, 16), :] = jnp.where(hit, new[kv, pl.ds(b, 1), :], old).astype(BF16)
+        for b in rows:
+            for cp in outs(b):
+                cp.start()
+        scores = []
+        for b, p in zip(rows, lens):
+            q = q_ref[pl.ds(b * 8, 8), :]
+            q2 = jnp.concatenate([jnp.where(row8 < 4, q, 0.0), jnp.where(row8 < 4, 0.0, q)], axis=1).astype(BF16)
+            k2 = jnp.concatenate([kbuf[b, 0], kbuf[b, 1]], axis=1)
+            s = lax.dot_general(q2, k2, (((1,), (1,)), ((), ())), preferred_element_type=F32) * HD ** -0.5
+            scores.append(jnp.where(tpos <= p, s, -jnp.inf))
+        tops = [jnp.max(s, axis=1, keepdims=True) for s in scores]
+        es = [jnp.exp(s - m) for s, m in zip(scores, tops)]
+        sums = [jnp.sum(e, axis=1, keepdims=True) for e in es]
+        prs = [(e / z).astype(BF16) for e, z in zip(es, sums)]
+        for b, pr in zip(rows, prs):
+            o = dot(pr, jnp.concatenate([vbuf[b, 0], vbuf[b, 1]], axis=1))
+            at_ref[pl.ds(b * 8, 8), :] = jnp.where(row8 < 4, o[:, 0:HD], o[:, HD:])
         return carry
 
-    lax.fori_loop(0, B, body, 0)
+    lax.fori_loop(0, B // ROWS, body, 0)
 
     def drain(b, carry):
         for cp in outs(b):
@@ -463,22 +468,18 @@
     lax.fori_loop(0, B, drain, 0)
 
 
-def attention(cache_len, q, kn, vn, k_cache, v_cache):
+def attention(cache_len, q, kn, vn, kbuf, vbuf):
     return pl.pallas_call(
         attention_kernel,
-        out_shape=[jax.ShapeDtypeStruct((B * 8, HD), F32), jax.ShapeDtypeStruct((B, KV, T, HD), BF16),
-                   jax.ShapeDtypeStruct((B, KV, T, HD), BF16)],
-        in_specs=[smem_spec(), vmem_spec(), vmem_spec(), vmem_spec(), any_spec(), any_spec()],
-        out_specs=[vmem_spec(), any_spec(), any_spec()],
-        scratch_shapes=[
-            pltpu.VMEM((B, KV, T, HD), BF16),
-            pltpu.VMEM((B, KV, T, HD), BF16),
-            pltpu.SemaphoreType.DMA((2, B)),
-            pltpu.SemaphoreType.DMA((2, B)),
-        ],
-        compiler_params=pltpu.CompilerParams(vmem_limit_bytes=VMEM_LIMIT),
+        out_shape=[jax.ShapeDtypeStruct((B * 8, HD), F32), pltpu.HBM((B, KV, T, HD), BF16),
+                   pltpu.HBM((B, KV, T, HD), BF16), pltpu.VMEM((B, KV, T, HD), BF16), pltpu.VMEM((B, KV, T, HD), BF16)],
+        in_specs=[smem_spec(), vmem_spec(), vmem_spec(), vmem_spec(), vmem_spec(), vmem_spec()],
+        out_specs=[vmem_spec(), any_spec(), any_spec(), vmem_spec(), vmem_spec()],
+        input_output_aliases={4: 3, 5: 4},
+        scratch_shapes=[pltpu.SemaphoreType.DMA((2, B))],
+        compiler_params=pltpu.CompilerParams(vmem_limit_bytes=4 * MIB),
         name="attention",
-    )(cache_len, q, kn, vn, k_cache, v_cache)
+    )(cache_len, q, kn, vn, kbuf, vbuf)[:3]
 
 
 def last_kernel(at_ref, h2_ref, alpha_ref, beta_ref, wout_ref, out_ref,
@@ -506,7 +507,7 @@
         in_specs=[vmem_spec(), vmem_spec(), smem_spec(), smem_spec(), any_spec()],
         out_specs=vmem_spec(),
         scratch_shapes=exchange_scratch(),
-        compiler_params=pltpu.CompilerParams(vmem_limit_bytes=VMEM_LIMIT, collective_id=1, has_side_effects=True),
+        compiler_params=pltpu.CompilerParams(vmem_limit_bytes=16 * MIB, collective_id=1, has_side_effects=True),
         name="last",
     )(at, h2, alpha, beta, w_out)
 
@@ -521,13 +522,17 @@
 
     def local_step(hidden, cache_len, lin_state, k_cache, v_cache, norm_first, w_qkv, w_gate, slopes, out_norm,
                    w_out_lin, norm_second, w_attn, w_out_attn, mix_alpha, mix_beta):
+        def hbm(x):
+            return pltpu.with_memory_space_constraint(x, pltpu.HBM)
+
         g1 = norm_first.reshape(NC, HD)
         g2 = norm_second.reshape(NC, HD)
         wa = jnp.transpose(w_attn, (0, 2, 1, 3)).reshape(WA_ROWS, HD)
-        state_out, og, ss, h1 = lightning(hidden, g1, slopes, out_norm, lin_state, w_qkv, w_gate)
-        q, kn, vn, h2 = middle(og, ss, h1, g2, mix_alpha, mix_beta, cache_len, w_out_lin.reshape(HL * HD, D), wa)
-        at, k_out, v_out = attention(cache_len, q, kn, vn, k_cache, v_cache)
-        hidden_out = last(at, h2, mix_alpha, mix_beta, w_out_attn.reshape(HL * HD, D))
+        state_out, og, ss, h1 = lightning(hidden, g1, slopes, out_norm, hbm(lin_state), hbm(w_qkv), hbm(w_gate))
+        q, kn, vn, h2, kbuf, vbuf = middle(og, ss, h1, g2, mix_alpha, mix_beta, cache_len,
+                                           hbm(w_out_lin.reshape(HL * HD, D)), hbm(wa), hbm(k_cache), hbm(v_cache))
+        at, k_out, v_out = attention(cache_len, q, kn, vn, kbuf, vbuf)
+        hidden_out = last(at, h2, mix_alpha, mix_beta, hbm(w_out_attn.reshape(HL * HD, D)))
         return hidden_out, state_out, k_out, v_out
 
     return jax.shard_map(local_step, mesh=mesh, in_specs=in_specs, out_specs=out_specs, check_vma=False)

time: 86.8 us -> 72 us (0.83)
  Pallas kernels: 84.2 us -> 67.3 us
  local copies, waits for them, and re-layouts: 1.67 us -> 3.72 us
    pallas_call x1, Pallas kernels: 19.6 us -> 7.91 us  [attention(): pl.pallas_call(attention_kernel, out_shape=[jax.ShapeDtypeStruct((B * 8,...]
    pallas_call x1, Pallas kernels: 29.7 us -> 26.8 us  [lightning(): pl.pallas_call(lightning_kernel, out_shape=[jax.ShapeDtypeStruct((B, HL,...]
    unnamed x1 -> x17, local copies, waits for them, and re-layouts: 1.67 us -> 3.72 us
    pallas_call x1, Pallas kernels: 13.4 us -> 12.2 us  [last(): pl.pallas_call(last_kernel, out_shape=jax.ShapeDtypeStruct((B, D), BF16),...]
    pallas_call x1, Pallas kernels: 21.5 us -> 20.4 us  [middle(): pl.pallas_call(mid_kernel, out_shape=[jax.ShapeDtypeStruct((B * 8, HD), F...]
where the time goes in v2:
time: 72 us; the launch traced here: 71.7 us
  Pallas kernels  67.3 us (93%)
  local copies, waits for them, and re-layouts  3.72 us (5%)
    pallas_call x1, Pallas kernels, lightning(): pl.pallas_call(lightning_kernel, out_shape=[jax.ShapeDtypeStruct((B, HL,...  26.8 us
    pallas_call x1, Pallas kernels, middle(): pl.pallas_call(mid_kernel, out_shape=[jax.ShapeDtypeStruct((B * 8, HD), F...  20.4 us
    pallas_call x1, Pallas kernels, last(): pl.pallas_call(last_kernel, out_shape=jax.ShapeDtypeStruct((B, D), BF16),...  12.2 us
    pallas_call x1, Pallas kernels, attention(): pl.pallas_call(attention_kernel, out_shape=[jax.ShapeDtypeStruct((B * 8,...  7.91 us
    unnamed x17, local copies, waits for them, and re-layouts  3.72 us

profile of v2, /device:TPU:0, one launch (start us, length us, event | category | flops | bytes accessed | tf_op | source)
XLA Modules:
  0.0 71.7 jit_solution(12002777613930617078)
XLA Ops:
  0.6 0.0 copy-start
  0.6 0.9 %copy-done = bf16[32,4096]{1,0:T(8,128)(2,1)S(1)} copy-done((bf16[32,4096]{1,0:T(8,128)(2,1)S(1)}, bf16[32,4096]{1,0:T(8,128)(2,1)}, u32[]{:S(2)}) %copy-start) | copy-done | bytes 262168
  1.6 0.0 copy-start.1
  1.6 0.7 copy-done.1
  2.3 0.0 copy-start.3
  2.3 0.7 copy-done.3
  3.0 0.0 copy-start.7
  3.0 0.7 copy-done.7
  3.6 0.0 copy-start.2
  3.6 0.0 copy-start.4
  3.7 0.0 copy-start.5
  3.7 0.0 copy-start.6
  3.7 26.8 %lightning.1 = (f32[32,8,128,128]{3,2,1,0:T(8,128)}, f32[32,1024]{1,0:T(8,128)S(1)}, f32[32,128]{1,0:T(8,128)S(1)}, bf16[32,4096]{1,0:T(8,128)(2,1)S(1)}) custom-call(bf16[32,4096]{1,0:T(8,128)(2,1)S(1)} %copy-done, f32[32,128]{1,0:T(8,128)S(1)} %bitcast.7, f32[8]{0:T(128)S(1)} %copy-done.7, f32[8,128]{1,0:T(8,128)S(1)} %copy-done.3, ...), custom_call_target="tpu_custom_call" | custom-call | tf_op jit(solution)/shard_map/lightning/pallas_call | solution.py:159
  30.5 0.0 copy-done.2
  30.5 0.0 copy-done.4
  30.5 0.0 copy-done.5
  30.5 0.0 copy-done.6
  30.5 20.4 %middle.1 = (f32[256,128]{1,0:T(8,128)S(1)}, f32[2,32,128]{2,1,0:T(8,128)S(1)}, f32[2,32,128]{2,1,0:T(8,128)S(1)}, bf16[32,4096]{1,0:T(8,128)(2,1)S(1)}, bf16[32...) custom-call(f32[32,1024]{1,0:T(8,128)S(1)} %get-tuple-element.17.og_ref, ...), custom_call_target="tpu_custom_call" | custom-call | tf_op jit(solution)/shard_map/middle/pallas_call | solution.py:397
  50.9 7.9 %attention.1 = (f32[256,128]{1,0:T(8,128)S(1)}, bf16[32,2,512,128]{3,2,1,0:T(8,128)(2,1)}, bf16[32,2,512,128]{3,2,1,0:T(8,128)(2,1)}, bf16[32,2,512,128]{3,2,1,0:T(8,128)(2,1)S(1)}, bf16[32,2,512,128]{3,2,1,0:T(8,128)(2,1)S(1)}) custom-call(s32[32]{0:T(128)S(1)} %copy-done.4, ...), custom_call_target="tpu_custom_call", output_to_operand_aliasing={{3}: (4, {}), {4}: (5, {})} | custom-call | tf_op jit(solution)/shard_map/attention/pallas_call | solution.py:472
  58.8 12.2 %last.1 = bf16[32,4096]{1,0:T(8,128)(2,1)S(1)} custom-call(f32[256,128]{1,0:T(8,128)S(1)} %get-tuple-element.25.at_ref, bf16[32,4096]{1,0:T(8,128)(2,1)S(1)} %get-tuple-element.26.h2_ref, f32[2]{0:T(128)S(1)} %copy-done.5, f32[2]{0:T(128)S(1)} %copy-done.6, bf16[1024,4096]{1,0:T(8,128)(2,1)} %bitcast.11), custom_call_target="tpu_custom_call" | custom-call | tf_op jit(solution)/shard_map/last/pallas_call | solution.py:504
  71.0 0.7 copy.25
Async XLA Ops:
  0.6 1.0 %copy-start = (bf16[32,4096]{1,0:T(8,128)(2,1)S(1)}, bf16[32,4096]{1,0:T(8,128)(2,1)}, u32[]{:S(2)}) copy-start(bf16[32,4096]{1,0:T(8,128)(2,1)} %hid_ref.1) | copy-start | bytes 786436
  1.6 0.7 %copy-start.1 = (f32[4096]{0:T(1024)S(1)}, f32[4096]{0:T(1024)}, u32[]{:S(2)}) copy-start(f32[4096]{0:T(1024)} %param.21) | copy-start | bytes 49156
  2.3 0.7 copy-start.3
  3.0 0.7 copy-start.7
  3.6 26.8 %copy-start.2 = (f32[4096]{0:T(1024)S(1)}, f32[4096]{0:T(1024)}, u32[]{:S(2)}) copy-start(f32[4096]{0:T(1024)} %param.27) | copy-start | bytes 49156
  3.6 26.8 %copy-start.4 = (s32[32]{0:T(128)S(1)}, s32[32]{0:T(128)}, u32[]{:S(2)}) copy-start(s32[32]{0:T(128)} %len_ref.3) | copy-start | bytes 388
  3.7 26.9 %copy-start.5 = (f32[2]{0:T(128)S(1)}, f32[2]{0:T(128)}, u32[]{:S(2)}) copy-start(f32[2]{0:T(128)} %alpha_ref.3) | copy-start | bytes 28
  3.7 26.9 %copy-start.6 = (f32[2]{0:T(128)S(1)}, f32[2]{0:T(128)}, u32[]{:S(2)}) copy-start(f32[2]{0:T(128)} %beta_ref.3) | copy-start | bytes 28

commit v3 on v2

--- a/solution.py
+++ b/solution.py
@@ -27,6 +27,7 @@
 DCH = 256
 STEPS = D // DCH
 RING = 4
+EARLY = 24
 
 
 def any_spec():
@@ -45,14 +46,13 @@
     return jnp.dot(a, b, preferred_element_type=F32)
 
 
-def lightning_kernel(hid_ref, g1_ref, slopes_ref, onorm_ref, state_ref, wqkv_ref, wgate_ref,
-                     sout_ref, og_ref, ss_ref, h1_ref,
-                     wbuf, sbuf, hstack, ebuf, lbuf, acc, qk_t, v_s, o_s, wsem, ssem, osem):
+def lightning_kernel(hid_hbm, g1_hbm, slopes_hbm, onorm_hbm, state_ref, wqkv_ref, wgate_ref,
+                     sout_ref, og_ref, ss_ref, h1_ref, hid_ref, g1_ref, onorm_ref, slopes_ref,
+                     wbuf, gbuf, sbuf, hstack, ebuf, lbuf, acc, qk_t, v_s, o_s, psem, wsem, ssem, osem):
     def w_copies(step, slot):
         rows = pl.ds(step * DCH, DCH)
-        out = [pltpu.make_async_copy(wqkv_ref.at[rows, c], wbuf.at[slot, c], wsem.at[slot, c]) for c in range(3)]
-        out.append(pltpu.make_async_copy(wgate_ref.at[rows], wbuf.at[slot, 3], wsem.at[slot, 3]))
-        return out
+        return (pltpu.make_async_copy(wqkv_ref.at[rows], wbuf.at[slot], wsem.at[slot, 0]),
+                pltpu.make_async_copy(wgate_ref.at[rows], gbuf.at[slot], wsem.at[slot, 1]))
 
     def s_copy(b):
         return pltpu.make_async_copy(state_ref.at[b], sbuf.at[b], ssem.at[b])
@@ -60,9 +60,15 @@
     def o_copy(b):
         return pltpu.make_async_copy(sbuf.at[b], sout_ref.at[b], osem.at[b])
 
+    small = [pltpu.make_async_copy(src, dst, psem.at[n]) for n, (src, dst) in enumerate(
+        ((hid_hbm, hid_ref), (g1_hbm, g1_ref), (onorm_hbm, onorm_ref), (slopes_hbm, slopes_ref)))]
+    for cp in small:
+        cp.start()
     for i in range(RING):
         for cp in w_copies(i, i):
             cp.start()
+    for cp in small:
+        cp.wait()
 
     sq = jnp.zeros((B, HD), F32)
     for c in range(NC):
@@ -90,8 +96,11 @@
 
     def step_fn(i, carry):
         slot = lax.rem(i, RING)
-        for k in range(B // STEPS):
-            s_copy(i * (B // STEPS) + k).start()
+        @pl.when(i >= STEPS - EARLY // 2)
+        def _():
+            for k in range(2):
+                s_copy((i - (STEPS - EARLY // 2)) * 2 + k).start()
+
         e = ebuf[i]
         for h in range(HL):
             keep = jnp.where(lane == h, 1.0, 0.0).astype(BF16)
@@ -100,8 +109,8 @@
             cp.wait()
         left = lbuf[...]
         for pair in range(2):
-            right = jnp.concatenate([wbuf[slot, 2 * pair].reshape(DCH * HL, HD),
-                                     wbuf[slot, 2 * pair + 1].reshape(DCH * HL, HD)], axis=1)
+            second = wbuf[slot, :, 1] if pair == 0 else gbuf[slot]
+            right = jnp.concatenate([wbuf[slot, :, 2 * pair].reshape(DCH * HL, HD), second.reshape(DCH * HL, HD)], axis=1)
             acc[pair] += dot(left, right)
 
         @pl.when(i + RING < STEPS)
@@ -111,6 +120,8 @@
         return carry
 
     lax.fori_loop(0, STEPS, step_fn, 0)
+    for b in range(EARLY, B):
+        s_copy(b).start()
 
     for h in range(HL):
         rows = slice(h * B, (h + 1) * B)
@@ -144,9 +155,12 @@
     for h in range(HL):
         o = o_s[:, h, :]
         ss = ss + o * o
+    ss = jnp.sum(ss, axis=1, keepdims=True)
+    ss_ref[...] = jnp.broadcast_to(ss, (B, HD))
+    inv_own = lax.rsqrt(ss / (HL * HD) + EPS)
+    for h in range(HL):
         gate = jax.nn.sigmoid(acc[1, h * B:(h + 1) * B, HD:2 * HD])
-        og_ref[:, h * HD:(h + 1) * HD] = o * onorm_ref[h:h + 1, :] * gate
-    ss_ref[...] = jnp.broadcast_to(jnp.sum(ss, axis=1, keepdims=True), (B, HD))
+        og_ref[:, h * HD:(h + 1) * HD] = (o_s[:, h, :] * inv_own * onorm_ref[h:h + 1, :] * gate).astype(BF16)
 
     def drain(b, carry):
         o_copy(b).wait()
@@ -158,12 +172,17 @@
 def lightning(hidden, g1, slopes, out_norm, lin_state, w_qkv, w_gate):
     return pl.pallas_call(
         lightning_kernel,
-        out_shape=[jax.ShapeDtypeStruct((B, HL, HD, HD), F32), jax.ShapeDtypeStruct((B, HL * HD), F32),
+        out_shape=[jax.ShapeDtypeStruct((B, HL, HD, HD), F32), jax.ShapeDtypeStruct((B, HL * HD), BF16),
                    jax.ShapeDtypeStruct((B, HD), F32), jax.ShapeDtypeStruct((B, D), BF16)],
-        in_specs=[vmem_spec(), vmem_spec(), smem_spec(), vmem_spec(), any_spec(), any_spec(), any_spec()],
+        in_specs=[any_spec()] * 7,
         out_specs=[any_spec(), vmem_spec(), vmem_spec(), vmem_spec()],
         scratch_shapes=[
-            pltpu.VMEM((RING, 4, DCH, HL, HD), BF16),
+            pltpu.VMEM((B, D), BF16),
+            pltpu.VMEM((NC, HD), F32),
+            pltpu.VMEM((HL, HD), F32),
+            pltpu.SMEM((HL,), F32),
+            pltpu.VMEM((RING, DCH, 3, HL, HD), BF16),
+            pltpu.VMEM((RING, DCH, HL, HD), BF16),
             pltpu.VMEM((B, HL, HD, HD), F32),
             pltpu.VMEM((NC * B, HD), BF16),
             pltpu.VMEM((STEPS, B, DCH * HL), BF16),
@@ -172,7 +191,8 @@
             pltpu.VMEM((HL, HD, 2 * B), BF16),
             pltpu.VMEM((HL, B, HD), BF16),
             pltpu.VMEM((B, HL, HD), F32),
-            pltpu.SemaphoreType.DMA((RING, 4)),
+            pltpu.SemaphoreType.DMA((4,)),
+            pltpu.SemaphoreType.DMA((RING, 2)),
             pltpu.SemaphoreType.DMA((B,)),
             pltpu.SemaphoreType.DMA((B,)),
         ],
@@ -192,15 +212,17 @@
     chip = me // 2
     mate = (dp, chip * 2 + (1 - core))
     across = (dp, (1 - chip) * 2 + core)
-    diag = (dp, (1 - chip) * 2 + (1 - core))
-    return core, mate, across, diag
-
-
-def entry_barrier(targets):
+    return core, mate, across
+
+
+def say_here(targets):
     barrier = pltpu.get_barrier_semaphore()
     for dev in targets:
         pl.semaphore_signal(barrier, inc=1, device_id=dev, device_id_type=MESH)
-    pl.semaphore_wait(barrier, len(targets))
+
+
+def await_peers(count):
+    pl.semaphore_wait(pltpu.get_barrier_semaphore(), count)
 
 
 def rcopy(src, dst, send, recv, dev):
@@ -208,63 +230,57 @@
                                         device_id=dev, device_id_type=MESH)
 
 
-def exchange(left, wbuf, wwait, mid_work, core, mate, across,
+def exchange(left, wbuf, wwait, before_sends, pair_scale, mid_work, cross_scale, core, mate, across,
              a_send, a_recv, b_send, b_recv, total, sems):
     sa, ra, sb, rb, sc, rc = sems
-    per = CW // HD
 
     def product(half, j):
-        base = half * (NC // 2) + j * per
-        cols = []
-        for p in range(per // 2):
-            w = jnp.concatenate([wbuf[base + 2 * p], wbuf[base + 2 * p + 1]], axis=1)
-            cols.append(dot(left, w))
-        return jnp.concatenate(cols, axis=1)
-
-    a_copies, b_copies, c_copies = [], [], []
+        wwait(half, j)
+        at = half * NCH + j
+        return jnp.concatenate([dot(left, wbuf[at, :, c:c + 2 * HD]) for c in range(0, CW, 2 * HD)], axis=1)
+
+    a_copies = [rcopy(a_send.at[j], a_recv.at[j], sa.at[j], ra.at[j], mate) for j in range(NCH)]
+    b_copies = [rcopy(b_send.at[j], b_recv.at[j], sb.at[j], rb.at[j], across) for j in range(NCH)]
+    c_copies = [rcopy(total.at[core, j], total.at[core, j], sc.at[j], rc.at[j], mate) for j in range(NCH)]
+
+    def send_across(j, scale):
+        a_copies[j].wait_recv()
+        b_send[j] = b_send[j] * scale[0] + a_recv[j] * scale[1] if scale else b_send[j] + a_recv[j]
+        b_copies[j].start()
+
+    scale = None
     for j in range(NCH):
-        wwait(1 - core, j)
         a_send[j] = product(1 - core, j)
-        cp = rcopy(a_send.at[j], a_recv.at[j], sa.at[j], ra.at[j], mate)
-        cp.start()
-        a_copies.append(cp)
-        wwait(core, j)
+        if j == 0:
+            before_sends()
+        a_copies[j].start()
         b_send[j] = product(core, j)
+        if j == 1:
+            scale = pair_scale()
         if j >= 1:
-            send_across(j - 1, a_copies, b_copies, a_recv, b_send, b_recv, sb, rb, across)
-    send_across(NCH - 1, a_copies, b_copies, a_recv, b_send, b_recv, sb, rb, across)
+            send_across(j - 1, scale)
+    send_across(NCH - 1, scale)
     mid_work()
+    scale = cross_scale()
     for j in range(NCH):
         b_copies[j].wait_recv()
-        total[core, j] = b_send[j] + b_recv[j]
-        cp = rcopy(total.at[core, j], total.at[core, j], sc.at[j], rc.at[j], mate)
-        cp.start()
-        c_copies.append(cp)
+        total[core, j] = b_send[j] * scale[0] + b_recv[j] * scale[1] if scale else b_send[j] + b_recv[j]
+        c_copies[j].start()
     for j in range(NCH):
         c_copies[j].wait_recv()
-    for j in range(NCH):
-        a_copies[j].wait_send()
-        b_copies[j].wait_send()
-        c_copies[j].wait_send()
-
-
-def send_across(j, a_copies, b_copies, a_recv, b_send, b_recv, sb, rb, across):
-    a_copies[j].wait_recv()
-    b_send[j] = b_send[j] + a_recv[j]
-    cp = rcopy(b_send.at[j], b_recv.at[j], sb.at[j], rb.at[j], across)
-    cp.start()
-    b_copies.append(cp)
+    for cp in a_copies + b_copies + c_copies:
+        cp.wait_send()
 
 
 def exchange_scratch():
     return [
-        pltpu.VMEM((NC, HL * HD, HD), BF16),
+        pltpu.VMEM((2 * NCH, HL * HD, CW), BF16),
         pltpu.VMEM((NCH, B, CW), F32),
         pltpu.VMEM((NCH, B, CW), F32),
         pltpu.VMEM((NCH, B, CW), F32),
         pltpu.VMEM((NCH, B, CW), F32),
         pltpu.VMEM((2, NCH, B, CW), F32),
-        pltpu.SemaphoreType.DMA((NC,)),
+        pltpu.SemaphoreType.DMA((2 * NCH,)),
         pltpu.SemaphoreType.DMA((NCH,)),
         pltpu.SemaphoreType.DMA((NCH,)),
         pltpu.SemaphoreType.DMA((NCH,)),
@@ -275,21 +291,18 @@
 
 
 def out_weights(w_ref, wbuf, wsem, core):
-    per = CW // HD
-
-    def copy(c):
-        cols = pl.ds(pl.multiple_of(c * HD, HD), HD)
-        return pltpu.make_async_copy(w_ref.at[:, cols], wbuf.at[c], wsem.at[c])
+    def copy(half, j):
+        at = half * NCH + j
+        cols = pl.ds(pl.multiple_of(at * CW, CW), CW)
+        return pltpu.make_async_copy(w_ref.at[:, cols], wbuf.at[at], wsem.at[at])
 
     def start():
         for j in range(NCH):
-            for half in (1 - core, core):
-                for p in range(per):
-                    copy(half * (NC // 2) + j * per + p).start()
+            copy(1 - core, j).start()
+            copy(core, j).start()
 
     def wait(half, j):
-        for p in range(per):
-            copy(half * (NC // 2) + j * per + p).wait()
+        copy(half, j).wait()
 
     return start, wait
 
@@ -303,8 +316,8 @@
 def mid_kernel(og_ref, ss_ref, h1_ref, g2_ref, alpha_ref, beta_ref, len_ref, wout_ref, wattn_ref,
                k_ref, v_ref, q_ref, kn_ref, vn_ref, h2_ref, kbuf, vbuf,
                wbuf, a_send, a_recv, b_send, b_recv, total, wsem, sa, ra, sb, rb, sc, rc,
-               wraw, wide, w2, ss_recv, wasem, ss_s, ss_r, csem):
-    core, mate, across, diag = peers()
+               wraw, wide, w2, ss_recv, ss_chip, wasem, ss_s, ss_r, csem):
+    core, mate, across = peers()
     start_w, wait_w = out_weights(wout_ref, wbuf, wsem, core)
     start_w()
 
@@ -319,17 +332,29 @@
     caches = [pltpu.make_async_copy(k_ref, kbuf, csem.at[0]), pltpu.make_async_copy(v_ref, vbuf, csem.at[1])]
     for cp in caches:
         cp.start()
-    entry_barrier((mate, across, diag))
-    ss_copies = []
-    for n, dev in enumerate((mate, across, diag)):
-        cp = rcopy(ss_ref, ss_recv.at[n], ss_s.at[n], ss_r.at[n], dev)
-        cp.start()
-        ss_copies.append(cp)
-    for cp in ss_copies:
-        cp.wait_recv()
-    ssum = (ss_ref[...] + ss_recv[0]) + (ss_recv[1] + ss_recv[2])
-    inv = lax.rsqrt(ssum[:, 0:1] / D + EPS)
-    left = (og_ref[...] * inv).astype(BF16)
+    say_here((mate, across))
+    ss_mate = rcopy(ss_ref, ss_recv.at[0], ss_s.at[0], ss_r.at[0], mate)
+    ss_across = rcopy(ss_chip, ss_recv.at[1], ss_s.at[1], ss_r.at[1], across)
+
+    def before_sends():
+        await_peers(2)
+        ss_mate.start()
+
+    def root(total_sq, count):
+        return jnp.minimum(jnp.sqrt(total_sq[:, 0:1] / count + EPS), 3e38)
+
+    def pair_scale():
+        ss_mate.wait_recv()
+        both = ss_ref[...] + ss_recv[0]
+        ss_chip[...] = both
+        ss_across.start()
+        inv = lax.rsqrt(both[:, 0:1] / (D // 2) + EPS)
+        return root(ss_ref[...], D // 4) * inv, root(ss_recv[0], D // 4) * inv
+
+    def cross_scale():
+        ss_across.wait_recv()
+        inv = lax.rsqrt((ss_chip[:, 0:1] + ss_recv[1, :, 0:1]) / D + EPS)
+        return root(ss_chip[...], D // 2) * inv, root(ss_recv[1], D // 2) * inv
 
     def relayout():
         def body(i, carry):
@@ -340,10 +365,10 @@
             return carry
         lax.fori_loop(0, WA_CH, body, 0)
 
-    exchange(left, wbuf, wait_w, relayout, core, mate, across, a_send, a_recv, b_send, b_recv, total,
-             (sa, ra, sb, rb, sc, rc))
-    for cp in ss_copies:
-        cp.wait_send()
+    exchange(og_ref[...], wbuf, wait_w, before_sends, pair_scale, relayout, cross_scale, core, mate, across,
+             a_send, a_recv, b_send, b_recv, total, (sa, ra, sb, rb, sc, rc))
+    ss_mate.wait_send()
+    ss_across.wait_send()
 
     per = CW // HD
     alpha = alpha_ref[0]
@@ -406,10 +431,11 @@
             pltpu.VMEM((WA_CH, WA_STEP, HD), BF16),
             pltpu.VMEM((WA_STEP, HD), F32),
             pltpu.VMEM((NJ, D, HD), BF16),
-            pltpu.VMEM((3, B, HD), F32),
+            pltpu.VMEM((2, B, HD), F32),
+            pltpu.VMEM((B, HD), F32),
             pltpu.SemaphoreType.DMA((WA_CH,)),
-            pltpu.SemaphoreType.DMA((3,)),
-            pltpu.SemaphoreType.DMA((3,)),
+            pltpu.SemaphoreType.DMA((2,)),
+            pltpu.SemaphoreType.DMA((2,)),
             pltpu.SemaphoreType.DMA((2,)),
         ],
         compiler_params=pltpu.CompilerParams(vmem_limit_bytes=37 * MIB, collective_id=0, has_side_effects=True),
@@ -429,10 +455,10 @@
     row16 = lax.broadcasted_iota(jnp.int32, (16, HD), 0)
     tpos = lax.broadcasted_iota(jnp.int32, (8, T), 1)
 
-    def body(i, carry):
+    def insert(i, carry):
         rows = [i * ROWS + r for r in range(ROWS)]
-        lens = [len_ref[b] for b in rows]
-        for b, p in zip(rows, lens):
+        for b in rows:
+            p = len_ref[b]
             base = pl.multiple_of((p // 16) * 16, 16)
             hit = row16 == p - base
             for kv in range(KV):
@@ -442,6 +468,13 @@
         for b in rows:
             for cp in outs(b):
                 cp.start()
+        return carry
+
+    lax.fori_loop(0, B // ROWS, insert, 0)
+
+    def body(i, carry):
+        rows = [i * ROWS + r for r in range(ROWS)]
+        lens = [len_ref[b] for b in rows]
         scores = []
         for b, p in zip(rows, lens):
             q = q_ref[pl.ds(b * 8, 8), :]
@@ -484,13 +517,13 @@
 
 def last_kernel(at_ref, h2_ref, alpha_ref, beta_ref, wout_ref, out_ref,
                 wbuf, a_send, a_recv, b_send, b_recv, total, wsem, sa, ra, sb, rb, sc, rc):
-    core, mate, across, diag = peers()
+    core, mate, across = peers()
     start_w, wait_w = out_weights(wout_ref, wbuf, wsem, core)
     start_w()
-    entry_barrier((mate, across))
+    say_here((mate, across))
     left = jnp.concatenate([at_ref[pl.ds(j, B, stride=8), :].astype(BF16) for j in range(8)], axis=1)
-    exchange(left, wbuf, wait_w, lambda: None, core, mate, across, a_send, a_recv, b_send, b_recv, total,
-             (sa, ra, sb, rb, sc, rc))
+    exchange(left, wbuf, wait_w, lambda: await_peers(2), lambda: None, lambda: None, lambda: None, core, mate, across,
+             a_send, a_recv, b_send, b_recv, total, (sa, ra, sb, rb, sc, rc))
     per = CW // HD
     alpha = alpha_ref[1]
     beta = beta_ref[1]
@@ -528,7 +561,7 @@
         g1 = norm_first.reshape(NC, HD)
         g2 = norm_second.reshape(NC, HD)
         wa = jnp.transpose(w_attn, (0, 2, 1, 3)).reshape(WA_ROWS, HD)
-        state_out, og, ss, h1 = lightning(hidden, g1, slopes, out_norm, hbm(lin_state), hbm(w_qkv), hbm(w_gate))
+        state_out, og, ss, h1 = lightning(hbm(hidden), hbm(g1), hbm(slopes), hbm(out_norm), hbm(lin_state), hbm(w_qkv), hbm(w_gate))
         q, kn, vn, h2, kbuf, vbuf = middle(og, ss, h1, g2, mix_alpha, mix_beta, cache_len,
                                            hbm(w_out_lin.reshape(HL * HD, D)), hbm(wa), hbm(k_cache), hbm(v_cache))
         at, k_out, v_out = attention(cache_len, q, kn, vn, kbuf, vbuf)

time: 72 us -> 66.2 us (0.919)
  local copies, waits for them, and re-layouts: 3.72 us -> 0.72 us
  Pallas kernels: 67.3 us -> 64.6 us
    unnamed x17 -> x9, local copies, waits for them, and re-layouts: 3.72 us -> 0.72 us
    pallas_call x1, Pallas kernels: 20.4 us -> 17.5 us  [middle(): pl.pallas_call(mid_kernel, out_shape=[jax.ShapeDtypeStruct((B * 8, HD), F...]
    pallas_call x1, Pallas kernels: 26.8 us -> 27.7 us  [lightning(): pl.pallas_call(lightning_kernel, out_shape=[jax.ShapeDtypeStruct((B, HL,...]
where the time goes in v3:
time: 66.2 us; the launch traced here: 66 us
  Pallas kernels  64.6 us (98%)
  between operations  0.73 us (1%)
  local copies, waits for them, and re-layouts  0.72 us (1%)
    pallas_call x1, Pallas kernels, lightning(): pl.pallas_call(lightning_kernel, out_shape=[jax.ShapeDtypeStruct((B, HL,...  27.7 us
    pallas_call x1, Pallas kernels, middle(): pl.pallas_call(mid_kernel, out_shape=[jax.ShapeDtypeStruct((B * 8, HD), F...  17.5 us
    pallas_call x1, Pallas kernels, last(): pl.pallas_call(last_kernel, out_shape=jax.ShapeDtypeStruct((B, D), BF16),...  11.9 us
    pallas_call x1, Pallas kernels, attention(): pl.pallas_call(attention_kernel, out_shape=[jax.ShapeDtypeStruct((B * 8,...  7.47 us

profile of v3, /device:TPU:0, one launch (start us, length us, event | category | flops | bytes accessed | tf_op | source)
XLA Modules:
  0.0 66.0 jit_solution(2709556483550867485)
XLA Ops:
  0.6 0.0 copy-start
  0.6 0.0 copy-start.1
  0.7 0.0 copy-start.2
  0.7 0.0 copy-start.3
  0.7 27.7 %lightning.1 = (f32[32,8,128,128]{3,2,1,0:T(8,128)}, bf16[32,1024]{1,0:T(8,128)(2,1)S(1)}, f32[32,128]{1,0:T(8,128)S(1)}, bf16[32,4096]{1,0:T(8,128)(2,1)S(1)}) custom-call(bf16[32,4096]{1,0:T(8,128)(2,1)} %hid_hbm.1, f32[32,128]{1,0:T(8,128)} %bitcast.11, f32[8]{0:T(128)} %slopes_hbm.1, f32[8,128]{1,0:T(8,128)} %onorm_hbm.1, f32[32,8,128,128]{3,2,1,0:T(8,128)} %state_ref.1, ...), custom_call_target="tpu_custom_call" | custom-call | tf_op jit(solution)/shard_map/lightning/pallas_call | solution.py:173
  28.4 0.0 copy-done
  28.4 0.0 copy-done.1
  28.4 0.0 copy-done.2
  28.4 0.0 copy-done.3
  28.4 17.5 %middle.1 = (f32[256,128]{1,0:T(8,128)S(1)}, f32[2,32,128]{2,1,0:T(8,128)S(1)}, f32[2,32,128]{2,1,0:T(8,128)S(1)}, bf16[32,4096]{1,0:T(8,128)(2,1)S(1)}, bf16[32...) custom-call(bf16[32,1024]{1,0:T(8,128)(2,1)S(1)} %get-tuple-element.17.og_ref, ...), custom_call_target="tpu_custom_call" | custom-call | tf_op jit(solution)/shard_map/middle/pallas_call | solution.py:422
  45.9 7.5 %attention.1 = (f32[256,128]{1,0:T(8,128)S(1)}, bf16[32,2,512,128]{3,2,1,0:T(8,128)(2,1)}, bf16[32,2,512,128]{3,2,1,0:T(8,128)(2,1)}, bf16[32,2,512,128]{3,2,1,0:T(8,128)(2,1)S(1)}, bf16[32,2,512,128]{3,2,1,0:T(8,128)(2,1)S(1)}) custom-call(s32[32]{0:T(128)S(1)} %copy-done.1, ...), custom_call_target="tpu_custom_call", output_to_operand_aliasing={{3}: (4, {}), {4}: (5, {})} | custom-call | tf_op jit(solution)/shard_map/attention/pallas_call | solution.py:505
  53.4 11.9 %last.1 = bf16[32,4096]{1,0:T(8,128)(2,1)S(1)} custom-call(f32[256,128]{1,0:T(8,128)S(1)} %get-tuple-element.25.at_ref, bf16[32,4096]{1,0:T(8,128)(2,1)S(1)} %get-tuple-element.26.h2_ref, f32[2]{0:T(128)S(1)} %copy-done.2, f32[2]{0:T(128)S(1)} %copy-done.3, bf16[1024,4096]{1,0:T(8,128)(2,1)} %bitcast.10), custom_call_target="tpu_custom_call" | custom-call | tf_op jit(solution)/shard_map/last/pallas_call | solution.py:537
  65.3 0.7 %copy.25 = bf16[32,4096]{1,0:T(8,128)(2,1)} copy(bf16[32,4096]{1,0:T(8,128)(2,1)S(1)} %last.1) | data formatting | bytes 524288
Async XLA Ops:
  0.6 27.8 %copy-start = (f32[4096]{0:T(1024)S(1)}, f32[4096]{0:T(1024)}, u32[]{:S(2)}) copy-start(f32[4096]{0:T(1024)} %param.27) | copy-start | bytes 49156
  0.6 27.8 %copy-start.1 = (s32[32]{0:T(128)S(1)}, s32[32]{0:T(128)}, u32[]{:S(2)}) copy-start(s32[32]{0:T(128)} %len_ref.3) | copy-start | bytes 388
  0.7 27.8 %copy-start.2 = (f32[2]{0:T(128)S(1)}, f32[2]{0:T(128)}, u32[]{:S(2)}) copy-start(f32[2]{0:T(128)} %alpha_ref.3) | copy-start | bytes 28
  0.7 27.8 %copy-start.3 = (f32[2]{0:T(128)S(1)}, f32[2]{0:T(128)}, u32[]{:S(2)}) copy-start(f32[2]{0:T(128)} %beta_ref.3) | copy-start | bytes 28

commit v4 on v3

--- a/solution.py
+++ b/solution.py
@@ -27,7 +27,7 @@
 DCH = 256
 STEPS = D // DCH
 RING = 4
-EARLY = 24
+EARLY = 12
 
 
 def any_spec():
@@ -48,7 +48,7 @@
 
 def lightning_kernel(hid_hbm, g1_hbm, slopes_hbm, onorm_hbm, state_ref, wqkv_ref, wgate_ref,
                      sout_ref, og_ref, ss_ref, h1_ref, hid_ref, g1_ref, onorm_ref, slopes_ref,
-                     wbuf, gbuf, sbuf, hstack, ebuf, lbuf, acc, qk_t, v_s, o_s, psem, wsem, ssem, osem):
+                     wbuf, gbuf, sbuf, hstack, ebuf, lbuf_a, lbuf_b, acc, kq_t, v_s, o_s, psem, wsem, ssem, osem):
     def w_copies(step, slot):
         rows = pl.ds(step * DCH, DCH)
         return (pltpu.make_async_copy(wqkv_ref.at[rows], wbuf.at[slot], wsem.at[slot, 0]),
@@ -92,26 +92,41 @@
                 ebuf[cc // (DCH // HD), :, off:off + 256] = e[k * B:(k + 1) * B, :]
 
     acc[...] = jnp.zeros_like(acc)
-    lane = lax.broadcasted_iota(jnp.int32, (B, DCH * HL), 1) % 8
+    half = DCH * HL // 2
+    lane = lax.broadcasted_iota(jnp.int32, (B, half), 1) % 8
+
+    def spread_heads(dst, i, part):
+        e = ebuf[i, :, part * half:(part + 1) * half]
+        for h in range(HL):
+            keep = jnp.where(lane == h, 1.0, 0.0).astype(BF16)
+            dst[h * B:(h + 1) * B, :] = e * keep
+
+    spread_heads(lbuf_a, 0, 0)
 
     def step_fn(i, carry):
         slot = lax.rem(i, RING)
+
         @pl.when(i >= STEPS - EARLY // 2)
         def _():
             for k in range(2):
                 s_copy((i - (STEPS - EARLY // 2)) * 2 + k).start()
 
-        e = ebuf[i]
-        for h in range(HL):
-            keep = jnp.where(lane == h, 1.0, 0.0).astype(BF16)
-            lbuf[h * B:(h + 1) * B, :] = e * keep
         for cp in w_copies(i, slot):
             cp.wait()
-        left = lbuf[...]
+
+        def product(left, part, pair):
+            rows = slice(part * DCH // 2, (part + 1) * DCH // 2)
+            second = wbuf[slot, rows, 1] if pair == 0 else gbuf[slot, rows]
+            right = jnp.concatenate([wbuf[slot, rows, 2 * pair].reshape(half, HD), second.reshape(half, HD)], axis=1)
+            return dot(left, right)
+
+        spread_heads(lbuf_b, i, 1)
+        left_a = lbuf_a[...]
+        first = [product(left_a, 0, pair) for pair in range(2)]
+        spread_heads(lbuf_a, jnp.minimum(i + 1, STEPS - 1), 0)
+        left_b = lbuf_b[...]
         for pair in range(2):
-            second = wbuf[slot, :, 1] if pair == 0 else gbuf[slot]
-            right = jnp.concatenate([wbuf[slot, :, 2 * pair].reshape(DCH * HL, HD), second.reshape(DCH * HL, HD)], axis=1)
-            acc[pair] += dot(left, right)
+            acc[pair] += first[pair] + product(left_b, 1, pair)
 
         @pl.when(i + RING < STEPS)
         def _():
@@ -129,27 +144,31 @@
         k = jax.nn.silu(acc[0, rows, HD:2 * HD]).astype(BF16)
         v = jax.nn.silu(acc[1, rows, 0:HD]).astype(BF16)
         qk = jnp.concatenate([k, q], axis=0).astype(F32)
-        qk_t[h] = jnp.transpose(qk).astype(BF16)
-        v_s[h] = v
-
-    def row_fn(b, carry):
-        s_copy(b).wait()
-        row_i = lax.broadcasted_iota(jnp.int32, (B, HD), 0)
-        hit = row_i == b
-        ones = jnp.where(hit, 1.0, 0.0).astype(BF16)
-        zero = jnp.zeros((B, HD), BF16)
+        both = jnp.transpose(qk).astype(BF16)
+        kq_t[h] = jnp.concatenate([both[:, 0:B], both[:, B:]], axis=0)
+        v_s[h] = v.astype(F32)
+
+    brow = lax.broadcasted_iota(jnp.int32, (B, 2 * HD), 0)
+    bcol = lax.broadcasted_iota(jnp.int32, (B, 2 * HD), 1) // HD
+
+    def row_fn(i, carry):
+        for r in range(2):
+            s_copy(2 * i + r).wait()
+        pick = jnp.where(brow == 2 * i + bcol, 1.0, 0.0).astype(BF16)
         for h in range(HL):
-            top = jnp.concatenate([v_s[h] * ones, zero], axis=1)
-            bot = jnp.concatenate([zero, ones], axis=1)
-            prod = dot(qk_t[h], jnp.concatenate([top, bot], axis=0))
+            kq = dot(kq_t[h], pick)
             decay = jnp.exp(jnp.full((1, HD), -slopes_ref[h], F32))
-            new = decay * sbuf[b, h] + prod[:, 0:HD]
-            sbuf[b, h] = new
-            o_s[b, h:h + 1, :] = jnp.sum(prod[:, HD:] * new, axis=0, keepdims=True)
-        o_copy(b).start()
-        return carry
-
-    lax.fori_loop(0, B, row_fn, 0)
+            for r in range(2):
+                b = 2 * i + r
+                lanes = slice(r * HD, (r + 1) * HD)
+                new = decay * sbuf[b, h] + kq[0:HD, lanes] * v_s[h, pl.ds(b, 1), :]
+                sbuf[b, h] = new
+                o_s[b, h:h + 1, :] = jnp.sum(kq[HD:, lanes] * new, axis=0, keepdims=True)
+        for r in range(2):
+            o_copy(2 * i + r).start()
+        return carry
+
+    lax.fori_loop(0, B // 2, row_fn, 0)
 
     ss = jnp.zeros((B, HD), F32)
     for h in range(HL):
@@ -186,10 +205,11 @@
             pltpu.VMEM((B, HL, HD, HD), F32),
             pltpu.VMEM((NC * B, HD), BF16),
             pltpu.VMEM((STEPS, B, DCH * HL), BF16),
-            pltpu.VMEM((HL * B, DCH * HL), BF16),
+            pltpu.VMEM((HL * B, DCH * HL // 2), BF16),
+            pltpu.VMEM((HL * B, DCH * HL // 2), BF16),
             pltpu.VMEM((2, HL * B, 2 * HD), F32),
-            pltpu.VMEM((HL, HD, 2 * B), BF16),
-            pltpu.VMEM((HL, B, HD), BF16),
+            pltpu.VMEM((HL, 2 * HD, B), BF16),
+            pltpu.VMEM((HL, B, HD), F32),
             pltpu.VMEM((B, HL, HD), F32),
             pltpu.SemaphoreType.DMA((4,)),
             pltpu.SemaphoreType.DMA((RING, 2)),
@@ -231,13 +251,13 @@
 
 
 def exchange(left, wbuf, wwait, before_sends, pair_scale, mid_work, cross_scale, core, mate, across,
-             a_send, a_recv, b_send, b_recv, total, sems):
+             a_send, a_recv, b_send, b_recv, total, sems, first=None):
     sa, ra, sb, rb, sc, rc = sems
 
     def product(half, j):
         wwait(half, j)
-        at = half * NCH + j
-        return jnp.concatenate([dot(left, wbuf[at, :, c:c + 2 * HD]) for c in range(0, CW, 2 * HD)], axis=1)
+        buf, at = (wbuf, half * NCH + j) if first is None or j > 0 else (first, half)
+        return jnp.concatenate([dot(left, buf[at, :, c:c + 2 * HD]) for c in range(0, CW, 2 * HD)], axis=1)
 
     a_copies = [rcopy(a_send.at[j], a_recv.at[j], sa.at[j], ra.at[j], mate) for j in range(NCH)]
     b_copies = [rcopy(b_send.at[j], b_recv.at[j], sb.at[j], rb.at[j], across) for j in range(NCH)]
@@ -290,19 +310,20 @@
     ]
 
 
-def out_weights(w_ref, wbuf, wsem, core):
+def out_weights(w_ref, wbuf, wsem, core, begin=0):
     def copy(half, j):
         at = half * NCH + j
         cols = pl.ds(pl.multiple_of(at * CW, CW), CW)
         return pltpu.make_async_copy(w_ref.at[:, cols], wbuf.at[at], wsem.at[at])
 
     def start():
-        for j in range(NCH):
+        for j in range(begin, NCH):
             copy(1 - core, j).start()
             copy(core, j).start()
 
     def wait(half, j):
-        copy(half, j).wait()
+        if j >= begin:
+            copy(half, j).wait()
 
     return start, wait
 
@@ -314,10 +335,11 @@
 
 
 def mid_kernel(og_ref, ss_ref, h1_ref, g2_ref, alpha_ref, beta_ref, len_ref, wout_ref, wattn_ref,
-               k_ref, v_ref, q_ref, kn_ref, vn_ref, h2_ref, kbuf, vbuf,
+               k_ref, v_ref, wnext_ref, q_ref, kn_ref, vn_ref, h2_ref, kbuf, vbuf, wnext,
                wbuf, a_send, a_recv, b_send, b_recv, total, wsem, sa, ra, sb, rb, sc, rc,
                wraw, wide, w2, ss_recv, ss_chip, wasem, ss_s, ss_r, csem):
     core, mate, across = peers()
+    say_here((mate, across))
     start_w, wait_w = out_weights(wout_ref, wbuf, wsem, core)
     start_w()
 
@@ -330,9 +352,9 @@
 
     lax.fori_loop(0, WA_CH, wa_start, 0)
     caches = [pltpu.make_async_copy(k_ref, kbuf, csem.at[0]), pltpu.make_async_copy(v_ref, vbuf, csem.at[1])]
+    caches += [pltpu.make_async_copy(wnext_ref.at[:, pl.ds(h * (D // 2), CW)], wnext.at[h], csem.at[2 + h]) for h in range(2)]
     for cp in caches:
         cp.start()
-    say_here((mate, across))
     ss_mate = rcopy(ss_ref, ss_recv.at[0], ss_s.at[0], ss_r.at[0], mate)
     ss_across = rcopy(ss_chip, ss_recv.at[1], ss_s.at[1], ss_r.at[1], across)
 
@@ -418,15 +440,16 @@
         cp.wait()
 
 
-def middle(og, ss, h1, g2, alpha, beta, cache_len, w_out, w_attn, k_cache, v_cache):
+def middle(og, ss, h1, g2, alpha, beta, cache_len, w_out, w_attn, k_cache, v_cache, w_next):
     return pl.pallas_call(
         mid_kernel,
         out_shape=[jax.ShapeDtypeStruct((B * 8, HD), F32), jax.ShapeDtypeStruct((KV, B, HD), F32),
                    jax.ShapeDtypeStruct((KV, B, HD), F32), jax.ShapeDtypeStruct((B, D), BF16),
-                   pltpu.VMEM((B, KV, T, HD), BF16), pltpu.VMEM((B, KV, T, HD), BF16)],
+                   pltpu.VMEM((B, KV, T, HD), BF16), pltpu.VMEM((B, KV, T, HD), BF16),
+                   pltpu.VMEM((2, HL * HD, CW), BF16)],
         in_specs=[vmem_spec(), vmem_spec(), vmem_spec(), vmem_spec(), smem_spec(), smem_spec(), smem_spec(),
-                  any_spec(), any_spec(), any_spec(), any_spec()],
-        out_specs=[vmem_spec()] * 6,
+                  any_spec(), any_spec(), any_spec(), any_spec(), any_spec()],
+        out_specs=[vmem_spec()] * 7,
         scratch_shapes=exchange_scratch() + [
             pltpu.VMEM((WA_CH, WA_STEP, HD), BF16),
             pltpu.VMEM((WA_STEP, HD), F32),
@@ -436,11 +459,11 @@
             pltpu.SemaphoreType.DMA((WA_CH,)),
             pltpu.SemaphoreType.DMA((2,)),
             pltpu.SemaphoreType.DMA((2,)),
-            pltpu.SemaphoreType.DMA((2,)),
+            pltpu.SemaphoreType.DMA((4,)),
         ],
         compiler_params=pltpu.CompilerParams(vmem_limit_bytes=37 * MIB, collective_id=0, has_side_effects=True),
         name="middle",
-    )(og, ss, h1, g2, alpha, beta, cache_len, w_out, w_attn, k_cache, v_cache)
+    )(og, ss, h1, g2, alpha, beta, cache_len, w_out, w_attn, k_cache, v_cache, w_next)
 
 
 ROWS = 4
@@ -515,15 +538,15 @@
     )(cache_len, q, kn, vn, kbuf, vbuf)[:3]
 
 
-def last_kernel(at_ref, h2_ref, alpha_ref, beta_ref, wout_ref, out_ref,
+def last_kernel(at_ref, h2_ref, alpha_ref, beta_ref, wout_ref, first_ref, out_ref,
                 wbuf, a_send, a_recv, b_send, b_recv, total, wsem, sa, ra, sb, rb, sc, rc):
     core, mate, across = peers()
-    start_w, wait_w = out_weights(wout_ref, wbuf, wsem, core)
+    say_here((mate, across))
+    start_w, wait_w = out_weights(wout_ref, wbuf, wsem, core, begin=1)
     start_w()
-    say_here((mate, across))
     left = jnp.concatenate([at_ref[pl.ds(j, B, stride=8), :].astype(BF16) for j in range(8)], axis=1)
     exchange(left, wbuf, wait_w, lambda: await_peers(2), lambda: None, lambda: None, lambda: None, core, mate, across,
-             a_send, a_recv, b_send, b_recv, total, (sa, ra, sb, rb, sc, rc))
+             a_send, a_recv, b_send, b_recv, total, (sa, ra, sb, rb, sc, rc), first=first_ref)
     per = CW // HD
     alpha = alpha_ref[1]
     beta = beta_ref[1]
@@ -533,16 +556,16 @@
         out_ref[:, cols] = (alpha * h2_ref[:, cols].astype(F32) + beta * a2).astype(BF16)
 
 
-def last(at, h2, alpha, beta, w_out):
+def last(at, h2, alpha, beta, w_out, w_first):
     return pl.pallas_call(
         last_kernel,
         out_shape=jax.ShapeDtypeStruct((B, D), BF16),
-        in_specs=[vmem_spec(), vmem_spec(), smem_spec(), smem_spec(), any_spec()],
+        in_specs=[vmem_spec(), vmem_spec(), smem_spec(), smem_spec(), any_spec(), vmem_spec()],
         out_specs=vmem_spec(),
         scratch_shapes=exchange_scratch(),
         compiler_params=pltpu.CompilerParams(vmem_limit_bytes=16 * MIB, collective_id=1, has_side_effects=True),
         name="last",
-    )(at, h2, alpha, beta, w_out)
+    )(at, h2, alpha, beta, w_out, w_first)
 
 
 def solution(mesh):
@@ -562,10 +585,12 @@
         g2 = norm_second.reshape(NC, HD)
         wa = jnp.transpose(w_attn, (0, 2, 1, 3)).reshape(WA_ROWS, HD)
         state_out, og, ss, h1 = lightning(hbm(hidden), hbm(g1), hbm(slopes), hbm(out_norm), hbm(lin_state), hbm(w_qkv), hbm(w_gate))
-        q, kn, vn, h2, kbuf, vbuf = middle(og, ss, h1, g2, mix_alpha, mix_beta, cache_len,
-                                           hbm(w_out_lin.reshape(HL * HD, D)), hbm(wa), hbm(k_cache), hbm(v_cache))
+        w_last = hbm(w_out_attn.reshape(HL * HD, D))
+        q, kn, vn, h2, kbuf, vbuf, w_first = middle(og, ss, h1, g2, mix_alpha, mix_beta, cache_len,
+                                                    hbm(w_out_lin.reshape(HL * HD, D)), hbm(wa), hbm(k_cache),
+                                                    hbm(v_cache), w_last)
         at, k_out, v_out = attention(cache_len, q, kn, vn, kbuf, vbuf)
-        hidden_out = last(at, h2, mix_alpha, mix_beta, hbm(w_out_attn.reshape(HL * HD, D)))
+        hidden_out = last(at, h2, mix_alpha, mix_beta, w_last, w_first)
         return hidden_out, state_out, k_out, v_out
 
     return jax.shard_map(local_step, mesh=mesh, in_specs=in_specs, out_specs=out_specs, check_vma=False)

time: 66.2 us -> 69.5 us (1.050)
  local copies, waits for them, and re-layouts: 0.72 us -> 5.06 us
  Pallas kernels: 64.6 us -> 63.4 us
    unnamed x9 -> x21, local copies, waits for them, and re-layouts: 0.72 us -> 5.06 us
    pallas_call x1, Pallas kernels: 27.7 us -> 25.6 us  [lightning(): pl.pallas_call(lightning_kernel, out_shape=[jax.ShapeDtypeStruct((B, HL,...]
    pallas_call x1, Pallas kernels: 17.5 us -> 18.7 us  [middle(): pl.pallas_call(mid_kernel, out_shape=[jax.ShapeDtypeStruct((B * 8, HD), F...]
where the time goes in v4:
time: 69.5 us; the launch traced here: 69.2 us
  Pallas kernels  63.4 us (91%)
  local copies, waits for them, and re-layouts  5.06 us (7%)
  between operations  0.72 us (1%)
    pallas_call x1, Pallas kernels, lightning(): pl.pallas_call(lightning_kernel, out_shape=[jax.ShapeDtypeStruct((B, HL,...  25.6 us
    pallas_call x1, Pallas kernels, middle(): pl.pallas_call(mid_kernel, out_shape=[jax.ShapeDtypeStruct((B * 8, HD), F...  18.7 us
    pallas_call x1, Pallas kernels, last(): pl.pallas_call(last_kernel, out_shape=jax.ShapeDtypeStruct((B, D), BF16),...  11.6 us
    pallas_call x1, Pallas kernels, attention(): pl.pallas_call(attention_kernel, out_shape=[jax.ShapeDtypeStruct((B * 8,...  7.47 us
    unnamed x21, local copies, waits for them, and re-layouts  5.06 us

profile of v4, /device:TPU:0, one launch (start us, length us, event | category | flops | bytes accessed | tf_op | source)
XLA Modules:
  0.0 69.2 jit_solution(10948769234321233458)
XLA Ops:
  0.6 25.6 %lightning.1 = (f32[32,8,128,128]{3,2,1,0:T(8,128)}, bf16[32,1024]{1,0:T(8,128)(2,1)S(1)}, f32[32,128]{1,0:T(8,128)S(1)}, bf16[32,4096]{1,0:T(8,128)(2,1)S(1)}) custom-call(bf16[32,4096]{1,0:T(8,128)(2,1)} %hid_hbm.1, f32[32,128]{1,0:T(8,128)} %bitcast.11, f32[8]{0:T(128)} %slopes_hbm.1, f32[8,128]{1,0:T(8,128)} %onorm_hbm.1, f32[32,8,128,128]{3,2,1,0:T(8,128)} %state_ref.1, ...), custom_call_target="tpu_custom_call" | custom-call | tf_op jit(solution)/shard_map/lightning/pallas_call | solution.py:192
  26.3 0.0 copy-start
  26.3 0.7 %copy-done = bf16[32,4096]{1,0:T(8,128)(2,1)} copy-done((bf16[32,4096]{1,0:T(8,128)(2,1)}, bf16[32,4096]{1,0:T(8,128)(2,1)S(1)}, u32[]{:S(2)}) %copy-start) | copy-done | bytes 262168
  27.0 0.0 copy-start.3
  27.0 0.6 copy-done.3
  27.6 0.0 copy-start.6
  27.6 0.6 copy-done.6
  28.2 0.0 copy-start.7
  28.2 18.7 %middle.1 = (f32[256,128]{1,0:T(8,128)}, f32[2,32,128]{2,1,0:T(8,128)}, f32[2,32,128]{2,1,0:T(8,128)}, bf16[32,4096]{1,0:T(8,128)(2,1)}, bf16[32,2,512,128]{3,2,...) custom-call(bf16[32,1024]{1,0:T(8,128)(2,1)} %copy-done.3, ...), custom_call_target="tpu_custom_call" | custom-call | tf_op jit(solution)/shard_map/middle/pallas_call | solution.py:444
  46.9 0.0 copy-done.7
  46.9 0.0 copy-start.2
  46.9 0.9 %copy-done.2 = f32[256,128]{1,0:T(8,128)S(1)} copy-done((f32[256,128]{1,0:T(8,128)S(1)}, f32[256,128]{1,0:T(8,128)}, u32[]{:S(2)}) %copy-start.2) | copy-done | bytes 131096
  47.8 0.0 copy-start.4
  47.8 0.8 %copy-done.4 = f32[2,32,128]{2,1,0:T(8,128)S(1)} copy-done((f32[2,32,128]{2,1,0:T(8,128)S(1)}, f32[2,32,128]{2,1,0:T(8,128)}, u32[]{:S(2)}) %copy-start.4) | copy-done | bytes 32792
  48.6 0.0 copy-start.5
  48.6 0.8 %copy-done.5 = f32[2,32,128]{2,1,0:T(8,128)S(1)} copy-done((f32[2,32,128]{2,1,0:T(8,128)S(1)}, f32[2,32,128]{2,1,0:T(8,128)}, u32[]{:S(2)}) %copy-start.5) | copy-done | bytes 32792
  49.4 0.0 copy-start.1
  49.4 0.0 copy-start.8
  49.4 0.0 copy-start.9
  49.4 7.5 %attention.1 = (f32[256,128]{1,0:T(8,128)S(1)}, bf16[32,2,512,128]{3,2,1,0:T(8,128)(2,1)}, bf16[32,2,512,128]{3,2,1,0:T(8,128)(2,1)}, bf16[32,2,512,128]{3,2,1,0:T(8,128)(2,1)S(1)}, bf16[32,2,512,128]{3,2,1,0:T(8,128)(2,1)S(1)}) custom-call(s32[32]{0:T(128)S(1)} %copy-done.7, ...), custom_call_target="tpu_custom_call", output_to_operand_aliasing={{3}: (4, {}), {4}: (5, {})} | custom-call | tf_op jit(solution)/shard_map/attention/pallas_call | solution.py:528
  56.8 0.0 copy-done.1
  56.8 0.0 copy-done.8
  56.9 0.0 copy-done.9
  56.9 11.6 %last.1 = bf16[32,4096]{1,0:T(8,128)(2,1)S(1)} custom-call(f32[256,128]{1,0:T(8,128)S(1)} %get-tuple-element.26.at_ref, bf16[32,4096]{1,0:T(8,128)(2,1)S(1)} %copy-done.1, f32[2]{0:T(128)S(1)} %copy-done.8, f32[2]{0:T(128)S(1)} %copy-done.9, bf16[1024,4096]{1,0:T(8,128)(2,1)} %bitcast.8, bf16[2,1024,512]{2,1,0:T(8,128)(2,1)S(1)} %get-tuple-element.28.first_ref), custom_call_target="tpu_custom_call" | custom-call | tf_op jit(solution)/shard_map/last/pallas_call | solution.py:560
  68.5 0.7 %copy.25 = bf16[32,4096]{1,0:T(8,128)(2,1)} copy(bf16[32,4096]{1,0:T(8,128)(2,1)S(1)} %last.1) | data formatting | bytes 524288
Async XLA Ops:
  26.3 0.7 %copy-start = (bf16[32,4096]{1,0:T(8,128)(2,1)}, bf16[32,4096]{1,0:T(8,128)(2,1)S(1)}, u32[]{:S(2)}) copy-start(bf16[32,4096]{1,0:T(8,128)(2,1)S(1)} %get-tuple-element.20.h1_ref) | copy-start | bytes 786436
  27.0 0.6 copy-start.3
  27.6 0.6 copy-start.6
  28.2 18.7 %copy-start.7 = (s32[32]{0:T(128)S(1)}, s32[32]{0:T(128)}, u32[]{:S(2)}) copy-start(s32[32]{0:T(128)} %len_ref.3) | copy-start | bytes 388
  46.9 0.9 %copy-start.2 = (f32[256,128]{1,0:T(8,128)S(1)}, f32[256,128]{1,0:T(8,128)}, u32[]{:S(2)}) copy-start(f32[256,128]{1,0:T(8,128)} %get-tuple-element.21.q_ref) | copy-start | bytes 393220
  47.8 0.8 %copy-start.4 = (f32[2,32,128]{2,1,0:T(8,128)S(1)}, f32[2,32,128]{2,1,0:T(8,128)}, u32[]{:S(2)}) copy-start(f32[2,32,128]{2,1,0:T(8,128)} %get-tuple-element.22.kn_ref) | copy-start | bytes 98308
  48.6 0.8 %copy-start.5 = (f32[2,32,128]{2,1,0:T(8,128)S(1)}, f32[2,32,128]{2,1,0:T(8,128)}, u32[]{:S(2)}) copy-start(f32[2,32,128]{2,1,0:T(8,128)} %get-tuple-element.23.vn_ref) | copy-start | bytes 98308
  49.4 7.5 %copy-start.1 = (bf16[32,4096]{1,0:T(8,128)(2,1)S(1)}, bf16[32,4096]{1,0:T(8,128)(2,1)}, u32[]{:S(2)}) copy-start(bf16[32,4096]{1,0:T(8,128)(2,1)} %get-tuple-element.27.h2_ref) | copy-start | bytes 786436
  49.4 7.5 %copy-start.8 = (f32[2]{0:T(128)S(1)}, f32[2]{0:T(128)}, u32[]{:S(2)}) copy-start(f32[2]{0:T(128)} %alpha_ref.3) | copy-start | bytes 28
  49.4 7.5 %copy-start.9 = (f32[2]{0:T(128)S(1)}, f32[2]{0:T(128)}, u32[]{:S(2)}) copy-start(f32[2]{0:T(128)} %beta_ref.3) | copy-start | bytes 28

commit v5 on v4

--- a/solution.py
+++ b/solution.py
@@ -27,7 +27,7 @@
 DCH = 256
 STEPS = D // DCH
 RING = 4
-EARLY = 12
+EARLY = 16
 
 
 def any_spec():
@@ -106,10 +106,10 @@
     def step_fn(i, carry):
         slot = lax.rem(i, RING)
 
-        @pl.when(i >= STEPS - EARLY // 2)
+        @pl.when(i >= STEPS - RING)
         def _():
-            for k in range(2):
-                s_copy((i - (STEPS - EARLY // 2)) * 2 + k).start()
+            for k in range(EARLY // RING):
+                s_copy((i - (STEPS - RING)) * (EARLY // RING) + k).start()
 
         for cp in w_copies(i, slot):
             cp.wait()
@@ -461,7 +461,7 @@
             pltpu.SemaphoreType.DMA((2,)),
             pltpu.SemaphoreType.DMA((4,)),
         ],
-        compiler_params=pltpu.CompilerParams(vmem_limit_bytes=37 * MIB, collective_id=0, has_side_effects=True),
+        compiler_params=pltpu.CompilerParams(vmem_limit_bytes=35 * MIB, collective_id=0, has_side_effects=True),
         name="middle",
     )(og, ss, h1, g2, alpha, beta, cache_len, w_out, w_attn, k_cache, v_cache, w_next)
 

time: 69.5 us -> 62.8 us (0.904)
  local copies, waits for them, and re-layouts: 5.06 us -> 0.72 us
  Pallas kernels: 63.4 us -> 61.3 us
    unnamed x21 -> x9, local copies, waits for them, and re-layouts: 5.06 us -> 0.72 us
    pallas_call x1, Pallas kernels: 18.7 us -> 17.5 us  [middle(): pl.pallas_call(mid_kernel, out_shape=[jax.ShapeDtypeStruct((B * 8, HD), F...]
    pallas_call x1, Pallas kernels: 25.6 us -> 24.7 us  [lightning(): pl.pallas_call(lightning_kernel, out_shape=[jax.ShapeDtypeStruct((B, HL,...]
where the time goes in v5:
time: 62.8 us; the launch traced here: 62.7 us
  Pallas kernels  61.3 us (98%)
  between operations  0.73 us (1%)
  local copies, waits for them, and re-layouts  0.72 us (1%)
    pallas_call x1, Pallas kernels, lightning(): pl.pallas_call(lightning_kernel, out_shape=[jax.ShapeDtypeStruct((B, HL,...  24.7 us
    pallas_call x1, Pallas kernels, middle(): pl.pallas_call(mid_kernel, out_shape=[jax.ShapeDtypeStruct((B * 8, HD), F...  17.5 us
    pallas_call x1, Pallas kernels, last(): pl.pallas_call(last_kernel, out_shape=jax.ShapeDtypeStruct((B, D), BF16),...  11.6 us
    pallas_call x1, Pallas kernels, attention(): pl.pallas_call(attention_kernel, out_shape=[jax.ShapeDtypeStruct((B * 8,...  7.47 us

profile of v5, /device:TPU:0, one launch (start us, length us, event | category | flops | bytes accessed | tf_op | source)
XLA Modules:
  0.0 62.7 jit_solution(13477224869403879429)
XLA Ops:
  0.6 0.0 copy-start
  0.6 0.0 copy-start.1
  0.7 0.0 copy-start.2
  0.7 0.0 copy-start.3
  0.7 24.7 %lightning.1 = (f32[32,8,128,128]{3,2,1,0:T(8,128)}, bf16[32,1024]{1,0:T(8,128)(2,1)S(1)}, f32[32,128]{1,0:T(8,128)S(1)}, bf16[32,4096]{1,0:T(8,128)(2,1)S(1)}) custom-call(bf16[32,4096]{1,0:T(8,128)(2,1)} %hid_hbm.1, f32[32,128]{1,0:T(8,128)} %bitcast.12, f32[8]{0:T(128)} %slopes_hbm.1, f32[8,128]{1,0:T(8,128)} %onorm_hbm.1, f32[32,8,128,128]{3,2,1,0:T(8,128)} %state_ref.1, ...), custom_call_target="tpu_custom_call" | custom-call | tf_op jit(solution)/shard_map/lightning/pallas_call | solution.py:192
  25.3 0.0 copy-done
  25.4 0.0 copy-done.1
  25.4 0.0 copy-done.2
  25.4 0.0 copy-done.3
  25.4 17.5 %middle.1 = (f32[256,128]{1,0:T(8,128)S(1)}, f32[2,32,128]{2,1,0:T(8,128)S(1)}, f32[2,32,128]{2,1,0:T(8,128)S(1)}, bf16[32,4096]{1,0:T(8,128)(2,1)S(1)}, bf16[32...) custom-call(bf16[32,1024]{1,0:T(8,128)(2,1)S(1)} %get-tuple-element.18.og_re, ...), custom_call_target="tpu_custom_call" | custom-call | tf_op jit(solution)/shard_map/middle/pallas_call | solution.py:444
  42.9 7.5 %attention.1 = (f32[256,128]{1,0:T(8,128)S(1)}, bf16[32,2,512,128]{3,2,1,0:T(8,128)(2,1)}, bf16[32,2,512,128]{3,2,1,0:T(8,128)(2,1)}, bf16[32,2,512,128]{3,2,1,0:T(8,128)(2,1)S(1)}, bf16[32,2,512,128]{3,2,1,0:T(8,128)(2,1)S(1)}) custom-call(s32[32]{0:T(128)S(1)} %copy-done.1, ...), custom_call_target="tpu_custom_call", output_to_operand_aliasing={{3}: (4, {}), {4}: (5, {})} | custom-call | tf_op jit(solution)/shard_map/attention/pallas_call | solution.py:528
  50.4 11.6 %last.1 = bf16[32,4096]{1,0:T(8,128)(2,1)S(1)} custom-call(f32[256,128]{1,0:T(8,128)S(1)} %get-tuple-element.26.at_ref, bf16[32,4096]{1,0:T(8,128)(2,1)S(1)} %get-tuple-element.27.h2_ref, f32[2]{0:T(128)S(1)} %copy-done.2, f32[2]{0:T(128)S(1)} %copy-done.3, bf16[1024,4096]{1,0:T(8,128)(2,1)} %bitcast.9, bf16[2,1024,512]{2,1,0:T(8,128)(2,1)S(1)} %get-tuple-element.28.first_ref), custom_call_target="tpu_custom_call" | custom-call | tf_op jit(solution)/shard_map/last/pallas_call | solution.py:560
  62.0 0.7 %copy.25 = bf16[32,4096]{1,0:T(8,128)(2,1)} copy(bf16[32,4096]{1,0:T(8,128)(2,1)S(1)} %last.1) | data formatting | bytes 524288
Async XLA Ops:
  0.6 24.7 %copy-start = (f32[4096]{0:T(1024)S(1)}, f32[4096]{0:T(1024)}, u32[]{:S(2)}) copy-start(f32[4096]{0:T(1024)} %param.27) | copy-start | bytes 49156
  0.6 24.7 %copy-start.1 = (s32[32]{0:T(128)S(1)}, s32[32]{0:T(128)}, u32[]{:S(2)}) copy-start(s32[32]{0:T(128)} %len_ref.3) | copy-start | bytes 388
  0.7 24.7 %copy-start.2 = (f32[2]{0:T(128)S(1)}, f32[2]{0:T(128)}, u32[]{:S(2)}) copy-start(f32[2]{0:T(128)} %alpha_ref.3) | copy-start | bytes 28
  0.7 24.7 %copy-start.3 = (f32[2]{0:T(128)S(1)}, f32[2]{0:T(128)}, u32[]{:S(2)}) copy-start(f32[2]{0:T(128)} %beta_ref.3) | copy-start | bytes 28

commit v6 on v5

--- a/solution.py
+++ b/solution.py
@@ -24,10 +24,11 @@
 T = 512
 NC = D // HD
 
-DCH = 256
+DCH = 512
 STEPS = D // DCH
-RING = 4
-EARLY = 16
+LCH = DCH * HL // 2 // HD
+RING = 3
+EARLY = 24
 
 
 def any_spec():
@@ -87,21 +88,20 @@
         for c in range(NC // 8):
             e = dot(hstack[c * 256:(c + 1) * 256, :], spread).astype(BF16)
             for k in range(8):
-                cc = c * 8 + k
-                off = (cc % (DCH // HD)) * 1024 + n * 256
-                ebuf[cc // (DCH // HD), :, off:off + 256] = e[k * B:(k + 1) * B, :]
+                for m in range(2):
+                    ebuf[(c * 8 + k) * 8 + n * 2 + m] = e[k * B:(k + 1) * B, m * HD:(m + 1) * HD]
 
     acc[...] = jnp.zeros_like(acc)
     half = DCH * HL // 2
-    lane = lax.broadcasted_iota(jnp.int32, (B, half), 1) % 8
-
-    def spread_heads(dst, i, part):
-        e = ebuf[i, :, part * half:(part + 1) * half]
+    lane = lax.broadcasted_iota(jnp.int32, (B, HD), 1) % 8
+
+    def spread_heads(dst, part):
         for h in range(HL):
             keep = jnp.where(lane == h, 1.0, 0.0).astype(BF16)
-            dst[h * B:(h + 1) * B, :] = e * keep
-
-    spread_heads(lbuf_a, 0, 0)
+            for q in range(LCH):
+                dst[q, h * B:(h + 1) * B, :] = ebuf[part * LCH + q] * keep
+
+    spread_heads(lbuf_a, 0)
 
     def step_fn(i, carry):
         slot = lax.rem(i, RING)
@@ -120,11 +120,11 @@
             right = jnp.concatenate([wbuf[slot, rows, 2 * pair].reshape(half, HD), second.reshape(half, HD)], axis=1)
             return dot(left, right)
 
-        spread_heads(lbuf_b, i, 1)
-        left_a = lbuf_a[...]
+        spread_heads(lbuf_b, 2 * i + 1)
+        left_a = jnp.concatenate([lbuf_a[q] for q in range(LCH)], axis=1)
         first = [product(left_a, 0, pair) for pair in range(2)]
-        spread_heads(lbuf_a, jnp.minimum(i + 1, STEPS - 1), 0)
-        left_b = lbuf_b[...]
+        spread_heads(lbuf_a, jnp.minimum(2 * i + 2, 2 * STEPS - 1))
+        left_b = jnp.concatenate([lbuf_b[q] for q in range(LCH)], axis=1)
         for pair in range(2):
             acc[pair] += first[pair] + product(left_b, 1, pair)
 
@@ -204,9 +204,9 @@
             pltpu.VMEM((RING, DCH, HL, HD), BF16),
             pltpu.VMEM((B, HL, HD, HD), F32),
             pltpu.VMEM((NC * B, HD), BF16),
-            pltpu.VMEM((STEPS, B, DCH * HL), BF16),
-            pltpu.VMEM((HL * B, DCH * HL // 2), BF16),
-            pltpu.VMEM((HL * B, DCH * HL // 2), BF16),
+            pltpu.VMEM((2 * STEPS * LCH, B, HD), BF16),
+            pltpu.VMEM((LCH, HL * B, HD), BF16),
+            pltpu.VMEM((LCH, HL * B, HD), BF16),
             pltpu.VMEM((2, HL * B, 2 * HD), F32),
             pltpu.VMEM((HL, 2 * HD, B), BF16),
             pltpu.VMEM((HL, B, HD), F32),
@@ -251,7 +251,7 @@
 
 
 def exchange(left, wbuf, wwait, before_sends, pair_scale, mid_work, cross_scale, core, mate, across,
-             a_send, a_recv, b_send, b_recv, total, sems, first=None):
+             a_send, a_recv, b_send, b_recv, total, sems, use, first=None):
     sa, ra, sb, rb, sc, rc = sems
 
     def product(half, j):
@@ -286,10 +286,12 @@
         b_copies[j].wait_recv()
         total[core, j] = b_send[j] * scale[0] + b_recv[j] * scale[1] if scale else b_send[j] + b_recv[j]
         c_copies[j].start()
-    for j in range(NCH):
-        c_copies[j].wait_recv()
-    for cp in a_copies + b_copies + c_copies:
-        cp.wait_send()
+        if j >= 1:
+            c_copies[j - 1].wait_recv()
+            use(j - 1)
+    c_copies[NCH - 1].wait_recv()
+    use(NCH - 1)
+    return a_copies + b_copies + c_copies
 
 
 def exchange_scratch():
@@ -387,22 +389,23 @@
             return carry
         lax.fori_loop(0, WA_CH, body, 0)
 
-    exchange(og_ref[...], wbuf, wait_w, before_sends, pair_scale, relayout, cross_scale, core, mate, across,
-             a_send, a_recv, b_send, b_recv, total, (sa, ra, sb, rb, sc, rc))
-    ss_mate.wait_send()
-    ss_across.wait_send()
-
-    per = CW // HD
     alpha = alpha_ref[0]
     beta = beta_ref[0]
-    sq = jnp.zeros((B, HD), F32)
-    mids = []
-    for c in range(NC):
-        a1 = total[c // (NC // 2), (c % (NC // 2)) // per, :, (c % per) * HD:(c % per + 1) * HD]
-        m = (alpha * h1_ref[:, c * HD:(c + 1) * HD].astype(F32) + beta * a1).astype(BF16)
-        h2_ref[:, c * HD:(c + 1) * HD] = m
-        x = m.astype(F32)
-        sq = sq + x * x
+    squares = [jnp.zeros((B, HD), F32)]
+
+    def use(j):
+        for half in range(2):
+            for p in range(CW // HD):
+                cols = slice(half * (D // 2) + j * CW + p * HD, half * (D // 2) + j * CW + (p + 1) * HD)
+                a1 = total[half, j, :, p * HD:(p + 1) * HD]
+                m = (alpha * h1_ref[:, cols].astype(F32) + beta * a1).astype(BF16)
+                h2_ref[:, cols] = m
+                x = m.astype(F32)
+                squares[0] = squares[0] + x * x
+
+    sent = exchange(og_ref[...], wbuf, wait_w, before_sends, pair_scale, relayout, cross_scale, core, mate, across,
+                    a_send, a_recv, b_send, b_recv, total, (sa, ra, sb, rb, sc, rc), use)
+    sq = squares[0]
     inv2 = lax.rsqrt(jnp.sum(sq, axis=1, keepdims=True) / D + EPS)
     for c in range(NC):
         m = h2_ref[:, c * HD:(c + 1) * HD].astype(F32)
@@ -438,6 +441,8 @@
                 vn_ref[kv] = x.astype(BF16).astype(F32)
     for cp in caches:
         cp.wait()
+    for cp in sent + [ss_mate, ss_across]:
+        cp.wait_send()
 
 
 def middle(og, ss, h1, g2, alpha, beta, cache_len, w_out, w_attn, k_cache, v_cache, w_next):
@@ -467,6 +472,7 @@
 
 
 ROWS = 4
+ROWS_MM = 8
 
 
 def attention_kernel(len_ref, q_ref, kn_ref, vn_ref, kin_ref, vin_ref, at_ref, ko_ref, vo_ref, kbuf, vbuf, osem):
@@ -496,7 +502,7 @@
     lax.fori_loop(0, B // ROWS, insert, 0)
 
     def body(i, carry):
-        rows = [i * ROWS + r for r in range(ROWS)]
+        rows = [i * ROWS_MM + r for r in range(ROWS_MM)]
         lens = [len_ref[b] for b in rows]
         scores = []
         for b, p in zip(rows, lens):
@@ -514,7 +520,7 @@
             at_ref[pl.ds(b * 8, 8), :] = jnp.where(row8 < 4, o[:, 0:HD], o[:, HD:])
         return carry
 
-    lax.fori_loop(0, B // ROWS, body, 0)
+    lax.fori_loop(0, B // ROWS_MM, body, 0)
 
     def drain(b, carry):
         for cp in outs(b):
@@ -545,15 +551,18 @@
     start_w, wait_w = out_weights(wout_ref, wbuf, wsem, core, begin=1)
     start_w()
     left = jnp.concatenate([at_ref[pl.ds(j, B, stride=8), :].astype(BF16) for j in range(8)], axis=1)
-    exchange(left, wbuf, wait_w, lambda: await_peers(2), lambda: None, lambda: None, lambda: None, core, mate, across,
-             a_send, a_recv, b_send, b_recv, total, (sa, ra, sb, rb, sc, rc), first=first_ref)
-    per = CW // HD
     alpha = alpha_ref[1]
     beta = beta_ref[1]
-    for c in range(NC):
-        a2 = total[c // (NC // 2), (c % (NC // 2)) // per, :, (c % per) * HD:(c % per + 1) * HD]
-        cols = slice(c * HD, (c + 1) * HD)
-        out_ref[:, cols] = (alpha * h2_ref[:, cols].astype(F32) + beta * a2).astype(BF16)
+
+    def use(j):
+        for half in range(2):
+            cols = slice(half * (D // 2) + j * CW, half * (D // 2) + (j + 1) * CW)
+            out_ref[:, cols] = (alpha * h2_ref[:, cols].astype(F32) + beta * total[half, j]).astype(BF16)
+
+    sent = exchange(left, wbuf, wait_w, lambda: await_peers(2), lambda: None, lambda: None, lambda: None, core, mate,
+                    across, a_send, a_recv, b_send, b_recv, total, (sa, ra, sb, rb, sc, rc), use, first=first_ref)
+    for cp in sent:
+        cp.wait_send()
 
 
 def last(at, h2, alpha, beta, w_out, w_first):

time: 62.8 us -> 60.2 us (0.959)
  Pallas kernels: 61.3 us -> 58.6 us
    pallas_call x1, Pallas kernels: 24.7 us -> 23.1 us  [lightning(): pl.pallas_call(lightning_kernel, out_shape=[jax.ShapeDtypeStruct((B, HL,...]
    pallas_call x1, Pallas kernels: 17.5 us -> 16.9 us  [middle(): pl.pallas_call(mid_kernel, out_shape=[jax.ShapeDtypeStruct((B * 8, HD), F...]
where the time goes in v6:
time: 60.2 us; the launch traced here: 60 us
  Pallas kernels  58.6 us (97%)
  between operations  0.73 us (1%)
  local copies, waits for them, and re-layouts  0.72 us (1%)
    pallas_call x1, Pallas kernels, lightning(): pl.pallas_call(lightning_kernel, out_shape=[jax.ShapeDtypeStruct((B, HL,...  23.1 us
    pallas_call x1, Pallas kernels, middle(): pl.pallas_call(mid_kernel, out_shape=[jax.ShapeDtypeStruct((B * 8, HD), F...  16.9 us
    pallas_call x1, Pallas kernels, last(): pl.pallas_call(last_kernel, out_shape=jax.ShapeDtypeStruct((B, D), BF16),...  11.7 us
    pallas_call x1, Pallas kernels, attention(): pl.pallas_call(attention_kernel, out_shape=[jax.ShapeDtypeStruct((B * 8,...  6.92 us

profile of v6, /device:TPU:0, one launch (start us, length us, event | category | flops | bytes accessed | tf_op | source)
XLA Modules:
  0.0 60.0 jit_solution(18074851889217425552)
XLA Ops:
  0.6 0.0 copy-start
  0.6 0.0 copy-start.1
  0.7 0.0 copy-start.2
  0.7 0.0 copy-start.3
  0.7 23.1 %lightning.1 = (f32[32,8,128,128]{3,2,1,0:T(8,128)}, bf16[32,1024]{1,0:T(8,128)(2,1)S(1)}, f32[32,128]{1,0:T(8,128)S(1)}, bf16[32,4096]{1,0:T(8,128)(2,1)S(1)}) custom-call(bf16[32,4096]{1,0:T(8,128)(2,1)} %hid_hbm.1, f32[32,128]{1,0:T(8,128)} %bitcast.12, f32[8]{0:T(128)} %slopes_hbm.1, f32[8,128]{1,0:T(8,128)} %onorm_hbm.1, f32[32,8,128,128]{3,2,1,0:T(8,128)} %state_ref.1, ...), custom_call_target="tpu_custom_call" | custom-call | tf_op jit(solution)/shard_map/lightning/pallas_call | solution.py:192
  23.7 0.0 copy-done
  23.8 0.0 copy-done.1
  23.8 0.0 copy-done.2
  23.8 0.0 copy-done.3
  23.8 16.9 %middle.1 = (f32[256,128]{1,0:T(8,128)S(1)}, f32[2,32,128]{2,1,0:T(8,128)S(1)}, f32[2,32,128]{2,1,0:T(8,128)S(1)}, bf16[32,4096]{1,0:T(8,128)(2,1)S(1)}, bf16[32...) custom-call(bf16[32,1024]{1,0:T(8,128)(2,1)S(1)} %get-tuple-element.18.og_re, ...), custom_call_target="tpu_custom_call" | custom-call | tf_op jit(solution)/shard_map/middle/pallas_call | solution.py:449
  40.7 6.9 %attention.1 = (f32[256,128]{1,0:T(8,128)S(1)}, bf16[32,2,512,128]{3,2,1,0:T(8,128)(2,1)}, bf16[32,2,512,128]{3,2,1,0:T(8,128)(2,1)}, bf16[32,2,512,128]{3,2,1,0:T(8,128)(2,1)S(1)}, bf16[32,2,512,128]{3,2,1,0:T(8,128)(2,1)S(1)}) custom-call(s32[32]{0:T(128)S(1)} %copy-done.1, ...), custom_call_target="tpu_custom_call", output_to_operand_aliasing={{3}: (4, {}), {4}: (5, {})} | custom-call | tf_op jit(solution)/shard_map/attention/pallas_call | solution.py:534
  47.6 11.7 %last.1 = bf16[32,4096]{1,0:T(8,128)(2,1)S(1)} custom-call(f32[256,128]{1,0:T(8,128)S(1)} %get-tuple-element.26.at_ref, bf16[32,4096]{1,0:T(8,128)(2,1)S(1)} %get-tuple-element.27.h2_ref, f32[2]{0:T(128)S(1)} %copy-done.2, f32[2]{0:T(128)S(1)} %copy-done.3, bf16[1024,4096]{1,0:T(8,128)(2,1)} %bitcast.9, bf16[2,1024,512]{2,1,0:T(8,128)(2,1)S(1)} %get-tuple-element.28.first_ref), custom_call_target="tpu_custom_call" | custom-call | tf_op jit(solution)/shard_map/last/pallas_call | solution.py:569
  59.3 0.7 %copy.25 = bf16[32,4096]{1,0:T(8,128)(2,1)} copy(bf16[32,4096]{1,0:T(8,128)(2,1)S(1)} %last.1) | data formatting | bytes 524288
Async XLA Ops:
  0.6 23.1 %copy-start = (f32[4096]{0:T(1024)S(1)}, f32[4096]{0:T(1024)}, u32[]{:S(2)}) copy-start(f32[4096]{0:T(1024)} %param.27) | copy-start | bytes 49156
  0.6 23.1 %copy-start.1 = (s32[32]{0:T(128)S(1)}, s32[32]{0:T(128)}, u32[]{:S(2)}) copy-start(s32[32]{0:T(128)} %len_ref.3) | copy-start | bytes 388
  0.7 23.1 %copy-start.2 = (f32[2]{0:T(128)S(1)}, f32[2]{0:T(128)}, u32[]{:S(2)}) copy-start(f32[2]{0:T(128)} %alpha_ref.3) | copy-start | bytes 28
  0.7 23.1 %copy-start.3 = (f32[2]{0:T(128)S(1)}, f32[2]{0:T(128)}, u32[]{:S(2)}) copy-start(f32[2]{0:T(128)} %beta_ref.3) | copy-start | bytes 28

commit v7 on v6

--- a/solution.py
+++ b/solution.py
@@ -221,7 +221,7 @@
     )(hidden, g1, slopes, out_norm, lin_state, w_qkv, w_gate)
 
 
-NCH = 4
+NCH = 8
 CW = D // 2 // NCH
 
 
@@ -336,12 +336,16 @@
 NJ = KV * (GQ + 2)
 
 
-def mid_kernel(og_ref, ss_ref, h1_ref, g2_ref, alpha_ref, beta_ref, len_ref, wout_ref, wattn_ref,
+def mid_kernel(og_ref, ss_ref, h1_ref, g2_ref, alpha_hbm, beta_hbm, len_hbm, wout_ref, wattn_ref,
                k_ref, v_ref, wnext_ref, q_ref, kn_ref, vn_ref, h2_ref, kbuf, vbuf, wnext,
                wbuf, a_send, a_recv, b_send, b_recv, total, wsem, sa, ra, sb, rb, sc, rc,
-               wraw, wide, w2, ss_recv, ss_chip, wasem, ss_s, ss_r, csem):
+               wraw, wide, w2, ss_recv, ss_chip, alpha_ref, beta_ref, len_ref, wasem, ss_s, ss_r, csem, psem):
     core, mate, across = peers()
     say_here((mate, across))
+    scalars = [pltpu.make_async_copy(src, dst, psem.at[n]) for n, (src, dst) in enumerate(
+        ((alpha_hbm, alpha_ref), (beta_hbm, beta_ref), (len_hbm, len_ref)))]
+    for cp in scalars:
+        cp.start()
     start_w, wait_w = out_weights(wout_ref, wbuf, wsem, core)
     start_w()
 
@@ -376,6 +380,8 @@
         return root(ss_ref[...], D // 4) * inv, root(ss_recv[0], D // 4) * inv
 
     def cross_scale():
+        for cp in scalars:
+            cp.wait()
         ss_across.wait_recv()
         inv = lax.rsqrt((ss_chip[:, 0:1] + ss_recv[1, :, 0:1]) / D + EPS)
         return root(ss_chip[...], D // 2) * inv, root(ss_recv[1], D // 2) * inv
@@ -389,8 +395,6 @@
             return carry
         lax.fori_loop(0, WA_CH, body, 0)
 
-    alpha = alpha_ref[0]
-    beta = beta_ref[0]
     squares = [jnp.zeros((B, HD), F32)]
 
     def use(j):
@@ -398,7 +402,7 @@
             for p in range(CW // HD):
                 cols = slice(half * (D // 2) + j * CW + p * HD, half * (D // 2) + j * CW + (p + 1) * HD)
                 a1 = total[half, j, :, p * HD:(p + 1) * HD]
-                m = (alpha * h1_ref[:, cols].astype(F32) + beta * a1).astype(BF16)
+                m = (alpha_ref[0] * h1_ref[:, cols].astype(F32) + beta_ref[0] * a1).astype(BF16)
                 h2_ref[:, cols] = m
                 x = m.astype(F32)
                 squares[0] = squares[0] + x * x
@@ -452,7 +456,7 @@
                    jax.ShapeDtypeStruct((KV, B, HD), F32), jax.ShapeDtypeStruct((B, D), BF16),
                    pltpu.VMEM((B, KV, T, HD), BF16), pltpu.VMEM((B, KV, T, HD), BF16),
                    pltpu.VMEM((2, HL * HD, CW), BF16)],
-        in_specs=[vmem_spec(), vmem_spec(), vmem_spec(), vmem_spec(), smem_spec(), smem_spec(), smem_spec(),
+        in_specs=[vmem_spec(), vmem_spec(), vmem_spec(), vmem_spec(), any_spec(), any_spec(), any_spec(),
                   any_spec(), any_spec(), any_spec(), any_spec(), any_spec()],
         out_specs=[vmem_spec()] * 7,
         scratch_shapes=exchange_scratch() + [
@@ -461,10 +465,14 @@
             pltpu.VMEM((NJ, D, HD), BF16),
             pltpu.VMEM((2, B, HD), F32),
             pltpu.VMEM((B, HD), F32),
+            pltpu.SMEM((2,), F32),
+            pltpu.SMEM((2,), F32),
+            pltpu.SMEM((B,), jnp.int32),
             pltpu.SemaphoreType.DMA((WA_CH,)),
             pltpu.SemaphoreType.DMA((2,)),
             pltpu.SemaphoreType.DMA((2,)),
             pltpu.SemaphoreType.DMA((4,)),
+            pltpu.SemaphoreType.DMA((3,)),
         ],
         compiler_params=pltpu.CompilerParams(vmem_limit_bytes=35 * MIB, collective_id=0, has_side_effects=True),
         name="middle",
@@ -544,22 +552,27 @@
     )(cache_len, q, kn, vn, kbuf, vbuf)[:3]
 
 
-def last_kernel(at_ref, h2_ref, alpha_ref, beta_ref, wout_ref, first_ref, out_ref,
-                wbuf, a_send, a_recv, b_send, b_recv, total, wsem, sa, ra, sb, rb, sc, rc):
+def last_kernel(at_ref, h2_ref, alpha_hbm, beta_hbm, wout_ref, first_ref, out_ref,
+                wbuf, a_send, a_recv, b_send, b_recv, total, wsem, sa, ra, sb, rb, sc, rc,
+                alpha_ref, beta_ref, psem):
     core, mate, across = peers()
     say_here((mate, across))
+    scalars = [pltpu.make_async_copy(alpha_hbm, alpha_ref, psem.at[0]), pltpu.make_async_copy(beta_hbm, beta_ref, psem.at[1])]
+    for cp in scalars:
+        cp.start()
     start_w, wait_w = out_weights(wout_ref, wbuf, wsem, core, begin=1)
     start_w()
     left = jnp.concatenate([at_ref[pl.ds(j, B, stride=8), :].astype(BF16) for j in range(8)], axis=1)
-    alpha = alpha_ref[1]
-    beta = beta_ref[1]
+    def settle():
+        for cp in scalars:
+            cp.wait()
 
     def use(j):
         for half in range(2):
             cols = slice(half * (D // 2) + j * CW, half * (D // 2) + (j + 1) * CW)
-            out_ref[:, cols] = (alpha * h2_ref[:, cols].astype(F32) + beta * total[half, j]).astype(BF16)
-
-    sent = exchange(left, wbuf, wait_w, lambda: await_peers(2), lambda: None, lambda: None, lambda: None, core, mate,
+            out_ref[:, cols] = (alpha_ref[1] * h2_ref[:, cols].astype(F32) + beta_ref[1] * total[half, j]).astype(BF16)
+
+    sent = exchange(left, wbuf, wait_w, lambda: await_peers(2), lambda: None, settle, lambda: None, core, mate,
                     across, a_send, a_recv, b_send, b_recv, total, (sa, ra, sb, rb, sc, rc), use, first=first_ref)
     for cp in sent:
         cp.wait_send()
@@ -569,9 +582,9 @@
     return pl.pallas_call(
         last_kernel,
         out_shape=jax.ShapeDtypeStruct((B, D), BF16),
-        in_specs=[vmem_spec(), vmem_spec(), smem_spec(), smem_spec(), any_spec(), vmem_spec()],
+        in_specs=[vmem_spec(), vmem_spec(), any_spec(), any_spec(), any_spec(), vmem_spec()],
         out_specs=vmem_spec(),
-        scratch_shapes=exchange_scratch(),
+        scratch_shapes=exchange_scratch() + [pltpu.SMEM((2,), F32), pltpu.SMEM((2,), F32), pltpu.SemaphoreType.DMA((2,))],
         compiler_params=pltpu.CompilerParams(vmem_limit_bytes=16 * MIB, collective_id=1, has_side_effects=True),
         name="last",
     )(at, h2, alpha, beta, w_out, w_first)
@@ -595,11 +608,11 @@
         wa = jnp.transpose(w_attn, (0, 2, 1, 3)).reshape(WA_ROWS, HD)
         state_out, og, ss, h1 = lightning(hbm(hidden), hbm(g1), hbm(slopes), hbm(out_norm), hbm(lin_state), hbm(w_qkv), hbm(w_gate))
         w_last = hbm(w_out_attn.reshape(HL * HD, D))
-        q, kn, vn, h2, kbuf, vbuf, w_first = middle(og, ss, h1, g2, mix_alpha, mix_beta, cache_len,
+        q, kn, vn, h2, kbuf, vbuf, w_first = middle(og, ss, h1, g2, hbm(mix_alpha), hbm(mix_beta), hbm(cache_len),
                                                     hbm(w_out_lin.reshape(HL * HD, D)), hbm(wa), hbm(k_cache),
                                                     hbm(v_cache), w_last)
         at, k_out, v_out = attention(cache_len, q, kn, vn, kbuf, vbuf)
-        hidden_out = last(at, h2, mix_alpha, mix_beta, w_last, w_first)
+        hidden_out = last(at, h2, hbm(mix_alpha), hbm(mix_beta), w_last, w_first)
         return hidden_out, state_out, k_out, v_out
 
     return jax.shard_map(local_step, mesh=mesh, in_specs=in_specs, out_specs=out_specs, check_vma=False)

time: 60.2 us -> 61.8 us (1.027)
  Pallas kernels: 58.6 us -> 60.2 us
    pallas_call x1, Pallas kernels: 16.9 us -> 19 us  [middle(): pl.pallas_call(mid_kernel, out_shape=[jax.ShapeDtypeStruct((B * 8, HD), F...]
where the time goes in v7:
time: 61.8 us; the launch traced here: 61.6 us
  Pallas kernels  60.2 us (97%)
  local copies, waits for them, and re-layouts  0.72 us (1%)
  between operations  0.7 us (1%)
    pallas_call x1, Pallas kernels, lightning(): pl.pallas_call(lightning_kernel, out_shape=[jax.ShapeDtypeStruct((B, HL,...  23.1 us
    pallas_call x1, Pallas kernels, middle(): pl.pallas_call(mid_kernel, out_shape=[jax.ShapeDtypeStruct((B * 8, HD), F...  19 us
    pallas_call x1, Pallas kernels, last(): pl.pallas_call(last_kernel, out_shape=jax.ShapeDtypeStruct((B, D), BF16),...  11.2 us
    pallas_call x1, Pallas kernels, attention(): pl.pallas_call(attention_kernel, out_shape=[jax.ShapeDtypeStruct((B * 8,...  6.92 us

profile of v7, /device:TPU:0, one launch (start us, length us, event | category | flops | bytes accessed | tf_op | source)
XLA Modules:
  0.0 61.6 jit_solution(13770500336658765303)
XLA Ops:
  0.6 0.0 copy-start
  0.6 23.1 %lightning.1 = (f32[32,8,128,128]{3,2,1,0:T(8,128)}, bf16[32,1024]{1,0:T(8,128)(2,1)S(1)}, f32[32,128]{1,0:T(8,128)S(1)}, bf16[32,4096]{1,0:T(8,128)(2,1)S(1)}) custom-call(bf16[32,4096]{1,0:T(8,128)(2,1)} %hid_hbm.1, f32[32,128]{1,0:T(8,128)} %bitcast.12, f32[8]{0:T(128)} %slopes_hbm.1, f32[8,128]{1,0:T(8,128)} %onorm_hbm.1, f32[32,8,128,128]{3,2,1,0:T(8,128)} %state_ref.1, ...), custom_call_target="tpu_custom_call" | custom-call | tf_op jit(solution)/shard_map/lightning/pallas_call | solution.py:192
  23.7 0.0 copy-done
  23.7 0.0 copy-start.1
  23.8 19.0 %middle.1 = (f32[256,128]{1,0:T(8,128)S(1)}, f32[2,32,128]{2,1,0:T(8,128)S(1)}, f32[2,32,128]{2,1,0:T(8,128)S(1)}, bf16[32,4096]{1,0:T(8,128)(2,1)S(1)}, bf16[32...) custom-call(bf16[32,1024]{1,0:T(8,128)(2,1)S(1)} %get-tuple-element.18.og_re, ...), custom_call_target="tpu_custom_call" | custom-call | tf_op jit(solution)/shard_map/middle/pallas_call | solution.py:453
  42.8 0.0 copy-done.1
  42.8 6.9 %attention.1 = (f32[256,128]{1,0:T(8,128)S(1)}, bf16[32,2,512,128]{3,2,1,0:T(8,128)(2,1)}, bf16[32,2,512,128]{3,2,1,0:T(8,128)(2,1)}, bf16[32,2,512,128]{3,2,1,0:T(8,128)(2,1)S(1)}, bf16[32,2,512,128]{3,2,1,0:T(8,128)(2,1)S(1)}) custom-call(s32[32]{0:T(128)S(1)} %copy-done.1, ...), custom_call_target="tpu_custom_call", output_to_operand_aliasing={{3}: (4, {}), {4}: (5, {})} | custom-call | tf_op jit(solution)/shard_map/attention/pallas_call | solution.py:542
  49.7 11.2 %last.1 = bf16[32,4096]{1,0:T(8,128)(2,1)S(1)} custom-call(f32[256,128]{1,0:T(8,128)S(1)} %get-tuple-element.26.at_ref, bf16[32,4096]{1,0:T(8,128)(2,1)S(1)} %get-tuple-element.27.h2_ref, f32[2]{0:T(128)} %alpha_hbm.3, f32[2]{0:T(128)} %beta_hbm.3, bf16[1024,4096]{1,0:T(8,128)(2,1)} %bitcast.9, bf16[2,1024,256]{2,1,0:T(8,128)(2,1)S(1)} %get-tuple-element.28.first_ref), custom_call_target="tpu_custom_call" | custom-call | tf_op jit(solution)/shard_map/last/pallas_call | solution.py:582
  60.9 0.7 %copy.25 = bf16[32,4096]{1,0:T(8,128)(2,1)} copy(bf16[32,4096]{1,0:T(8,128)(2,1)S(1)} %last.1) | data formatting | bytes 524288
Async XLA Ops:
  0.6 23.1 %copy-start = (f32[4096]{0:T(1024)S(1)}, f32[4096]{0:T(1024)}, u32[]{:S(2)}) copy-start(f32[4096]{0:T(1024)} %param.27) | copy-start | bytes 49156
  23.7 19.1 %copy-start.1 = (s32[32]{0:T(128)S(1)}, s32[32]{0:T(128)}, u32[]{:S(2)}) copy-start(s32[32]{0:T(128)} %len_ref.1) | copy-start | bytes 388

commit v8 on v7

--- a/solution.py
+++ b/solution.py
@@ -221,8 +221,8 @@
     )(hidden, g1, slopes, out_norm, lin_state, w_qkv, w_gate)
 
 
-NCH = 8
-CW = D // 2 // NCH
+MID_CHUNKS = 4
+LAST_CHUNKS = 8
 
 
 def peers():
@@ -251,17 +251,18 @@
 
 
 def exchange(left, wbuf, wwait, before_sends, pair_scale, mid_work, cross_scale, core, mate, across,
-             a_send, a_recv, b_send, b_recv, total, sems, use, first=None):
+             a_send, a_recv, b_send, b_recv, total, sems, use, nch, first=None):
     sa, ra, sb, rb, sc, rc = sems
+    width = D // 2 // nch
 
     def product(half, j):
         wwait(half, j)
-        buf, at = (wbuf, half * NCH + j) if first is None or j > 0 else (first, half)
-        return jnp.concatenate([dot(left, buf[at, :, c:c + 2 * HD]) for c in range(0, CW, 2 * HD)], axis=1)
-
-    a_copies = [rcopy(a_send.at[j], a_recv.at[j], sa.at[j], ra.at[j], mate) for j in range(NCH)]
-    b_copies = [rcopy(b_send.at[j], b_recv.at[j], sb.at[j], rb.at[j], across) for j in range(NCH)]
-    c_copies = [rcopy(total.at[core, j], total.at[core, j], sc.at[j], rc.at[j], mate) for j in range(NCH)]
+        buf, at = (wbuf, half * nch + j) if first is None or j > 0 else (first, half)
+        return jnp.concatenate([dot(left, buf[at, :, c:c + 2 * HD]) for c in range(0, width, 2 * HD)], axis=1)
+
+    a_copies = [rcopy(a_send.at[j], a_recv.at[j], sa.at[j], ra.at[j], mate) for j in range(nch)]
+    b_copies = [rcopy(b_send.at[j], b_recv.at[j], sb.at[j], rb.at[j], across) for j in range(nch)]
+    c_copies = [rcopy(total.at[core, j], total.at[core, j], sc.at[j], rc.at[j], mate) for j in range(nch)]
 
     def send_across(j, scale):
         a_copies[j].wait_recv()
@@ -269,7 +270,7 @@
         b_copies[j].start()
 
     scale = None
-    for j in range(NCH):
+    for j in range(nch):
         a_send[j] = product(1 - core, j)
         if j == 0:
             before_sends()
@@ -279,47 +280,50 @@
             scale = pair_scale()
         if j >= 1:
             send_across(j - 1, scale)
-    send_across(NCH - 1, scale)
+    send_across(nch - 1, scale)
     mid_work()
     scale = cross_scale()
-    for j in range(NCH):
+    for j in range(nch):
         b_copies[j].wait_recv()
         total[core, j] = b_send[j] * scale[0] + b_recv[j] * scale[1] if scale else b_send[j] + b_recv[j]
         c_copies[j].start()
         if j >= 1:
             c_copies[j - 1].wait_recv()
             use(j - 1)
-    c_copies[NCH - 1].wait_recv()
-    use(NCH - 1)
+    c_copies[nch - 1].wait_recv()
+    use(nch - 1)
     return a_copies + b_copies + c_copies
 
 
-def exchange_scratch():
+def exchange_scratch(nch):
+    width = D // 2 // nch
     return [
-        pltpu.VMEM((2 * NCH, HL * HD, CW), BF16),
-        pltpu.VMEM((NCH, B, CW), F32),
-        pltpu.VMEM((NCH, B, CW), F32),
-        pltpu.VMEM((NCH, B, CW), F32),
-        pltpu.VMEM((NCH, B, CW), F32),
-        pltpu.VMEM((2, NCH, B, CW), F32),
-        pltpu.SemaphoreType.DMA((2 * NCH,)),
-        pltpu.SemaphoreType.DMA((NCH,)),
-        pltpu.SemaphoreType.DMA((NCH,)),
-        pltpu.SemaphoreType.DMA((NCH,)),
-        pltpu.SemaphoreType.DMA((NCH,)),
-        pltpu.SemaphoreType.DMA((NCH,)),
-        pltpu.SemaphoreType.DMA((NCH,)),
+        pltpu.VMEM((2 * nch, HL * HD, width), BF16),
+        pltpu.VMEM((nch, B, width), F32),
+        pltpu.VMEM((nch, B, width), F32),
+        pltpu.VMEM((nch, B, width), F32),
+        pltpu.VMEM((nch, B, width), F32),
+        pltpu.VMEM((2, nch, B, width), F32),
+        pltpu.SemaphoreType.DMA((2 * nch,)),
+        pltpu.SemaphoreType.DMA((nch,)),
+        pltpu.SemaphoreType.DMA((nch,)),
+        pltpu.SemaphoreType.DMA((nch,)),
+        pltpu.SemaphoreType.DMA((nch,)),
+        pltpu.SemaphoreType.DMA((nch,)),
+        pltpu.SemaphoreType.DMA((nch,)),
     ]
 
 
-def out_weights(w_ref, wbuf, wsem, core, begin=0):
+def out_weights(w_ref, wbuf, wsem, core, nch, begin=0):
+    width = D // 2 // nch
+
     def copy(half, j):
-        at = half * NCH + j
-        cols = pl.ds(pl.multiple_of(at * CW, CW), CW)
+        at = half * nch + j
+        cols = pl.ds(pl.multiple_of(at * width, width), width)
         return pltpu.make_async_copy(w_ref.at[:, cols], wbuf.at[at], wsem.at[at])
 
     def start():
-        for j in range(begin, NCH):
+        for j in range(begin, nch):
             copy(1 - core, j).start()
             copy(core, j).start()
 
@@ -346,7 +350,7 @@
         ((alpha_hbm, alpha_ref), (beta_hbm, beta_ref), (len_hbm, len_ref)))]
     for cp in scalars:
         cp.start()
-    start_w, wait_w = out_weights(wout_ref, wbuf, wsem, core)
+    start_w, wait_w = out_weights(wout_ref, wbuf, wsem, core, MID_CHUNKS)
     start_w()
 
     def wa_copy(i):
@@ -358,7 +362,7 @@
 
     lax.fori_loop(0, WA_CH, wa_start, 0)
     caches = [pltpu.make_async_copy(k_ref, kbuf, csem.at[0]), pltpu.make_async_copy(v_ref, vbuf, csem.at[1])]
-    caches += [pltpu.make_async_copy(wnext_ref.at[:, pl.ds(h * (D // 2), CW)], wnext.at[h], csem.at[2 + h]) for h in range(2)]
+    caches += [pltpu.make_async_copy(wnext_ref.at[:, pl.ds(h * (D // 2), D // 2 // LAST_CHUNKS)], wnext.at[h], csem.at[2 + h]) for h in range(2)]
     for cp in caches:
         cp.start()
     ss_mate = rcopy(ss_ref, ss_recv.at[0], ss_s.at[0], ss_r.at[0], mate)
@@ -398,9 +402,10 @@
     squares = [jnp.zeros((B, HD), F32)]
 
     def use(j):
+        wide_cols = D // 2 // MID_CHUNKS
         for half in range(2):
-            for p in range(CW // HD):
-                cols = slice(half * (D // 2) + j * CW + p * HD, half * (D // 2) + j * CW + (p + 1) * HD)
+            for p in range(wide_cols // HD):
+                cols = slice(half * (D // 2) + j * wide_cols + p * HD, half * (D // 2) + j * wide_cols + (p + 1) * HD)
                 a1 = total[half, j, :, p * HD:(p + 1) * HD]
                 m = (alpha_ref[0] * h1_ref[:, cols].astype(F32) + beta_ref[0] * a1).astype(BF16)
                 h2_ref[:, cols] = m
@@ -408,7 +413,7 @@
                 squares[0] = squares[0] + x * x
 
     sent = exchange(og_ref[...], wbuf, wait_w, before_sends, pair_scale, relayout, cross_scale, core, mate, across,
-                    a_send, a_recv, b_send, b_recv, total, (sa, ra, sb, rb, sc, rc), use)
+                    a_send, a_recv, b_send, b_recv, total, (sa, ra, sb, rb, sc, rc), use, MID_CHUNKS)
     sq = squares[0]
     inv2 = lax.rsqrt(jnp.sum(sq, axis=1, keepdims=True) / D + EPS)
     for c in range(NC):
@@ -455,11 +460,11 @@
         out_shape=[jax.ShapeDtypeStruct((B * 8, HD), F32), jax.ShapeDtypeStruct((KV, B, HD), F32),
                    jax.ShapeDtypeStruct((KV, B, HD), F32), jax.ShapeDtypeStruct((B, D), BF16),
                    pltpu.VMEM((B, KV, T, HD), BF16), pltpu.VMEM((B, KV, T, HD), BF16),
-                   pltpu.VMEM((2, HL * HD, CW), BF16)],
+                   pltpu.VMEM((2, HL * HD, D // 2 // LAST_CHUNKS), BF16)],
         in_specs=[vmem_spec(), vmem_spec(), vmem_spec(), vmem_spec(), any_spec(), any_spec(), any_spec(),
                   any_spec(), any_spec(), any_spec(), any_spec(), any_spec()],
         out_specs=[vmem_spec()] * 7,
-        scratch_shapes=exchange_scratch() + [
+        scratch_shapes=exchange_scratch(MID_CHUNKS) + [
             pltpu.VMEM((WA_CH, WA_STEP, HD), BF16),
             pltpu.VMEM((WA_STEP, HD), F32),
             pltpu.VMEM((NJ, D, HD), BF16),
@@ -560,7 +565,7 @@
     scalars = [pltpu.make_async_copy(alpha_hbm, alpha_ref, psem.at[0]), pltpu.make_async_copy(beta_hbm, beta_ref, psem.at[1])]
     for cp in scalars:
         cp.start()
-    start_w, wait_w = out_weights(wout_ref, wbuf, wsem, core, begin=1)
+    start_w, wait_w = out_weights(wout_ref, wbuf, wsem, core, LAST_CHUNKS, begin=1)
     start_w()
     left = jnp.concatenate([at_ref[pl.ds(j, B, stride=8), :].astype(BF16) for j in range(8)], axis=1)
     def settle():
@@ -569,11 +574,12 @@
 
     def use(j):
         for half in range(2):
-            cols = slice(half * (D // 2) + j * CW, half * (D // 2) + (j + 1) * CW)
+            at = half * (D // 2) + j * (D // 2 // LAST_CHUNKS)
+            cols = slice(at, at + D // 2 // LAST_CHUNKS)
             out_ref[:, cols] = (alpha_ref[1] * h2_ref[:, cols].astype(F32) + beta_ref[1] * total[half, j]).astype(BF16)
 
     sent = exchange(left, wbuf, wait_w, lambda: await_peers(2), lambda: None, settle, lambda: None, core, mate,
-                    across, a_send, a_recv, b_send, b_recv, total, (sa, ra, sb, rb, sc, rc), use, first=first_ref)
+                    across, a_send, a_recv, b_send, b_recv, total, (sa, ra, sb, rb, sc, rc), use, LAST_CHUNKS, first=first_ref)
     for cp in sent:
         cp.wait_send()
 
@@ -584,7 +590,7 @@
         out_shape=jax.ShapeDtypeStruct((B, D), BF16),
         in_specs=[vmem_spec(), vmem_spec(), any_spec(), any_spec(), any_spec(), vmem_spec()],
         out_specs=vmem_spec(),
-        scratch_shapes=exchange_scratch() + [pltpu.SMEM((2,), F32), pltpu.SMEM((2,), F32), pltpu.SemaphoreType.DMA((2,))],
+        scratch_shapes=exchange_scratch(LAST_CHUNKS) + [pltpu.SMEM((2,), F32), pltpu.SMEM((2,), F32), pltpu.SemaphoreType.DMA((2,))],
         compiler_params=pltpu.CompilerParams(vmem_limit_bytes=16 * MIB, collective_id=1, has_side_effects=True),
         name="last",
     )(at, h2, alpha, beta, w_out, w_first)

time: 61.8 us -> 59.4 us (0.961)
  Pallas kernels: 60.2 us -> 57.8 us
    pallas_call x1, Pallas kernels: 19 us -> 16.3 us  [middle(): pl.pallas_call(mid_kernel, out_shape=[jax.ShapeDtypeStruct((B * 8, HD), F...]
where the time goes in v8:
time: 59.4 us; the launch traced here: 59.2 us
  Pallas kernels  57.8 us (97%)
  local copies, waits for them, and re-layouts  0.72 us (1%)
  between operations  0.7 us (1%)
    pallas_call x1, Pallas kernels, lightning(): pl.pallas_call(lightning_kernel, out_shape=[jax.ShapeDtypeStruct((B, HL,...  23.1 us
    pallas_call x1, Pallas kernels, middle(): pl.pallas_call(mid_kernel, out_shape=[jax.ShapeDtypeStruct((B * 8, HD), F...  16.3 us
    pallas_call x1, Pallas kernels, last(): pl.pallas_call(last_kernel, out_shape=jax.ShapeDtypeStruct((B, D), BF16),...  11.5 us
    pallas_call x1, Pallas kernels, attention(): pl.pallas_call(attention_kernel, out_shape=[jax.ShapeDtypeStruct((B * 8,...  6.92 us

profile of v8, /device:TPU:0, one launch (start us, length us, event | category | flops | bytes accessed | tf_op | source)
XLA Modules:
  0.0 59.2 jit_solution(8737526710451312952)
XLA Ops:
  0.6 0.0 copy-start
  0.6 23.1 %lightning.1 = (f32[32,8,128,128]{3,2,1,0:T(8,128)}, bf16[32,1024]{1,0:T(8,128)(2,1)S(1)}, f32[32,128]{1,0:T(8,128)S(1)}, bf16[32,4096]{1,0:T(8,128)(2,1)S(1)}) custom-call(bf16[32,4096]{1,0:T(8,128)(2,1)} %hid_hbm.1, f32[32,128]{1,0:T(8,128)} %bitcast.12, f32[8]{0:T(128)} %slopes_hbm.1, f32[8,128]{1,0:T(8,128)} %onorm_hbm.1, f32[32,8,128,128]{3,2,1,0:T(8,128)} %state_ref.1, ...), custom_call_target="tpu_custom_call" | custom-call | tf_op jit(solution)/shard_map/lightning/pallas_call | solution.py:192
  23.7 0.0 copy-done
  23.7 0.0 copy-start.1
  23.8 16.3 %middle.1 = (f32[256,128]{1,0:T(8,128)S(1)}, f32[2,32,128]{2,1,0:T(8,128)S(1)}, f32[2,32,128]{2,1,0:T(8,128)S(1)}, bf16[32,4096]{1,0:T(8,128)(2,1)S(1)}, bf16[32...) custom-call(bf16[32,1024]{1,0:T(8,128)(2,1)S(1)} %get-tuple-element.18.og_re, ...), custom_call_target="tpu_custom_call" | custom-call | tf_op jit(solution)/shard_map/middle/pallas_call | solution.py:458
  40.1 0.0 copy-done.1
  40.1 6.9 %attention.1 = (f32[256,128]{1,0:T(8,128)S(1)}, bf16[32,2,512,128]{3,2,1,0:T(8,128)(2,1)}, bf16[32,2,512,128]{3,2,1,0:T(8,128)(2,1)}, bf16[32,2,512,128]{3,2,1,0:T(8,128)(2,1)S(1)}, bf16[32,2,512,128]{3,2,1,0:T(8,128)(2,1)S(1)}) custom-call(s32[32]{0:T(128)S(1)} %copy-done.1, ...), custom_call_target="tpu_custom_call", output_to_operand_aliasing={{3}: (4, {}), {4}: (5, {})} | custom-call | tf_op jit(solution)/shard_map/attention/pallas_call | solution.py:547
  47.0 11.5 %last.1 = bf16[32,4096]{1,0:T(8,128)(2,1)S(1)} custom-call(f32[256,128]{1,0:T(8,128)S(1)} %get-tuple-element.26.at_ref, bf16[32,4096]{1,0:T(8,128)(2,1)S(1)} %get-tuple-element.27.h2_ref, f32[2]{0:T(128)} %alpha_hbm.3, f32[2]{0:T(128)} %beta_hbm.3, bf16[1024,4096]{1,0:T(8,128)(2,1)} %bitcast.9, bf16[2,1024,256]{2,1,0:T(8,128)(2,1)S(1)} %get-tuple-element.28.first_ref), custom_call_target="tpu_custom_call" | custom-call | tf_op jit(solution)/shard_map/last/pallas_call | solution.py:588
  58.5 0.7 %copy.25 = bf16[32,4096]{1,0:T(8,128)(2,1)} copy(bf16[32,4096]{1,0:T(8,128)(2,1)S(1)} %last.1) | data formatting | bytes 524288
Async XLA Ops:
  0.6 23.1 %copy-start = (f32[4096]{0:T(1024)S(1)}, f32[4096]{0:T(1024)}, u32[]{:S(2)}) copy-start(f32[4096]{0:T(1024)} %param.27) | copy-start | bytes 49156
  23.7 16.3 %copy-start.1 = (s32[32]{0:T(128)S(1)}, s32[32]{0:T(128)}, u32[]{:S(2)}) copy-start(s32[32]{0:T(128)} %len_ref.1) | copy-start | bytes 388

commit v9 on v8

--- a/solution.py
+++ b/solution.py
@@ -254,82 +254,138 @@
              a_send, a_recv, b_send, b_recv, total, sems, use, nch, first=None):
     sa, ra, sb, rb, sc, rc = sems
     width = D // 2 // nch
-
-    def product(half, j):
-        wwait(half, j)
-        buf, at = (wbuf, half * nch + j) if first is None or j > 0 else (first, half)
+    both = nch - 1
+    rest = (nch - 1, nch)
+    own = (1 - core) * (nch + 1)
+    other = core * (nch + 1)
+
+    def product(at, j, owner):
+        wwait(at, j)
+        buf, at = (wbuf, at) if first is None or j > 0 else (first, 1 - owner)
         return jnp.concatenate([dot(left, buf[at, :, c:c + 2 * HD]) for c in range(0, width, 2 * HD)], axis=1)
 
-    a_copies = [rcopy(a_send.at[j], a_recv.at[j], sa.at[j], ra.at[j], mate) for j in range(nch)]
-    b_copies = [rcopy(b_send.at[j], b_recv.at[j], sb.at[j], rb.at[j], across) for j in range(nch)]
-    c_copies = [rcopy(total.at[core, j], total.at[core, j], sc.at[j], rc.at[j], mate) for j in range(nch)]
+    a_copies = [rcopy(a_send.at[j], a_recv.at[j], sa.at[j], ra.at[j], mate) for j in range(nch + 1)]
+    b_copies = [rcopy(b_send.at[j], b_recv.at[j], sb.at[j], rb.at[j], across) for j in range(nch + 1)]
+    c_places = [own + j for j in range(both)] + list(rest)
+    c_copies = [rcopy(total.at[at], total.at[at], sc.at[j], rc.at[j], mate) for j, at in enumerate(c_places)]
 
     def send_across(j, scale):
         a_copies[j].wait_recv()
         b_send[j] = b_send[j] * scale[0] + a_recv[j] * scale[1] if scale else b_send[j] + a_recv[j]
         b_copies[j].start()
 
-    scale = None
-    for j in range(nch):
-        a_send[j] = product(1 - core, j)
+    def finish(j, scale):
+        b_copies[j].wait_recv()
+        total[c_places[j]] = b_send[j] * scale[0] + b_recv[j] * scale[1] if scale else b_send[j] + b_recv[j]
+        c_copies[j].start()
+
+    pair = None
+    for j in range(both):
+        a_send[j] = product(other + j, j, 1 - core)
         if j == 0:
             before_sends()
         a_copies[j].start()
-        b_send[j] = product(core, j)
+        b_send[j] = product(own + j, j, core)
         if j == 1:
-            scale = pair_scale()
+            pair = pair_scale()
         if j >= 1:
-            send_across(j - 1, scale)
-    send_across(nch - 1, scale)
+            send_across(j - 1, pair)
+
+    @pl.when(core == 0)
+    def _():
+        for j in rest:
+            a_send[j] = product(j, j, 1)
+            a_copies[j].start()
+
+    @pl.when(core == 1)
+    def _():
+        for j in rest:
+            b_send[j] = product(j, j, 1)
+
+    send_across(both - 1, pair)
+
+    @pl.when(core == 1)
+    def _():
+        for j in rest:
+            send_across(j, pair)
+
     mid_work()
-    scale = cross_scale()
-    for j in range(nch):
-        b_copies[j].wait_recv()
-        total[core, j] = b_send[j] * scale[0] + b_recv[j] * scale[1] if scale else b_send[j] + b_recv[j]
-        c_copies[j].start()
+    cross = cross_scale()
+    for j in range(both):
+        finish(j, cross)
         if j >= 1:
             c_copies[j - 1].wait_recv()
-            use(j - 1)
-    c_copies[nch - 1].wait_recv()
-    use(nch - 1)
-    return a_copies + b_copies + c_copies
+            use((j - 1, nch + j))
+
+    @pl.when(core == 1)
+    def _():
+        for j in rest:
+            finish(j, cross)
+
+    c_copies[both - 1].wait_recv()
+    use((both - 1, nch + both))
+
+    @pl.when(core == 0)
+    def _():
+        for j in rest:
+            c_copies[j].wait_recv()
+
+    use(rest)
+
+    def settle_sends():
+        for cp in a_copies[:both] + b_copies[:both] + c_copies[:both]:
+            cp.wait_send()
+
+        @pl.when(core == 0)
+        def _():
+            for j in rest:
+                a_copies[j].wait_send()
+
+        @pl.when(core == 1)
+        def _():
+            for j in rest:
+                b_copies[j].wait_send()
+                c_copies[j].wait_send()
+
+    return settle_sends
 
 
 def exchange_scratch(nch):
     width = D // 2 // nch
     return [
         pltpu.VMEM((2 * nch, HL * HD, width), BF16),
-        pltpu.VMEM((nch, B, width), F32),
-        pltpu.VMEM((nch, B, width), F32),
-        pltpu.VMEM((nch, B, width), F32),
-        pltpu.VMEM((nch, B, width), F32),
-        pltpu.VMEM((2, nch, B, width), F32),
+        pltpu.VMEM((nch + 1, B, width), F32),
+        pltpu.VMEM((nch + 1, B, width), F32),
+        pltpu.VMEM((nch + 1, B, width), F32),
+        pltpu.VMEM((nch + 1, B, width), F32),
+        pltpu.VMEM((2 * nch, B, width), F32),
         pltpu.SemaphoreType.DMA((2 * nch,)),
-        pltpu.SemaphoreType.DMA((nch,)),
-        pltpu.SemaphoreType.DMA((nch,)),
-        pltpu.SemaphoreType.DMA((nch,)),
-        pltpu.SemaphoreType.DMA((nch,)),
-        pltpu.SemaphoreType.DMA((nch,)),
-        pltpu.SemaphoreType.DMA((nch,)),
+        pltpu.SemaphoreType.DMA((nch + 1,)),
+        pltpu.SemaphoreType.DMA((nch + 1,)),
+        pltpu.SemaphoreType.DMA((nch + 1,)),
+        pltpu.SemaphoreType.DMA((nch + 1,)),
+        pltpu.SemaphoreType.DMA((nch + 1,)),
+        pltpu.SemaphoreType.DMA((nch + 1,)),
     ]
 
 
 def out_weights(w_ref, wbuf, wsem, core, nch, begin=0):
     width = D // 2 // nch
 
-    def copy(half, j):
-        at = half * nch + j
+    def copy(at):
         cols = pl.ds(pl.multiple_of(at * width, width), width)
         return pltpu.make_async_copy(w_ref.at[:, cols], wbuf.at[at], wsem.at[at])
 
     def start():
-        for j in range(begin, nch):
-            copy(1 - core, j).start()
-            copy(core, j).start()
-
-    def wait(half, j):
+        for j in range(begin, nch - 1):
+            copy(core * (nch + 1) + j).start()
+            copy((1 - core) * (nch + 1) + j).start()
+        for at in (nch - 1, nch):
+            copy(at).start()
+
+    def wait(at, j):
         if j >= begin:
-            copy(half, j).wait()
+            copy(at).wait()
 
     return start, wait
 
@@ -362,7 +418,7 @@
 
     lax.fori_loop(0, WA_CH, wa_start, 0)
     caches = [pltpu.make_async_copy(k_ref, kbuf, csem.at[0]), pltpu.make_async_copy(v_ref, vbuf, csem.at[1])]
-    caches += [pltpu.make_async_copy(wnext_ref.at[:, pl.ds(h * (D // 2), D // 2 // LAST_CHUNKS)], wnext.at[h], csem.at[2 + h]) for h in range(2)]
+    caches += [pltpu.make_async_copy(wnext_ref.at[:, pl.ds(h * (LAST_CHUNKS + 1) * (D // 2 // LAST_CHUNKS), D // 2 // LAST_CHUNKS)], wnext.at[h], csem.at[2 + h]) for h in range(2)]
     for cp in caches:
         cp.start()
     ss_mate = rcopy(ss_ref, ss_recv.at[0], ss_s.at[0], ss_r.at[0], mate)
@@ -401,18 +457,18 @@
 
     squares = [jnp.zeros((B, HD), F32)]
 
-    def use(j):
+    def use(chunks):
         wide_cols = D // 2 // MID_CHUNKS
-        for half in range(2):
+        for at in chunks:
             for p in range(wide_cols // HD):
-                cols = slice(half * (D // 2) + j * wide_cols + p * HD, half * (D // 2) + j * wide_cols + (p + 1) * HD)
-                a1 = total[half, j, :, p * HD:(p + 1) * HD]
+                cols = slice(at * wide_cols + p * HD, at * wide_cols + (p + 1) * HD)
+                a1 = total[at, :, p * HD:(p + 1) * HD]
                 m = (alpha_ref[0] * h1_ref[:, cols].astype(F32) + beta_ref[0] * a1).astype(BF16)
                 h2_ref[:, cols] = m
                 x = m.astype(F32)
                 squares[0] = squares[0] + x * x
 
-    sent = exchange(og_ref[...], wbuf, wait_w, before_sends, pair_scale, relayout, cross_scale, core, mate, across,
+    settle_sends = exchange(og_ref[...], wbuf, wait_w, before_sends, pair_scale, relayout, cross_scale, core, mate, across,
                     a_send, a_recv, b_send, b_recv, total, (sa, ra, sb, rb, sc, rc), use, MID_CHUNKS)
     sq = squares[0]
     inv2 = lax.rsqrt(jnp.sum(sq, axis=1, keepdims=True) / D + EPS)
@@ -450,7 +506,8 @@
                 vn_ref[kv] = x.astype(BF16).astype(F32)
     for cp in caches:
         cp.wait()
-    for cp in sent + [ss_mate, ss_across]:
+    settle_sends()
+    for cp in (ss_mate, ss_across):
         cp.wait_send()
 
 
@@ -572,16 +629,14 @@
         for cp in scalars:
             cp.wait()
 
-    def use(j):
-        for half in range(2):
-            at = half * (D // 2) + j * (D // 2 // LAST_CHUNKS)
-            cols = slice(at, at + D // 2 // LAST_CHUNKS)
-            out_ref[:, cols] = (alpha_ref[1] * h2_ref[:, cols].astype(F32) + beta_ref[1] * total[half, j]).astype(BF16)
-
-    sent = exchange(left, wbuf, wait_w, lambda: await_peers(2), lambda: None, settle, lambda: None, core, mate,
+    def use(chunks):
+        for at in chunks:
+            cols = slice(at * (D // 2 // LAST_CHUNKS), (at + 1) * (D // 2 // LAST_CHUNKS))
+            out_ref[:, cols] = (alpha_ref[1] * h2_ref[:, cols].astype(F32) + beta_ref[1] * total[at]).astype(BF16)
+
+    settle_sends = exchange(left, wbuf, wait_w, lambda: await_peers(2), lambda: None, settle, lambda: None, core, mate,
                     across, a_send, a_recv, b_send, b_recv, total, (sa, ra, sb, rb, sc, rc), use, LAST_CHUNKS, first=first_ref)
-    for cp in sent:
-        cp.wait_send()
+    settle_sends()
 
 
 def last(at, h2, alpha, beta, w_out, w_first):

time: 59.4 us -> 59.3 us (level)
  no operation moved by 1% of the time
where the time goes in v9:
time: 59.3 us; the launch traced here: 59.2 us
  Pallas kernels  57.7 us (97%)
  local copies, waits for them, and re-layouts  0.72 us (1%)
  between operations  0.7 us (1%)
    pallas_call x1, Pallas kernels, lightning(): pl.pallas_call(lightning_kernel, out_shape=[jax.ShapeDtypeStruct((B, HL,...  23.1 us
    pallas_call x1, Pallas kernels, middle(): pl.pallas_call(mid_kernel, out_shape=[jax.ShapeDtypeStruct((B * 8, HD), F...  16.5 us
    pallas_call x1, Pallas kernels, last(): pl.pallas_call(last_kernel, out_shape=jax.ShapeDtypeStruct((B, D), BF16),...  11.2 us
    pallas_call x1, Pallas kernels, attention(): pl.pallas_call(attention_kernel, out_shape=[jax.ShapeDtypeStruct((B * 8,...  6.92 us

profile of v9, /device:TPU:0, one launch (start us, length us, event | category | flops | bytes accessed | tf_op | source)
XLA Modules:
  0.0 59.2 jit_solution(8484139296580868121)
XLA Ops:
  0.6 0.0 copy-start
  0.6 23.1 %lightning.1 = (f32[32,8,128,128]{3,2,1,0:T(8,128)}, bf16[32,1024]{1,0:T(8,128)(2,1)S(1)}, f32[32,128]{1,0:T(8,128)S(1)}, bf16[32,4096]{1,0:T(8,128)(2,1)S(1)}) custom-call(bf16[32,4096]{1,0:T(8,128)(2,1)} %hid_hbm.1, f32[32,128]{1,0:T(8,128)} %bitcast.12, f32[8]{0:T(128)} %slopes_hbm.1, f32[8,128]{1,0:T(8,128)} %onorm_hbm.1, f32[32,8,128,128]{3,2,1,0:T(8,128)} %state_ref.1, ...), custom_call_target="tpu_custom_call" | custom-call | tf_op jit(solution)/shard_map/lightning/pallas_call | solution.py:192
  23.7 0.0 copy-done
  23.7 0.0 copy-start.1
  23.8 16.5 %middle.1 = (f32[256,128]{1,0:T(8,128)S(1)}, f32[2,32,128]{2,1,0:T(8,128)S(1)}, f32[2,32,128]{2,1,0:T(8,128)S(1)}, bf16[32,4096]{1,0:T(8,128)(2,1)S(1)}, bf16[32...) custom-call(bf16[32,1024]{1,0:T(8,128)(2,1)S(1)} %get-tuple-element.18.og_re, ...), custom_call_target="tpu_custom_call" | custom-call | tf_op jit(solution)/shard_map/middle/pallas_call | solution.py:515
  40.3 0.0 copy-done.1
  40.3 6.9 %attention.1 = (f32[256,128]{1,0:T(8,128)S(1)}, bf16[32,2,512,128]{3,2,1,0:T(8,128)(2,1)}, bf16[32,2,512,128]{3,2,1,0:T(8,128)(2,1)}, bf16[32,2,512,128]{3,2,1,0:T(8,128)(2,1)S(1)}, bf16[32,2,512,128]{3,2,1,0:T(8,128)(2,1)S(1)}) custom-call(s32[32]{0:T(128)S(1)} %copy-done.1, ...), custom_call_target="tpu_custom_call", output_to_operand_aliasing={{3}: (4, {}), {4}: (5, {})} | custom-call | tf_op jit(solution)/shard_map/attention/pallas_call | solution.py:604
  47.2 11.2 %last.1 = bf16[32,4096]{1,0:T(8,128)(2,1)S(1)} custom-call(f32[256,128]{1,0:T(8,128)S(1)} %get-tuple-element.26.at_ref, bf16[32,4096]{1,0:T(8,128)(2,1)S(1)} %get-tuple-element.27.h2_ref, f32[2]{0:T(128)} %alpha_hbm.3, f32[2]{0:T(128)} %beta_hbm.3, bf16[1024,4096]{1,0:T(8,128)(2,1)} %bitcast.9, bf16[2,1024,256]{2,1,0:T(8,128)(2,1)S(1)} %get-tuple-element.28.first_ref), custom_call_target="tpu_custom_call" | custom-call | tf_op jit(solution)/shard_map/last/pallas_call | solution.py:643
  58.5 0.7 %copy.25 = bf16[32,4096]{1,0:T(8,128)(2,1)} copy(bf16[32,4096]{1,0:T(8,128)(2,1)S(1)} %last.1) | data formatting | bytes 524288
Async XLA Ops:
  0.6 23.1 %copy-start = (f32[4096]{0:T(1024)S(1)}, f32[4096]{0:T(1024)}, u32[]{:S(2)}) copy-start(f32[4096]{0:T(1024)} %param.27) | copy-start | bytes 49156
  23.7 16.5 %copy-start.1 = (s32[32]{0:T(128)S(1)}, s32[32]{0:T(128)}, u32[]{:S(2)}) copy-start(s32[32]{0:T(128)} %len_ref.1) | copy-start | bytes 388

commit v10 on v9

--- a/solution.py
+++ b/solution.py
@@ -28,7 +28,7 @@
 STEPS = D // DCH
 LCH = DCH * HL // 2 // HD
 RING = 3
-EARLY = 24
+EARLY = 30
 
 
 def any_spec():
@@ -542,7 +542,7 @@
 
 
 ROWS = 4
-ROWS_MM = 8
+ROWS_MM = 16
 
 
 def attention_kernel(len_ref, q_ref, kn_ref, vn_ref, kin_ref, vin_ref, at_ref, ko_ref, vo_ref, kbuf, vbuf, osem):

time: 59.3 us -> 59.3 us (level)
  no operation moved by 1% of the time
where the time goes in v10:
time: 59.3 us; the launch traced here: 59.2 us
  Pallas kernels  57.8 us (97%)
  local copies, waits for them, and re-layouts  0.72 us (1%)
  between operations  0.7 us (1%)
    pallas_call x1, Pallas kernels, lightning(): pl.pallas_call(lightning_kernel, out_shape=[jax.ShapeDtypeStruct((B, HL,...  23.1 us
    pallas_call x1, Pallas kernels, middle(): pl.pallas_call(mid_kernel, out_shape=[jax.ShapeDtypeStruct((B * 8, HD), F...  16.5 us
    pallas_call x1, Pallas kernels, last(): pl.pallas_call(last_kernel, out_shape=jax.ShapeDtypeStruct((B, D), BF16),...  11.2 us
    pallas_call x1, Pallas kernels, attention(): pl.pallas_call(attention_kernel, out_shape=[jax.ShapeDtypeStruct((B * 8,...  6.92 us

profile of v10, /device:TPU:0, one launch (start us, length us, event | category | flops | bytes accessed | tf_op | source)
XLA Modules:
  0.0 59.2 jit_solution(565064325989891951)
XLA Ops:
  0.6 0.0 copy-start
  0.6 23.1 %lightning.1 = (f32[32,8,128,128]{3,2,1,0:T(8,128)}, bf16[32,1024]{1,0:T(8,128)(2,1)S(1)}, f32[32,128]{1,0:T(8,128)S(1)}, bf16[32,4096]{1,0:T(8,128)(2,1)S(1)}) custom-call(bf16[32,4096]{1,0:T(8,128)(2,1)} %hid_hbm.1, f32[32,128]{1,0:T(8,128)} %bitcast.12, f32[8]{0:T(128)} %slopes_hbm.1, f32[8,128]{1,0:T(8,128)} %onorm_hbm.1, f32[32,8,128,128]{3,2,1,0:T(8,128)} %state_ref.1, ...), custom_call_target="tpu_custom_call" | custom-call | tf_op jit(solution)/shard_map/lightning/pallas_call | solution.py:192
  23.7 0.0 copy-done
  23.8 0.0 copy-start.1
  23.8 16.5 %middle.1 = (f32[256,128]{1,0:T(8,128)S(1)}, f32[2,32,128]{2,1,0:T(8,128)S(1)}, f32[2,32,128]{2,1,0:T(8,128)S(1)}, bf16[32,4096]{1,0:T(8,128)(2,1)S(1)}, bf16[32...) custom-call(bf16[32,1024]{1,0:T(8,128)(2,1)S(1)} %get-tuple-element.18.og_re, ...), custom_call_target="tpu_custom_call" | custom-call | tf_op jit(solution)/shard_map/middle/pallas_call | solution.py:515
  40.3 0.0 copy-done.1
  40.3 6.9 %attention.1 = (f32[256,128]{1,0:T(8,128)S(1)}, bf16[32,2,512,128]{3,2,1,0:T(8,128)(2,1)}, bf16[32,2,512,128]{3,2,1,0:T(8,128)(2,1)}, bf16[32,2,512,128]{3,2,1,0:T(8,128)(2,1)S(1)}, bf16[32,2,512,128]{3,2,1,0:T(8,128)(2,1)S(1)}) custom-call(s32[32]{0:T(128)S(1)} %copy-done.1, ...), custom_call_target="tpu_custom_call", output_to_operand_aliasing={{3}: (4, {}), {4}: (5, {})} | custom-call | tf_op jit(solution)/shard_map/attention/pallas_call | solution.py:604
  47.2 11.2 %last.1 = bf16[32,4096]{1,0:T(8,128)(2,1)S(1)} custom-call(f32[256,128]{1,0:T(8,128)S(1)} %get-tuple-element.26.at_ref, bf16[32,4096]{1,0:T(8,128)(2,1)S(1)} %get-tuple-element.27.h2_ref, f32[2]{0:T(128)} %alpha_hbm.3, f32[2]{0:T(128)} %beta_hbm.3, bf16[1024,4096]{1,0:T(8,128)(2,1)} %bitcast.9, bf16[2,1024,256]{2,1,0:T(8,128)(2,1)S(1)} %get-tuple-element.28.first_ref), custom_call_target="tpu_custom_call" | custom-call | tf_op jit(solution)/shard_map/last/pallas_call | solution.py:643
  58.5 0.7 %copy.25 = bf16[32,4096]{1,0:T(8,128)(2,1)} copy(bf16[32,4096]{1,0:T(8,128)(2,1)S(1)} %last.1) | data formatting | bytes 524288
Async XLA Ops:
  0.6 23.1 %copy-start = (f32[4096]{0:T(1024)S(1)}, f32[4096]{0:T(1024)}, u32[]{:S(2)}) copy-start(f32[4096]{0:T(1024)} %param.27) | copy-start | bytes 49156
  23.8 16.6 %copy-start.1 = (s32[32]{0:T(128)S(1)}, s32[32]{0:T(128)}, u32[]{:S(2)}) copy-start(s32[32]{0:T(128)} %len_ref.1) | copy-start | bytes 388
